TPU v7x, 32 devices: a whole 2x2x4 slice. The times are simulated.
32 devices in a mesh: dp: 2 (over y), expert: 16 (over z, x, core).
Axes of the slice: x: 2, y: 2, z: 4, core: 2. Of those that a mesh axis runs over, the one named last changes fastest.
Arguments:
- tokens: bfloat16 [256, 2880], P(('dp', 'expert')), may hold values from -6 to 6
- routes: int32 [2, 256, 4], P(None, ('dp', 'expert')), may hold values from 0 to 15, all different within a row; in each aligned block of 8 rows (0 to 7, 8 to 15, ..., all dimensions but the last counted through in order) at most 4 rows name the same one
- placement: int32 [2, 16], replicated, may hold values from 0 to 15, each once within a row
- up_weight: bfloat16 [2, 16, 2880, 1440], P(None, 'expert', None, 'dp'), may hold values from -0.109375 to 0.109375
- down_weight: bfloat16 [2, 16, 1440, 2880], P(None, 'expert', 'dp'), may hold values from -0.15625 to 0.15625
- router_weight: bfloat16 [2, 16, 2880], P(None, 'expert'), may hold values from -0.21875 to 0.21875
Outputs:
- final_stream: bfloat16 [256, 2880], P(('dp', 'expert'))
Inputs may be any that keep to these rules, and one draw needn't show every extreme that they name: `routes`: each row names 4 different experts. Within one layer's rows of one device no expert is named by more than 4 rows, and some device names some expert exactly 4 times. `placement`: each layer's row is a permutation of the slots.
All inputs are finite; a program needn't handle non-finite values.
Results may differ from a plain program's by a relative error of at most 0.008.
Values may be sent and summed in bfloat16 or wider, within the bound.
No kernel may reach another device: no remote copies, remote signals or barrier semaphores. Data moves between devices by JAX's collectives and lax.ppermute only.
A program may use at most 64 MiB of HBM per device.

v0:
```python
import jax
import jax.numpy as jnp
from jax import lax
from jax.sharding import PartitionSpec as P


def rms_rows(stream):
    values = stream.astype(jnp.float32)
    inverse = lax.rsqrt(jnp.mean(values * values, axis=-1, keepdims=True) + 1e-05)
    return (values * inverse).astype(jnp.bfloat16)


def slot_table(route_rows, place_row, columns, capacity):
    tok_rows, top_k = route_rows.shape
    experts = place_row.shape[0]
    matches = route_rows[:, :, None] == jnp.arange(experts, dtype=jnp.int32)[None, None, :]
    target = jnp.sum(jnp.where(matches, place_row[None, None, :], 0), axis=2).reshape(-1)
    row_count = target.shape[0]
    positions = jnp.arange(row_count, dtype=jnp.int32)
    earlier = (positions[None, :] < positions[:, None]) & (target[None, :] == target[:, None])
    row_rank = jnp.sum(earlier.astype(jnp.int32), axis=1)
    placed = (target[:, None, None] == jnp.arange(columns, dtype=jnp.int32)[None, :, None]) & (
        row_rank[:, None, None] == jnp.arange(capacity, dtype=jnp.int32)[None, None, :]
    )
    slot_map = jnp.sum(
        placed.reshape(tok_rows, top_k, columns, capacity).astype(jnp.float32), axis=1
    )
    return jnp.transpose(slot_map, (1, 2, 0))


def per_device(tokens, routes, placement, up_weight, down_weight, router_weight):
    groups = lax.axis_size("dp")
    columns = lax.axis_size("expert")
    tok_rows = tokens.shape[0]
    top_k = routes.shape[2]
    capacity = 2 * tok_rows * top_k // columns

    def layer_step(stream, packed):
        route_rows, place_row, up_part, down_part, router_part = packed
        normed = rms_rows(stream)
        slot_map = slot_table(route_rows, place_row, columns, capacity)
        outgoing = jnp.einsum(
            "jct,td->jcd", slot_map.astype(jnp.bfloat16), normed, preferred_element_type=jnp.float32
        ).astype(jnp.bfloat16)
        arrived = lax.all_to_all(
            outgoing, "expert", split_axis=0, concat_axis=0, tiled=True
        ).reshape(columns * capacity, -1)
        affinity = jax.nn.sigmoid(
            jnp.dot(arrived, router_part[0], preferred_element_type=jnp.float32)
        ).astype(jnp.bfloat16)
        all_rows, all_gates = (
            lax.all_gather(arrived, "dp", axis=0, tiled=True),
            lax.all_gather(affinity, "dp", axis=0, tiled=True),
        )
        hidden = jax.nn.silu(
            jnp.dot(all_rows, up_part[0], preferred_element_type=jnp.float32)
        ).astype(jnp.bfloat16)
        part_sums = jnp.dot(hidden, down_part[0], preferred_element_type=jnp.float32).astype(
            jnp.bfloat16
        )
        part_sums = part_sums.reshape(groups, columns, capacity, -1)
        all_gates = all_gates.reshape(groups, columns, capacity)
        returned, gates_back = (
            lax.all_to_all(
                lax.all_to_all(part_sums, "dp", split_axis=0, concat_axis=0, tiled=True),
                "expert",
                split_axis=1,
                concat_axis=1,
                tiled=True,
            ),
            lax.all_to_all(
                lax.all_to_all(all_gates, "dp", split_axis=0, concat_axis=0, tiled=True),
                "expert",
                split_axis=1,
                concat_axis=1,
                tiled=True,
            ),
        )
        weights = slot_map * gates_back[0].astype(jnp.float32)[:, :, None]
        numerator = jnp.einsum(
            "ect,gecd->td",
            weights.astype(jnp.bfloat16),
            returned,
            preferred_element_type=jnp.float32,
        )
        denominator = jnp.sum(weights, axis=(0, 1))
        updated = stream.astype(jnp.float32) + numerator / jnp.maximum(denominator, 0.5)[:, None]
        return (updated.astype(jnp.bfloat16), None)

    result_stream, unused = lax.scan(
        layer_step, tokens, (routes, placement, up_weight, down_weight, router_weight)
    )
    return result_stream


def solution(mesh):
    return jax.shard_map(
        per_device,
        mesh=mesh,
        in_specs=(
            P(("dp", "expert"), None),
            P(None, ("dp", "expert"), None),
            P(),
            P(None, "expert", None, "dp"),
            P(None, "expert", "dp", None),
            P(None, "expert", None),
        ),
        out_specs=P(("dp", "expert"), None),
        check_vma=False,
    )
```

profile of v0, /device:TPU:0, one launch (start us, length us, event | category | flops | bytes accessed | tf_op | source)
XLA Modules:
  0.0 197.5 jit_solution(17094374580464921686)
XLA Ops:
  0.8 196.1 %while.10 = (s32[]{:T(128)}, bf16[8,2880]{1,0:T(8,128)(2,1)S(1)}, s32[2,8,4]{1,2,0:T(4,128)}, s32[2,16]{1,0:T(2,128)}, bf16[2,1,2880]{2,0,1:T(2,128)(2,1)}, /*in...) while((s32[]{:T(128)}, bf16[8,2880]{1,0:T(8,128)(2,1)S(1)}, ...), condition=%wide.region_7.8_spmd, body=%wide.region_0.7_spmd.sunk | while | flops 1069763072 | bytes 25014808 | solution.py:90
  4.4 7.4 %all-to-all-start = ((bf16[16,4,2880]{2,1,0:T(4,128)(2,1)}), bf16[16,4,2880]{2,1,0:T(4,128)(2,1)S(1)}, u32[]{:S(2)}, u32[]{:S(2)}) async-start(bf16[16,4,2880]{2,1,0:T(4,128)(2,1)} %copy.58), calls=%async_computation | async-start | bytes 753664 | tf_op jit(solution)/shard_map/while/body/eval_jaxpr/all_to_all | solution.py:45
  11.8 1.2 dynamic-slice.2
  13.7 10.0 %all-to-all-done = bf16[16,4,2880]{2,1,0:T(4,128)(2,1)S(1)} async-done(((bf16[16,4,2880]{2,1,0:T(4,128)(2,1)}), bf16[16,4,2880]{2,1,0:T(4,128)(2,1)S(1)}, u32[]{:S(2)}, u32[]{:S(2)}) %all-to-all-start) | async-done | bytes 368672 | tf_op jit(solution)/shard_map/while/body/eval_jaxpr/all_to_all | solution.py:45
  23.9 11.4 %all_gather.7 = bf16[128,2880]{1,0:T(8,128)(2,1)S(1)} all-gather(bf16[64,2880]{1,0:T(8,128)(2,1)S(1)} %reshape.105), channel_id=1, replica_groups=mesh['dp'=2,'expert'=16] {'dp'}, dimensions={0}, use_global_device_ids=true | all-gather | bytes 1105920 | tf_op jit(solution)/shard_map/while/body/eval_jaxpr/all_gather | solution.py:52
  35.3 0.9 fusion.69
  36.5 4.9 %all-reduce.2 = bf16[128]{0:T(256)(128)(2,1)S(1)} all-reduce(bf16[128]{0:T(256)(128)(2,1)S(1)} %dynamic-update-slice.2), channel_id=1, replica_groups=mesh['dp'=2,'expert'=16] {'dp'}, use_global_device_ids=true, to_apply=%add | all-reduce | flops 128 | bytes 512 | tf_op jit(solution)/shard_map/while
  42.2 3.2 %all-to-all-start.3 = ((bf16[2,16,4]{1,2,0:T(4,128)(2,1)}), bf16[2,16,4]{1,2,0:T(4,128)(2,1)S(1)}, u32[]{:S(2)}, u32[]{:S(2)}) async-start(bf16[2,16,4]{1,2,0:T(4,128)(2,1)} %copy.61), calls=%async_computation.3 | async-start | bytes 4096 | tf_op jit(solution)/shard_map/while/body/eval_jaxpr/all_to_all | solution.py:72
  45.4 8.2 %fusion.68 = bf16[128,2880]{0,1:T(8,128)(2,1)S(1)} fusion(bf16[2,1,720,2880]{3,2,1,0:T(8,128)(2,1)} %get-tuple-element.130, s32[]{:T(128)} %get-tuple-element.112, bf16[128,2880]{1,0:T(8,128)(2,1)S(1)} %all_gather.7, bf16[2,1,2880,720]{2,3,1,0:T(8,128)(2,1)} %get-tuple-element.129), kind=kOutput, calls=%fused_computation.6.clone.1 | convolution fusion | flops 1062512640 | bytes 9954304 | tf_op jit(solution)/shard_map/while/body/eval_jaxpr/dot_general | solution.py:58
  54.0 1.1 reshape.106
  55.1 3.5 %all-to-all-start.1 = ((bf16[2,16,4,2880]{3,2,1,0:T(4,128)(2,1)}), bf16[2,16,4,2880]{3,2,1,0:T(4,128)(2,1)S(1)}, u32[]{:S(2)}, u32[]{:S(2)}) async-start(bf16[2,16,4,2880]{3,2,1,0:T(4,128)(2,1)} %reshape.106), calls=%async_computation.1 | async-start | bytes 1507328 | tf_op jit(solution)/shard_map/while/body/eval_jaxpr/all_to_all | solution.py:65
  59.3 8.3 %all-to-all-done.1 = bf16[2,16,4,2880]{3,2,1,0:T(4,128)(2,1)S(1)} async-done(((bf16[2,16,4,2880]{3,2,1,0:T(4,128)(2,1)}), bf16[2,16,4,2880]{3,2,1,0:T(4,128)(2,1)S(1)}, u32[]{:S(2)}, u32[]{:S(2)}) %all-to-all-start.1) | async-done | bytes 737312 | tf_op jit(solution)/shard_map/while/body/eval_jaxpr/all_to_all | solution.py:65
  67.6 3.9 %all-to-all-start.4 = ((bf16[2,16,4]{2,0,1:T(2,128)(2,1)}), bf16[2,16,4]{2,0,1:T(2,128)(2,1)S(1)}, u32[]{:S(2)}, u32[]{:S(2)}) async-start(bf16[2,16,4]{2,0,1:T(2,128)(2,1)} %copy.62), calls=%async_computation.4 | async-start | bytes 16384 | tf_op jit(solution)/shard_map/while/body/eval_jaxpr/all_to_all | solution.py:71
  71.5 1.1 copy.60
  72.6 5.2 %all-to-all-done.4 = bf16[2,16,4]{2,0,1:T(2,128)(2,1)S(1)} async-done(((bf16[2,16,4]{2,0,1:T(2,128)(2,1)}), bf16[2,16,4]{2,0,1:T(2,128)(2,1)S(1)}, u32[]{:S(2)}, u32[]{:S(2)}) %all-to-all-start.4) | async-done | bytes 288 | tf_op jit(solution)/shard_map/while/body/eval_jaxpr/all_to_all | solution.py:71
  77.8 3.6 %all-to-all-start.2 = ((bf16[2,16,4,2880]{3,2,0,1:T(4,128)(2,1)}), bf16[2,16,4,2880]{3,2,0,1:T(4,128)(2,1)S(1)}, u32[]{:S(2)}, u32[]{:S(2)}) async-start(bf16[2,16,4,2880]{3,2,0,1:T(4,128)(2,1)} %copy.60), calls=%async_computation.2 | async-start | bytes 1507328 | tf_op jit(solution)/shard_map/while/body/eval_jaxpr/all_to_all | solution.py:64
  81.7 17.9 %all-to-all-done.2 = bf16[2,16,4,2880]{3,2,0,1:T(4,128)(2,1)S(1)} async-done(((bf16[2,16,4,2880]{3,2,0,1:T(4,128)(2,1)}), bf16[2,16,4,2880]{3,2,0,1:T(4,128)(2,1)S(1)}, u32[]{:S(2)}, u32[]{:S(2)}) %all-to-all-start.2) | async-done | bytes 737312 | tf_op jit(solution)/shard_map/while/body/eval_jaxpr/all_to_all | solution.py:64
  103.6 5.2 %all-to-all-start = ((bf16[16,4,2880]{2,1,0:T(4,128)(2,1)}), bf16[16,4,2880]{2,1,0:T(4,128)(2,1)S(1)}, u32[]{:S(2)}, u32[]{:S(2)}) async-start(bf16[16,4,2880]{2,1,0:T(4,128)(2,1)} %copy.58), calls=%async_computation | async-start | bytes 753664 | tf_op jit(solution)/shard_map/while/body/eval_jaxpr/all_to_all | solution.py:45
  108.8 1.2 dynamic-slice.2
  110.7 10.0 %all-to-all-done = bf16[16,4,2880]{2,1,0:T(4,128)(2,1)S(1)} async-done(((bf16[16,4,2880]{2,1,0:T(4,128)(2,1)}), bf16[16,4,2880]{2,1,0:T(4,128)(2,1)S(1)}, u32[]{:S(2)}, u32[]{:S(2)}) %all-to-all-start) | async-done | bytes 368672 | tf_op jit(solution)/shard_map/while/body/eval_jaxpr/all_to_all | solution.py:45
  120.8 11.4 %all_gather.7 = bf16[128,2880]{1,0:T(8,128)(2,1)S(1)} all-gather(bf16[64,2880]{1,0:T(8,128)(2,1)S(1)} %reshape.105), channel_id=1, replica_groups=mesh['dp'=2,'expert'=16] {'dp'}, dimensions={0}, use_global_device_ids=true | all-gather | bytes 1105920 | tf_op jit(solution)/shard_map/while/body/eval_jaxpr/all_gather | solution.py:52
  133.4 4.9 %all-reduce.2 = bf16[128]{0:T(256)(128)(2,1)S(1)} all-reduce(bf16[128]{0:T(256)(128)(2,1)S(1)} %dynamic-update-slice.2), channel_id=1, replica_groups=mesh['dp'=2,'expert'=16] {'dp'}, use_global_device_ids=true, to_apply=%add | all-reduce | flops 128 | bytes 512 | tf_op jit(solution)/shard_map/while
  139.1 3.2 %all-to-all-start.3 = ((bf16[2,16,4]{1,2,0:T(4,128)(2,1)}), bf16[2,16,4]{1,2,0:T(4,128)(2,1)S(1)}, u32[]{:S(2)}, u32[]{:S(2)}) async-start(bf16[2,16,4]{1,2,0:T(4,128)(2,1)} %copy.61), calls=%async_computation.3 | async-start | bytes 4096 | tf_op jit(solution)/shard_map/while/body/eval_jaxpr/all_to_all | solution.py:72
  142.3 8.2 %fusion.68 = bf16[128,2880]{0,1:T(8,128)(2,1)S(1)} fusion(bf16[2,1,720,2880]{3,2,1,0:T(8,128)(2,1)} %get-tuple-element.130, s32[]{:T(128)} %get-tuple-element.112, bf16[128,2880]{1,0:T(8,128)(2,1)S(1)} %all_gather.7, bf16[2,1,2880,720]{2,3,1,0:T(8,128)(2,1)} %get-tuple-element.129), kind=kOutput, calls=%fused_computation.6.clone.1 | convolution fusion | flops 1062512640 | bytes 9954304 | tf_op jit(solution)/shard_map/while/body/eval_jaxpr/dot_general | solution.py:58
  150.9 1.1 reshape.106
  152.0 3.5 %all-to-all-start.1 = ((bf16[2,16,4,2880]{3,2,1,0:T(4,128)(2,1)}), bf16[2,16,4,2880]{3,2,1,0:T(4,128)(2,1)S(1)}, u32[]{:S(2)}, u32[]{:S(2)}) async-start(bf16[2,16,4,2880]{3,2,1,0:T(4,128)(2,1)} %reshape.106), calls=%async_computation.1 | async-start | bytes 1507328 | tf_op jit(solution)/shard_map/while/body/eval_jaxpr/all_to_all | solution.py:65
  156.2 8.3 %all-to-all-done.1 = bf16[2,16,4,2880]{3,2,1,0:T(4,128)(2,1)S(1)} async-done(((bf16[2,16,4,2880]{3,2,1,0:T(4,128)(2,1)}), bf16[2,16,4,2880]{3,2,1,0:T(4,128)(2,1)S(1)}, u32[]{:S(2)}, u32[]{:S(2)}) %all-to-all-start.1) | async-done | bytes 737312 | tf_op jit(solution)/shard_map/while/body/eval_jaxpr/all_to_all | solution.py:65
  164.5 3.9 %all-to-all-start.4 = ((bf16[2,16,4]{2,0,1:T(2,128)(2,1)}), bf16[2,16,4]{2,0,1:T(2,128)(2,1)S(1)}, u32[]{:S(2)}, u32[]{:S(2)}) async-start(bf16[2,16,4]{2,0,1:T(2,128)(2,1)} %copy.62), calls=%async_computation.4 | async-start | bytes 16384 | tf_op jit(solution)/shard_map/while/body/eval_jaxpr/all_to_all | solution.py:71
  168.4 1.1 copy.60
  169.6 5.2 %all-to-all-done.4 = bf16[2,16,4]{2,0,1:T(2,128)(2,1)S(1)} async-done(((bf16[2,16,4]{2,0,1:T(2,128)(2,1)}), bf16[2,16,4]{2,0,1:T(2,128)(2,1)S(1)}, u32[]{:S(2)}, u32[]{:S(2)}) %all-to-all-start.4) | async-done | bytes 288 | tf_op jit(solution)/shard_map/while/body/eval_jaxpr/all_to_all | solution.py:71
  174.8 3.6 %all-to-all-start.2 = ((bf16[2,16,4,2880]{3,2,0,1:T(4,128)(2,1)}), bf16[2,16,4,2880]{3,2,0,1:T(4,128)(2,1)S(1)}, u32[]{:S(2)}, u32[]{:S(2)}) async-start(bf16[2,16,4,2880]{3,2,0,1:T(4,128)(2,1)} %copy.60), calls=%async_computation.2 | async-start | bytes 1507328 | tf_op jit(solution)/shard_map/while/body/eval_jaxpr/all_to_all | solution.py:64
  178.6 17.9 %all-to-all-done.2 = bf16[2,16,4,2880]{3,2,0,1:T(4,128)(2,1)S(1)} async-done(((bf16[2,16,4,2880]{3,2,0,1:T(4,128)(2,1)}), bf16[2,16,4,2880]{3,2,0,1:T(4,128)(2,1)S(1)}, u32[]{:S(2)}, u32[]{:S(2)}) %all-to-all-start.2) | async-done | bytes 737312 | tf_op jit(solution)/shard_map/while/body/eval_jaxpr/all_to_all | solution.py:64
  (62 shorter events, 15.3 us)
Async XLA Ops:
  4.4 19.3 %all-to-all-start = ((bf16[16,4,2880]{2,1,0:T(4,128)(2,1)}), bf16[16,4,2880]{2,1,0:T(4,128)(2,1)S(1)}, u32[]{:S(2)}, u32[]{:S(2)}) async-start(bf16[16,4,2880]{2,1,0:T(4,128)(2,1)} %copy.58), calls=%async_computation | async-start | bytes 753664 | tf_op jit(solution)/shard_map/while/body/eval_jaxpr/all_to_all | solution.py:45
  42.2 12.9 %all-to-all-start.3 = ((bf16[2,16,4]{1,2,0:T(4,128)(2,1)}), bf16[2,16,4]{1,2,0:T(4,128)(2,1)S(1)}, u32[]{:S(2)}, u32[]{:S(2)}) async-start(bf16[2,16,4]{1,2,0:T(4,128)(2,1)} %copy.61), calls=%async_computation.3 | async-start | bytes 4096 | tf_op jit(solution)/shard_map/while/body/eval_jaxpr/all_to_all | solution.py:72
  55.1 12.5 %all-to-all-start.1 = ((bf16[2,16,4,2880]{3,2,1,0:T(4,128)(2,1)}), bf16[2,16,4,2880]{3,2,1,0:T(4,128)(2,1)S(1)}, u32[]{:S(2)}, u32[]{:S(2)}) async-start(bf16[2,16,4,2880]{3,2,1,0:T(4,128)(2,1)} %reshape.106), calls=%async_computation.1 | async-start | bytes 1507328 | tf_op jit(solution)/shard_map/while/body/eval_jaxpr/all_to_all | solution.py:65
  67.6 10.3 %all-to-all-start.4 = ((bf16[2,16,4]{2,0,1:T(2,128)(2,1)}), bf16[2,16,4]{2,0,1:T(2,128)(2,1)S(1)}, u32[]{:S(2)}, u32[]{:S(2)}) async-start(bf16[2,16,4]{2,0,1:T(2,128)(2,1)} %copy.62), calls=%async_computation.4 | async-start | bytes 16384 | tf_op jit(solution)/shard_map/while/body/eval_jaxpr/all_to_all | solution.py:71
  77.8 21.7 %all-to-all-start.2 = ((bf16[2,16,4,2880]{3,2,0,1:T(4,128)(2,1)}), bf16[2,16,4,2880]{3,2,0,1:T(4,128)(2,1)S(1)}, u32[]{:S(2)}, u32[]{:S(2)}) async-start(bf16[2,16,4,2880]{3,2,0,1:T(4,128)(2,1)} %copy.60), calls=%async_computation.2 | async-start | bytes 1507328 | tf_op jit(solution)/shard_map/while/body/eval_jaxpr/all_to_all | solution.py:64
  103.6 17.0 %all-to-all-start = ((bf16[16,4,2880]{2,1,0:T(4,128)(2,1)}), bf16[16,4,2880]{2,1,0:T(4,128)(2,1)S(1)}, u32[]{:S(2)}, u32[]{:S(2)}) async-start(bf16[16,4,2880]{2,1,0:T(4,128)(2,1)} %copy.58), calls=%async_computation | async-start | bytes 753664 | tf_op jit(solution)/shard_map/while/body/eval_jaxpr/all_to_all | solution.py:45
  139.1 12.9 %all-to-all-start.3 = ((bf16[2,16,4]{1,2,0:T(4,128)(2,1)}), bf16[2,16,4]{1,2,0:T(4,128)(2,1)S(1)}, u32[]{:S(2)}, u32[]{:S(2)}) async-start(bf16[2,16,4]{1,2,0:T(4,128)(2,1)} %copy.61), calls=%async_computation.3 | async-start | bytes 4096 | tf_op jit(solution)/shard_map/while/body/eval_jaxpr/all_to_all | solution.py:72
  152.0 12.5 %all-to-all-start.1 = ((bf16[2,16,4,2880]{3,2,1,0:T(4,128)(2,1)}), bf16[2,16,4,2880]{3,2,1,0:T(4,128)(2,1)S(1)}, u32[]{:S(2)}, u32[]{:S(2)}) async-start(bf16[2,16,4,2880]{3,2,1,0:T(4,128)(2,1)} %reshape.106), calls=%async_computation.1 | async-start | bytes 1507328 | tf_op jit(solution)/shard_map/while/body/eval_jaxpr/all_to_all | solution.py:65
  164.5 10.3 %all-to-all-start.4 = ((bf16[2,16,4]{2,0,1:T(2,128)(2,1)}), bf16[2,16,4]{2,0,1:T(2,128)(2,1)S(1)}, u32[]{:S(2)}, u32[]{:S(2)}) async-start(bf16[2,16,4]{2,0,1:T(2,128)(2,1)} %copy.62), calls=%async_computation.4 | async-start | bytes 16384 | tf_op jit(solution)/shard_map/while/body/eval_jaxpr/all_to_all | solution.py:71
  174.8 21.7 %all-to-all-start.2 = ((bf16[2,16,4,2880]{3,2,0,1:T(4,128)(2,1)}), bf16[2,16,4,2880]{3,2,0,1:T(4,128)(2,1)S(1)}, u32[]{:S(2)}, u32[]{:S(2)}) async-start(bf16[2,16,4,2880]{3,2,0,1:T(4,128)(2,1)} %copy.60), calls=%async_computation.2 | async-start | bytes 1507328 | tf_op jit(solution)/shard_map/while/body/eval_jaxpr/all_to_all | solution.py:64
  196.9 0.6 copy-start
where the time goes:
time: 199 us; the launch traced here: 198 us
  waiting for transfers between devices  82.7 us (42%)
  starting transfers between devices  41.1 us (21%)
  blocking collectives  32.7 us (16%)
  matrix products  19.4 us (10%)
  local copies, waits for them, and re-layouts  18.1 us (9%)
    all_to_all x2, waiting for transfers between devices, layer_step(): lax.all_to_all(lax.all_to_all(part_sums, 'dp', split_axis=0, concat_axis=...  35.8 us
    all_gather x2, blocking collectives, layer_step(): lax.all_gather(arrived, 'dp', axis=0, tiled=True)  22.9 us
    all_to_all x2, waiting for transfers between devices, layer_step(): lax.all_to_all(outgoing, 'expert', split_axis=0, concat_axis=0, tiled=True)  19.9 us
    all_to_all x2, waiting for transfers between devices, layer_step(): lax.all_to_all(part_sums, 'dp', split_axis=0, concat_axis=0, tiled=True)  16.5 us
    dot_general x2, matrix products, layer_step(): jnp.dot(hidden, down_part[0], preferred_element_type=jnp.float32)  16.4 us
    all_to_all x2, starting transfers between devices, layer_step(): lax.all_to_all(outgoing, 'expert', split_axis=0, concat_axis=0, tiled=True)  12.5 us
    all_to_all x2, waiting for transfers between devices, layer_step(): lax.all_to_all(lax.all_to_all(all_gates, 'dp', split_axis=0, concat_axis=...  10.5 us
    while x2, blocking collectives  9.82 us
  transfers between devices with their start and end apart: 10, of which 8 were waited for; matrix products, arithmetic and copies ran while one was open for 13% of the time, Pallas kernels for 0%

commit v1 on v0

--- a/solution.py
+++ b/solution.py
@@ -1,13 +1,157 @@
+import functools
+
 import jax
 import jax.numpy as jnp
 from jax import lax
+from jax.experimental import pallas as pl
+from jax.experimental.pallas import tpu as pltpu
 from jax.sharding import PartitionSpec as P
+
+LANES = 128
 
 
 def rms_rows(stream):
     values = stream.astype(jnp.float32)
     inverse = lax.rsqrt(jnp.mean(values * values, axis=-1, keepdims=True) + 1e-05)
     return (values * inverse).astype(jnp.bfloat16)
+
+
+def round_up(value, unit):
+    return -(-value // unit) * unit
+
+
+def column_blocks(extent, step):
+    return [(start, min(step, extent - start)) for start in range(0, extent, step)]
+
+
+def ffn_kernel(layer, width, up_blocks, down_blocks, ids_ref, near_ref, far_ref, router_ref, up_hbm, down_hbm, near_out, far_out, rows_ref, hidden_ref, *scratch):
+    up_parts, down_parts = scratch[: len(up_blocks)], scratch[len(up_blocks) : -1]
+    sems = scratch[-1]
+    copies = []
+    for index, (start, size) in enumerate(up_blocks):
+        copies.append(pltpu.make_async_copy(up_hbm.at[layer, 0, :, pl.ds(start, size)], up_parts[index], sems.at[index]))
+    for index, (start, size) in enumerate(down_blocks):
+        copies.append(
+            pltpu.make_async_copy(down_hbm.at[layer, 0, :, pl.ds(start, size)], down_parts[index], sems.at[len(up_blocks) + index])
+        )
+    for copy in copies:
+        copy.start()
+    half = near_ref.shape[0]
+    model = router_ref.shape[-1]
+    rows_ref[:half, :] = near_ref[...]
+    rows_ref[half:, :] = far_ref[...]
+    slot, block = ids_ref[0], ids_ref[1]
+    tail = model // LANES * LANES
+    lane = lax.broadcasted_iota(jnp.int32, (2 * half, width - tail), 1)
+    here = lane == (model - tail) + slot
+    member = jnp.sum(jnp.where(here, rows_ref[:, tail:].astype(jnp.float32), 0.0), axis=1, keepdims=True)
+    router = router_ref[layer].astype(jnp.float32)
+    logits = jnp.sum(rows_ref[:, :model].astype(jnp.float32) * router, axis=1, keepdims=True)
+    gate = jax.nn.sigmoid(logits).astype(jnp.bfloat16).astype(jnp.float32) * member
+    for index, (start, size) in enumerate(up_blocks):
+        copies[index].wait()
+        raw = jnp.dot(rows_ref[:, :model], up_parts[index][...], preferred_element_type=jnp.float32)
+        hidden_ref[:, start : start + size] = jax.nn.silu(raw).astype(jnp.bfloat16)
+    for index, (start, size) in enumerate(down_blocks):
+        copies[len(up_blocks) + index].wait()
+        part = jnp.dot(hidden_ref[...], down_parts[index][...], preferred_element_type=jnp.float32)
+        weighted = (part.astype(jnp.bfloat16).astype(jnp.float32) * gate).astype(jnp.bfloat16)
+        near_out[:, start : start + size] = weighted[:half]
+        far_out[:, start : start + size] = weighted[half:]
+    sent = jnp.where(here & (block == 0), gate, 0.0)[:, model - tail :].astype(jnp.bfloat16)
+    near_out[:, model:] = sent[:half]
+    far_out[:, model:] = sent[half:]
+
+
+def expert_ffn(layer, ids, near, far, router, up, down):
+    half, width = near.shape
+    model, units = up.shape[2], up.shape[3]
+    up_blocks = column_blocks(units, 256)
+    down_blocks = column_blocks(model, 768)
+    scratch = [pltpu.VMEM((2 * half, width), jnp.bfloat16), pltpu.VMEM((2 * half, units), jnp.bfloat16)]
+    scratch += [pltpu.VMEM((model, size), jnp.bfloat16) for _, size in up_blocks]
+    scratch += [pltpu.VMEM((units, size), jnp.bfloat16) for _, size in down_blocks]
+    scratch += [pltpu.SemaphoreType.DMA((len(up_blocks) + len(down_blocks),))]
+    vmem = pl.BlockSpec(memory_space=pltpu.VMEM)
+    return pl.pallas_call(
+        functools.partial(ffn_kernel, layer, width, up_blocks, down_blocks),
+        out_shape=[jax.ShapeDtypeStruct((half, width), jnp.bfloat16)] * 2,
+        in_specs=[
+            pl.BlockSpec(memory_space=pltpu.SMEM),
+            vmem,
+            vmem,
+            vmem,
+            pl.BlockSpec(memory_space=pl.ANY),
+            pl.BlockSpec(memory_space=pl.ANY),
+        ],
+        out_specs=[vmem, vmem],
+        scratch_shapes=scratch,
+        compiler_params=pltpu.CompilerParams(vmem_limit_bytes=32 * 1024 * 1024),
+        name=f"ffn_{layer}",
+    )(ids, near, far, router, up, down)
+
+
+def dense_moves(groups, columns):
+    lengths = columns // 4
+
+    def pairs(move):
+        listed = []
+        for group in range(groups):
+            for far in range(lengths):
+                for side in range(2):
+                    for core in range(2):
+                        to = move(group, far, side, core)
+                        listed.append((((group * lengths + far) * 2 + side) * 2 + core, ((to[0] * lengths + to[1]) * 2 + to[2]) * 2 + to[3]))
+        return listed
+
+    def axis_swap(which):
+        def move(group, far, side, core):
+            return (group, far, 1 - side, core) if core == which else (1 - group, far, side, core)
+
+        return pairs(move)
+
+    def shift(amount):
+        return pairs(lambda group, far, side, core: (group, (far + amount) % lengths, side, core))
+
+    return lengths, shift, axis_swap(0), axis_swap(1), pairs(lambda group, far, side, core: (group, far, side, 1 - core))
+
+
+def dense_device(tokens, routes, placement, up_weight, down_weight, router_weight):
+    groups, columns = lax.axis_size("dp"), lax.axis_size("expert")
+    layers, tok_rows, _ = routes.shape
+    model = tokens.shape[1]
+    width = round_up(model + columns, LANES)
+    lengths, shift, first_swap, second_swap, core_swap = dense_moves(groups, columns)
+    axes = ("dp", "expert")
+    ids = jnp.stack([lax.axis_index("expert"), lax.axis_index("dp")]).astype(jnp.int32)
+    slots = jnp.arange(columns, dtype=jnp.int32)
+    stream = tokens
+
+    for layer in range(layers):
+        chosen = routes[layer][:, :, None] == slots[None, None, :]
+        target = jnp.sum(jnp.where(chosen, placement[layer][None, None, :], 0), axis=2)
+        member = jnp.any(target[:, :, None] == slots[None, None, :], axis=1).astype(jnp.bfloat16)
+        padding = jnp.zeros((tok_rows, width - model - columns), jnp.bfloat16)
+        own = jnp.concatenate([rms_rows(stream), member, padding], axis=1)
+        line = [own] + [lax.ppermute(own, axes, shift(step)) for step in range(1, lengths)]
+        rows = jnp.concatenate(line, axis=0)
+        rows = jnp.concatenate([rows, lax.ppermute(rows, axes, first_swap)], axis=0)
+        near = jnp.concatenate([rows, lax.ppermute(rows, axes, second_swap)], axis=0)
+        far = lax.ppermute(near, axes, core_swap)
+        near_out, far_out = expert_ffn(layer, ids, near, far, router_weight, up_weight, down_weight)
+        total = near_out.astype(jnp.float32) + lax.ppermute(far_out, axes, core_swap).astype(jnp.float32)
+        for swap in (second_swap, first_swap):
+            half = total.shape[0] // 2
+            moved = lax.ppermute(total[half:].astype(jnp.bfloat16), axes, swap)
+            total = total[:half] + moved.astype(jnp.float32)
+        pieces = total.reshape(lengths, tok_rows, width)
+        summed = pieces[0]
+        for step in range(1, lengths):
+            summed = summed + lax.ppermute(pieces[step].astype(jnp.bfloat16), axes, shift(lengths - step)).astype(jnp.float32)
+        denominator = jnp.maximum(jnp.sum(summed[:, model:], axis=1, keepdims=True), 0.5)
+        updated = stream.astype(jnp.float32) + summed[:, :model] / denominator
+        stream = updated.astype(jnp.bfloat16)
+    return stream
 
 
 def slot_table(route_rows, place_row, columns, capacity):
@@ -28,7 +172,7 @@
     return jnp.transpose(slot_map, (1, 2, 0))
 
 
-def per_device(tokens, routes, placement, up_weight, down_weight, router_weight):
+def dispatch_device(tokens, routes, placement, up_weight, down_weight, router_weight):
     groups = lax.axis_size("dp")
     columns = lax.axis_size("expert")
     tok_rows = tokens.shape[0]
@@ -93,6 +237,15 @@
     return result_stream
 
 
+def per_device(tokens, routes, placement, up_weight, down_weight, router_weight):
+    groups, columns = lax.axis_size("dp"), lax.axis_size("expert")
+    tok_rows, top_k = tokens.shape[0], routes.shape[2]
+    capacity = 2 * tok_rows * top_k // columns
+    dense = groups == 2 and columns % 4 == 0 and tok_rows <= 2 * capacity
+    plan = dense_device if dense else dispatch_device
+    return plan(tokens, routes, placement, up_weight, down_weight, router_weight)
+
+
 def solution(mesh):
     return jax.shard_map(
         per_device,

time: 199 us -> 144 us (0.72)
  blocking collectives: 32.7 us -> 0 us
  matrix products: 19.4 us -> 0 us
  waiting for transfers between devices: 82.7 us -> 67.7 us
  Pallas kernels: 0 us -> 14.1 us
  starting transfers between devices: 41.1 us -> 28.9 us
  local copies, waits for them, and re-layouts: 18.1 us -> 27.8 us
  other arithmetic: 1.91 us -> 4.34 us
    all_to_all x10 -> x0, waiting for transfers between devices: 82.7 us -> none  [the longest x2 35.8 us: layer_step(): lax.all_to_all(lax.all_to_all(part_sums, 'dp', split_axis=0, concat_axis=...]
    ppermute x0 -> x24, waiting for transfers between devices: none -> 67.7 us  [the longest x4 20.1 us: dense_device(): moved = lax.ppermute(total[half:].astype(jnp.bfloat16), axes, swap)]
    all_to_all x10 -> x0, starting transfers between devices: 41.1 us -> none  [the longest x2 12.5 us: layer_step(): lax.all_to_all(outgoing, 'expert', split_axis=0, concat_axis=0, tiled=True)]
    ppermute x0 -> x24, starting transfers between devices: none -> 28.9 us  [the longest x6 8.62 us: dense_device(): lax.ppermute(own, axes, shift(step))]
    unnamed x3 -> x22, local copies, waits for them, and re-layouts: 1.41 us -> 25.8 us
    all_gather x2 -> x0, blocking collectives: 22.9 us -> none  [layer_step(): lax.all_gather(arrived, 'dp', axis=0, tiled=True)]
    dot_general x8 -> x0, matrix products: 19.4 us -> none  [the longest x2 16.4 us: layer_step(): jnp.dot(hidden, down_part[0], preferred_element_type=jnp.float32)]
    pallas_call x0 -> x2, Pallas kernels: none -> 14.1 us  [expert_ffn(): pl.pallas_call(functools.partial(ffn_kernel, layer, width, up_blocks, dow...]
  transfers between devices with their start and end apart: 10 -> 24, of which waited for: 8 -> 23; matrix products, arithmetic and copies ran while one was open for 13% -> 9% of each run, Pallas kernels for 0% -> 0%
where the time goes in v1:
time: 144 us; the launch traced here: 143 us
  waiting for transfers between devices  67.7 us (47%)
  starting transfers between devices  28.9 us (20%)
  local copies, waits for them, and re-layouts  27.8 us (19%)
  Pallas kernels  14.1 us (10%)
  other arithmetic  4.34 us (3%)
    unnamed x22, local copies, waits for them, and re-layouts  25.8 us
    ppermute x4, waiting for transfers between devices, dense_device(): moved = lax.ppermute(total[half:].astype(jnp.bfloat16), axes, swap)  20.1 us
    pallas_call x2, Pallas kernels, expert_ffn(): pl.pallas_call(functools.partial(ffn_kernel, layer, width, up_blocks, dow...  14.1 us
    ppermute x2, waiting for transfers between devices, dense_device(): lax.ppermute(rows, axes, second_swap)  12.1 us
    ppermute x6, waiting for transfers between devices, dense_device(): lax.ppermute(own, axes, shift(step))  10.1 us
    ppermute x2, waiting for transfers between devices, dense_device(): rows = jnp.concatenate([rows, lax.ppermute(rows, axes, first_swap)], axis=0)  9.98 us
    ppermute x6, waiting for transfers between devices, dense_device(): lax.ppermute(pieces[step].astype(jnp.bfloat16), axes, shift(lengths - step))  9.2 us
    ppermute x6, starting transfers between devices, dense_device(): lax.ppermute(own, axes, shift(step))  8.62 us
  transfers between devices with their start and end apart: 24, of which 23 were waited for; matrix products, arithmetic and copies ran while one was open for 9% of the time, Pallas kernels for 0%

profile of v1, /device:TPU:0, one launch (start us, length us, event | category | flops | bytes accessed | tf_op | source)
XLA Modules:
  0.0 142.9 jit_solution(9622193852266425050)
XLA Ops:
  3.8 5.1 %collective-permute-start.2 = (bf16[8,2944]{1,0:T(8,128)(2,1)S(1)}, bf16[8,2944]{1,0:T(8,128)(2,1)S(1)}, u32[]{:S(2)}, u32[]{:S(2)}) collective-permute-start(bf16[8,2944]{1,0:T(8,128)(2,1)S(1)} %concatenate.28), channel_id=1, source_target_pairs={{0,12},{1,13},{2,14},{3,15},{4,0},{5,1},{6,2},{7,3},{8,4},{9,5},{1... | collective-permute-start | bytes 141320 | tf_op jit(solution)/shard_map/ppermute | solution.py:136
  10.8 3.0 %collective-permute-done.1 = bf16[8,2944]{1,0:T(8,128)(2,1)S(1)} collective-permute-done((bf16[8,2944]{1,0:T(8,128)(2,1)S(1)}, bf16[8,2944]{1,0:T(8,128)(2,1)S(1)}, u32[]{:S(2)}, u32[]{:S(2)}) %collective-permute-start.1) | collective-permute-done | bytes 47136 | tf_op jit(solution)/shard_map/ppermute | solution.py:136
  16.3 4.1 %collective-permute-done.3 = bf16[32,2944]{1,0:T(8,128)(2,1)S(1)} collective-permute-done((bf16[32,2944]{1,0:T(8,128)(2,1)S(1)}, bf16[32,2944]{1,0:T(8,128)(2,1)S(1)}, u32[]{:S(2)}, u32[]{:S(2)}) %collective-permute-start.3) | collective-permute-done | bytes 188448 | tf_op jit(solution)/shard_map/ppermute | solution.py:138
  20.5 1.6 %collective-permute-start.4 = (bf16[64,2944]{1,0:T(8,128)(2,1)S(1)}, bf16[64,2944]{1,0:T(8,128)(2,1)S(1)}, u32[]{:S(2)}, u32[]{:S(2)}) collective-permute-start(bf16[64,2944]{1,0:T(8,128)(2,1)S(1)} %get-tuple-element.27), channel_id=1, source_target_pairs={{0,16},{1,3},{2,18},{3,1},{4,20},{5,7},{6,22},{7,5},{8,24},{9,11},... | collective-permute-start | bytes 1130504 | tf_op jit(solution)/shard_map/ppermute | solution.py:139
  22.1 6.1 %collective-permute-done.4 = bf16[64,2944]{1,0:T(8,128)(2,1)S(1)} collective-permute-done((bf16[64,2944]{1,0:T(8,128)(2,1)S(1)}, bf16[64,2944]{1,0:T(8,128)(2,1)S(1)}, u32[]{:S(2)}, u32[]{:S(2)}) %collective-permute-start.4) | collective-permute-done | bytes 376864 | tf_op jit(solution)/shard_map/ppermute | solution.py:139
  28.3 11.9 %copy.14.up_hbm = bf16[2,1,2880,720]{3,2,1,0:T(8,128)(2,1)} copy(bf16[2,1,2880,720]{2,3,1,0:T(8,128)(2,1)} %param.9) | data formatting | bytes 16588800 | tf_op args[3]
  40.2 3.5 %copy-done = bf16[2,1,2880,720]{3,2,1,0:T(8,128)(2,1)S(1)} copy-done((bf16[2,1,2880,720]{3,2,1,0:T(8,128)(2,1)S(1)}, bf16[2,1,2880,720]{3,2,1,0:T(8,128)(2,1)}, u32[]{:S(2)}) %copy-start) | copy-done | bytes 8294424
  43.8 3.4 %copy-done.2 = bf16[2,1,720,2880]{3,2,1,0:T(8,128)(2,1)S(1)} copy-done((bf16[2,1,720,2880]{3,2,1,0:T(8,128)(2,1)S(1)}, bf16[2,1,720,2880]{3,2,1,0:T(8,128)(2,1)}, u32[]{:S(2)}) %copy-start.2) | copy-done | bytes 8294424
  47.2 7.0 %ffn_0.1 = (bf16[128,2944]{1,0:T(8,128)(2,1)S(1)}, bf16[128,2944]{1,0:T(8,128)(2,1)S(1)}) custom-call(s32[2]{0:T(128)S(1)} %pad_add_fusion.ids_ref, bf16[128,2944]{1,0:T(8,128)(2,1)S(1)} %constant_dynamic-update-slice_fusion.5.near_ref, bf16[128,2944]{1,0:T(8,128)(2,1)S(1)} %collective-permute-done.5.far_ref, bf16[2,1,2880]{2,1,0:T(2,128)(2,1)S(1)} %copy.13.router_ref, ...), custom_call_target="tpu_custom_call" | custom-call | tf_op jit(solution)/shard_map/ffn_0/pallas_call | solution.py:76
  54.8 1.9 %collective-permute-done.6 = bf16[128,2944]{1,0:T(8,128)(2,1)S(1)} collective-permute-done((bf16[128,2944]{1,0:T(8,128)(2,1)S(1)}, bf16[128,2944]{1,0:T(8,128)(2,1)S(1)}, u32[]{:S(2)}, u32[]{:S(2)}) %collective-permute-start.6) | collective-permute-done | bytes 753696 | tf_op jit(solution)/shard_map/ppermute | solution.py:142
  56.8 1.6 %collective-permute-start.7 = (bf16[64,2944]{1,0:T(8,128)(2,1)S(1)}, bf16[64,2944]{1,0:T(8,128)(2,1)S(1)}, u32[]{:S(2)}, u32[]{:S(2)}) collective-permute-start(bf16[64,2944]{1,0:T(8,128)(2,1)S(1)} %slice.165), channel_id=1, source_target_pairs={{0,16},{1,3},{2,18},{3,1},{4,20},{5,7},{6,22},{7,5},{8,24},{9,11},... | collective-permute-start | bytes 1130504 | tf_op jit(solution)/shard_map/ppermute | solution.py:145
  58.4 6.1 %collective-permute-done.7 = bf16[64,2944]{1,0:T(8,128)(2,1)S(1)} collective-permute-done((bf16[64,2944]{1,0:T(8,128)(2,1)S(1)}, bf16[64,2944]{1,0:T(8,128)(2,1)S(1)}, u32[]{:S(2)}, u32[]{:S(2)}) %collective-permute-start.7) | collective-permute-done | bytes 376864 | tf_op jit(solution)/shard_map/ppermute | solution.py:145
  64.6 1.6 %collective-permute-start.8 = (bf16[32,2944]{1,0:T(8,128)(2,1)S(1)}, bf16[32,2944]{1,0:T(8,128)(2,1)S(1)}, u32[]{:S(2)}, u32[]{:S(2)}) collective-permute-start(bf16[32,2944]{1,0:T(8,128)(2,1)S(1)} %slice.167), channel_id=1, source_target_pairs={{0,2},{1,17},{2,0},{3,19},{4,6},{5,21},{6,4},{7,23},{8,10},{9,25},... | collective-permute-start | bytes 565256 | tf_op jit(solution)/shard_map/ppermute | solution.py:145
  66.2 4.1 %collective-permute-done.8 = bf16[32,2944]{1,0:T(8,128)(2,1)S(1)} collective-permute-done((bf16[32,2944]{1,0:T(8,128)(2,1)S(1)}, bf16[32,2944]{1,0:T(8,128)(2,1)S(1)}, u32[]{:S(2)}, u32[]{:S(2)}) %collective-permute-start.8) | collective-permute-done | bytes 188448 | tf_op jit(solution)/shard_map/ppermute | solution.py:145
  73.6 1.9 %collective-permute-done.9 = bf16[8,2944]{1,0:T(8,128)(2,1)S(1)} collective-permute-done((bf16[8,2944]{1,0:T(8,128)(2,1)S(1)}, bf16[8,2944]{1,0:T(8,128)(2,1)S(1)}, u32[]{:S(2)}, u32[]{:S(2)}) %collective-permute-start.9) | collective-permute-done | bytes 47136 | tf_op jit(solution)/shard_map/ppermute | solution.py:150
  75.4 1.9 %collective-permute-done.11 = bf16[8,2944]{1,0:T(8,128)(2,1)S(1)} collective-permute-done((bf16[8,2944]{1,0:T(8,128)(2,1)S(1)}, bf16[8,2944]{1,0:T(8,128)(2,1)S(1)}, u32[]{:S(2)}, u32[]{:S(2)}) %collective-permute-start.11) | collective-permute-done | bytes 47136 | tf_op jit(solution)/shard_map/ppermute | solution.py:150
  79.0 1.9 %collective-permute-start.14 = (bf16[8,2944]{1,0:T(8,128)(2,1)S(1)}, bf16[8,2944]{1,0:T(8,128)(2,1)S(1)}, u32[]{:S(2)}, u32[]{:S(2)}) collective-permute-start(bf16[8,2944]{1,0:T(8,128)(2,1)S(1)} %concatenate.32), channel_id=1, source_target_pairs={{0,12},{1,13},{2,14},{3,15},{4,0},{5,1},{6,2},{7,3},{8,4},{9,5},{1... | collective-permute-start | bytes 141320 | tf_op jit(solution)/shard_map/ppermute | solution.py:136
  81.5 2.0 %collective-permute-done.14 = bf16[8,2944]{1,0:T(8,128)(2,1)S(1)} collective-permute-done((bf16[8,2944]{1,0:T(8,128)(2,1)S(1)}, bf16[8,2944]{1,0:T(8,128)(2,1)S(1)}, u32[]{:S(2)}, u32[]{:S(2)}) %collective-permute-start.14) | collective-permute-done | bytes 47136 | tf_op jit(solution)/shard_map/ppermute | solution.py:136
  83.6 2.4 %collective-permute-done.13 = bf16[8,2944]{1,0:T(8,128)(2,1)S(1)} collective-permute-done((bf16[8,2944]{1,0:T(8,128)(2,1)S(1)}, bf16[8,2944]{1,0:T(8,128)(2,1)S(1)}, u32[]{:S(2)}, u32[]{:S(2)}) %collective-permute-start.13) | collective-permute-done | bytes 47136 | tf_op jit(solution)/shard_map/ppermute | solution.py:136
  88.4 5.9 %collective-permute-done.15 = bf16[32,2944]{1,0:T(8,128)(2,1)S(1)} collective-permute-done((bf16[32,2944]{1,0:T(8,128)(2,1)S(1)}, bf16[32,2944]{1,0:T(8,128)(2,1)S(1)}, u32[]{:S(2)}, u32[]{:S(2)}) %collective-permute-start.15) | collective-permute-done | bytes 188448 | tf_op jit(solution)/shard_map/ppermute | solution.py:138
  94.3 1.7 %collective-permute-start.16 = (bf16[64,2944]{1,0:T(8,128)(2,1)S(1)}, bf16[64,2944]{1,0:T(8,128)(2,1)S(1)}, u32[]{:S(2)}, u32[]{:S(2)}) collective-permute-start(bf16[64,2944]{1,0:T(8,128)(2,1)S(1)} %get-tuple-element.22), channel_id=1, source_target_pairs={{0,16},{1,3},{2,18},{3,1},{4,20},{5,7},{6,22},{7,5},{8,24},{9,11},... | collective-permute-start | bytes 1130504 | tf_op jit(solution)/shard_map/ppermute | solution.py:139
  96.0 6.0 %collective-permute-done.16 = bf16[64,2944]{1,0:T(8,128)(2,1)S(1)} collective-permute-done((bf16[64,2944]{1,0:T(8,128)(2,1)S(1)}, bf16[64,2944]{1,0:T(8,128)(2,1)S(1)}, u32[]{:S(2)}, u32[]{:S(2)}) %collective-permute-start.16) | collective-permute-done | bytes 376864 | tf_op jit(solution)/shard_map/ppermute | solution.py:139
  102.1 2.2 %collective-permute-done.17.far_ref = bf16[128,2944]{1,0:T(8,128)(2,1)S(1)} collective-permute-done((bf16[128,2944]{1,0:T(8,128)(2,1)S(1)}, bf16[128,2944]{1,0:T(8,128)(2,1)S(1)}, u32[]{:S(2)}, u32[]{:S(2)}) %collective-permute-start.17) | collective-permute-done | bytes 753696 | tf_op jit(solution)/shard_map/ppermute | solution.py:140
  104.3 3.5 %copy-done.1 = bf16[2,1,2880,720]{3,2,1,0:T(8,128)(2,1)S(1)} copy-done((bf16[2,1,2880,720]{3,2,1,0:T(8,128)(2,1)S(1)}, bf16[2,1,2880,720]{3,2,1,0:T(8,128)(2,1)}, u32[]{:S(2)}) %copy-start.1) | copy-done | bytes 8294424
  107.8 3.4 %copy-done.3 = bf16[2,1,720,2880]{3,2,1,0:T(8,128)(2,1)S(1)} copy-done((bf16[2,1,720,2880]{3,2,1,0:T(8,128)(2,1)S(1)}, bf16[2,1,720,2880]{3,2,1,0:T(8,128)(2,1)}, u32[]{:S(2)}) %copy-start.3) | copy-done | bytes 8294424
  111.2 7.0 %ffn_1.1 = (bf16[128,2944]{1,0:T(8,128)(2,1)S(1)}, bf16[128,2944]{1,0:T(8,128)(2,1)S(1)}) custom-call(s32[2]{0:T(128)S(1)} %pad_add_fusion.ids_ref, bf16[128,2944]{1,0:T(8,128)(2,1)S(1)} %constant_dynamic-update-slice_fusion.16.near_ref, bf16[128,2944]{1,0:T(8,128)(2,1)S(1)} %collective-permute-done.17.far_ref, bf16[2,1,2880]{2,1,0:T(2,128)(2,1)S(1)} %copy.13.router_ref, ...), custom_call_target="tpu_custom_call" | custom-call | tf_op jit(solution)/shard_map/ffn_1/pallas_call | solution.py:76
  118.4 2.1 %collective-permute-done.18 = bf16[128,2944]{1,0:T(8,128)(2,1)S(1)} collective-permute-done((bf16[128,2944]{1,0:T(8,128)(2,1)S(1)}, bf16[128,2944]{1,0:T(8,128)(2,1)S(1)}, u32[]{:S(2)}, u32[]{:S(2)}) %collective-permute-start.18) | collective-permute-done | bytes 753696 | tf_op jit(solution)/shard_map/ppermute | solution.py:142
  120.8 1.7 %collective-permute-start.19 = (bf16[64,2944]{1,0:T(8,128)(2,1)S(1)}, bf16[64,2944]{1,0:T(8,128)(2,1)S(1)}, u32[]{:S(2)}, u32[]{:S(2)}) collective-permute-start(bf16[64,2944]{1,0:T(8,128)(2,1)S(1)} %slice.164), channel_id=1, source_target_pairs={{0,16},{1,3},{2,18},{3,1},{4,20},{5,7},{6,22},{7,5},{8,24},{9,11},... | collective-permute-start | bytes 1130504 | tf_op jit(solution)/shard_map/ppermute | solution.py:145
  122.4 6.0 %collective-permute-done.19 = bf16[64,2944]{1,0:T(8,128)(2,1)S(1)} collective-permute-done((bf16[64,2944]{1,0:T(8,128)(2,1)S(1)}, bf16[64,2944]{1,0:T(8,128)(2,1)S(1)}, u32[]{:S(2)}, u32[]{:S(2)}) %collective-permute-start.19) | collective-permute-done | bytes 376864 | tf_op jit(solution)/shard_map/ppermute | solution.py:145
  128.5 1.7 %collective-permute-start.20 = (bf16[32,2944]{1,0:T(8,128)(2,1)S(1)}, bf16[32,2944]{1,0:T(8,128)(2,1)S(1)}, u32[]{:S(2)}, u32[]{:S(2)}) collective-permute-start(bf16[32,2944]{1,0:T(8,128)(2,1)S(1)} %slice.166), channel_id=1, source_target_pairs={{0,2},{1,17},{2,0},{3,19},{4,6},{5,21},{6,4},{7,23},{8,10},{9,25},... | collective-permute-start | bytes 565256 | tf_op jit(solution)/shard_map/ppermute | solution.py:145
  130.2 4.0 %collective-permute-done.20 = bf16[32,2944]{1,0:T(8,128)(2,1)S(1)} collective-permute-done((bf16[32,2944]{1,0:T(8,128)(2,1)S(1)}, bf16[32,2944]{1,0:T(8,128)(2,1)S(1)}, u32[]{:S(2)}, u32[]{:S(2)}) %collective-permute-start.20) | collective-permute-done | bytes 188448 | tf_op jit(solution)/shard_map/ppermute | solution.py:145
  138.8 2.2 %collective-permute-done.23 = bf16[8,2944]{1,0:T(8,128)(2,1)S(1)} collective-permute-done((bf16[8,2944]{1,0:T(8,128)(2,1)S(1)}, bf16[8,2944]{1,0:T(8,128)(2,1)S(1)}, u32[]{:S(2)}, u32[]{:S(2)}) %collective-permute-start.23) | collective-permute-done | bytes 47136 | tf_op jit(solution)/shard_map/ppermute | solution.py:150
  (82 shorter events, 24.4 us)
Async XLA Ops:
  0.0 28.3 %copy-start.5 = (bf16[2,1,2880]{2,0,1:T(2,128)(2,1)S(1)}, bf16[2,1,2880]{2,0,1:T(2,128)(2,1)}, u32[]{:S(2)}) copy-start(bf16[2,1,2880]{2,0,1:T(2,128)(2,1)} %param.11) | copy-start | bytes 34564
  3.8 7.0 %collective-permute-start.2 = (bf16[8,2944]{1,0:T(8,128)(2,1)S(1)}, bf16[8,2944]{1,0:T(8,128)(2,1)S(1)}, u32[]{:S(2)}, u32[]{:S(2)}) collective-permute-start(bf16[8,2944]{1,0:T(8,128)(2,1)S(1)} %concatenate.28), channel_id=1, source_target_pairs={{0,12},{1,13},{2,14},{3,15},{4,0},{5,1},{6,2},{7,3},{8,4},{9,5},{1... | collective-permute-start | bytes 141320 | tf_op jit(solution)/shard_map/ppermute | solution.py:136
  8.8 5.0 %collective-permute-start.1 = (bf16[8,2944]{1,0:T(8,128)(2,1)S(1)}, bf16[8,2944]{1,0:T(8,128)(2,1)S(1)}, u32[]{:S(2)}, u32[]{:S(2)}) collective-permute-start(bf16[8,2944]{1,0:T(8,128)(2,1)S(1)} %concatenate.28), channel_id=1, source_target_pairs={{0,8},{1,9},{2,10},{3,11},{4,12},{5,13},{6,14},{7,15},{8,0},{9,1},... | collective-permute-start | bytes 141320 | tf_op jit(solution)/shard_map/ppermute | solution.py:136
  8.9 5.9 %collective-permute-start = (bf16[8,2944]{1,0:T(8,128)(2,1)S(1)}, bf16[8,2944]{1,0:T(8,128)(2,1)S(1)}, u32[]{:S(2)}, u32[]{:S(2)}) collective-permute-start(bf16[8,2944]{1,0:T(8,128)(2,1)S(1)} %concatenate.28), channel_id=1, source_target_pairs={{0,4},{1,5},{2,6},{3,7},{4,8},{5,9},{6,10},{7,11},{8,12},{9,13},{1... | collective-permute-start | bytes 141320 | tf_op jit(solution)/shard_map/ppermute | solution.py:136
  14.7 5.7 %collective-permute-start.3 = (bf16[32,2944]{1,0:T(8,128)(2,1)S(1)}, bf16[32,2944]{1,0:T(8,128)(2,1)S(1)}, u32[]{:S(2)}, u32[]{:S(2)}) collective-permute-start(bf16[32,2944]{1,0:T(8,128)(2,1)S(1)} %pad_maximum_fusion), channel_id=1, source_target_pairs={{0,2},{1,17},{2,0},{3,19},{4,6},{5,21},{6,4},{7,23},{8,10},{9,25},... | collective-permute-start | bytes 565256 | tf_op jit(solution)/shard_map/ppermute | solution.py:138
  20.5 7.7 %collective-permute-start.4 = (bf16[64,2944]{1,0:T(8,128)(2,1)S(1)}, bf16[64,2944]{1,0:T(8,128)(2,1)S(1)}, u32[]{:S(2)}, u32[]{:S(2)}) collective-permute-start(bf16[64,2944]{1,0:T(8,128)(2,1)S(1)} %get-tuple-element.27), channel_id=1, source_target_pairs={{0,16},{1,3},{2,18},{3,1},{4,20},{5,7},{6,22},{7,5},{8,24},{9,11},... | collective-permute-start | bytes 1130504 | tf_op jit(solution)/shard_map/ppermute | solution.py:139
  28.2 12.1 %collective-permute-start.5 = (bf16[128,2944]{1,0:T(8,128)(2,1)S(1)}, bf16[128,2944]{1,0:T(8,128)(2,1)S(1)}, u32[]{:S(2)}, u32[]{:S(2)}) collective-permute-start(bf16[128,2944]{1,0:T(8,128)(2,1)S(1)} %constant_dynamic-update-slice_fusion.5.near_ref), channel_id=1, source_target_pairs={{0,1},{1,0},{2,3},{3,2},{4,5},{5,4},{6,7},{7,6},{8,9},{9,8},{10,11... | collective-permute-start | bytes 2261000 | tf_op jit(solution)/shard_map/ppermute | solution.py:140
  40.2 3.5 %copy-start = (bf16[2,1,2880,720]{3,2,1,0:T(8,128)(2,1)S(1)}, bf16[2,1,2880,720]{3,2,1,0:T(8,128)(2,1)}, u32[]{:S(2)}) copy-start(bf16[2,1,2880,720]{3,2,1,0:T(8,128)(2,1)} %copy.14.up_hbm) | copy-start | bytes 24883204
  43.7 3.4 %copy-start.2 = (bf16[2,1,720,2880]{3,2,1,0:T(8,128)(2,1)S(1)}, bf16[2,1,720,2880]{3,2,1,0:T(8,128)(2,1)}, u32[]{:S(2)}) copy-start(bf16[2,1,720,2880]{3,2,1,0:T(8,128)(2,1)} %down_hbm.3) | copy-start | bytes 24883204
  54.2 2.4 %collective-permute-start.6 = (bf16[128,2944]{1,0:T(8,128)(2,1)S(1)}, bf16[128,2944]{1,0:T(8,128)(2,1)S(1)}, u32[]{:S(2)}, u32[]{:S(2)}) collective-permute-start(bf16[128,2944]{1,0:T(8,128)(2,1)S(1)} %get-tuple-element.10), channel_id=1, source_target_pairs={{0,1},{1,0},{2,3},{3,2},{4,5},{5,4},{6,7},{7,6},{8,9},{9,8},{10,11... | collective-permute-start | bytes 2261000 | tf_op jit(solution)/shard_map/ppermute | solution.py:142
  56.8 7.7 %collective-permute-start.7 = (bf16[64,2944]{1,0:T(8,128)(2,1)S(1)}, bf16[64,2944]{1,0:T(8,128)(2,1)S(1)}, u32[]{:S(2)}, u32[]{:S(2)}) collective-permute-start(bf16[64,2944]{1,0:T(8,128)(2,1)S(1)} %slice.165), channel_id=1, source_target_pairs={{0,16},{1,3},{2,18},{3,1},{4,20},{5,7},{6,22},{7,5},{8,24},{9,11},... | collective-permute-start | bytes 1130504 | tf_op jit(solution)/shard_map/ppermute | solution.py:145
  64.6 14.0 %copy-start.4 = (bf16[8,2880]{1,0:T(8,128)(2,1)S(1)}, bf16[8,2880]{1,0:T(8,128)(2,1)}, u32[]{:S(2)}) copy-start(bf16[8,2880]{1,0:T(8,128)(2,1)} %param.6) | copy-start | bytes 138244
  64.6 5.6 %collective-permute-start.8 = (bf16[32,2944]{1,0:T(8,128)(2,1)S(1)}, bf16[32,2944]{1,0:T(8,128)(2,1)S(1)}, u32[]{:S(2)}, u32[]{:S(2)}) collective-permute-start(bf16[32,2944]{1,0:T(8,128)(2,1)S(1)} %slice.167), channel_id=1, source_target_pairs={{0,2},{1,17},{2,0},{3,19},{4,6},{5,21},{6,4},{7,23},{8,10},{9,25},... | collective-permute-start | bytes 565256 | tf_op jit(solution)/shard_map/ppermute | solution.py:145
  70.3 5.1 %collective-permute-start.9 = (bf16[8,2944]{1,0:T(8,128)(2,1)S(1)}, bf16[8,2944]{1,0:T(8,128)(2,1)S(1)}, u32[]{:S(2)}, u32[]{:S(2)}) collective-permute-start(bf16[8,2944]{1,0:T(8,128)(2,1)S(1)} %get-tuple-element.24), channel_id=1, source_target_pairs={{0,12},{1,13},{2,14},{3,15},{4,0},{5,1},{6,2},{7,3},{8,4},{9,5},{1... | collective-permute-start | bytes 141320 | tf_op jit(solution)/shard_map/ppermute | solution.py:150
  71.5 5.9 %collective-permute-start.11 = (bf16[8,2944]{1,0:T(8,128)(2,1)S(1)}, bf16[8,2944]{1,0:T(8,128)(2,1)S(1)}, u32[]{:S(2)}, u32[]{:S(2)}) collective-permute-start(bf16[8,2944]{1,0:T(8,128)(2,1)S(1)} %get-tuple-element.25), channel_id=1, source_target_pairs={{0,4},{1,5},{2,6},{3,7},{4,8},{5,9},{6,10},{7,11},{8,12},{9,13},{1... | collective-permute-start | bytes 141320 | tf_op jit(solution)/shard_map/ppermute | solution.py:150
  72.4 6.0 %collective-permute-start.10 = (bf16[8,2944]{1,0:T(8,128)(2,1)S(1)}, bf16[8,2944]{1,0:T(8,128)(2,1)S(1)}, u32[]{:S(2)}, u32[]{:S(2)}) collective-permute-start(bf16[8,2944]{1,0:T(8,128)(2,1)S(1)} %get-tuple-element.26), channel_id=1, source_target_pairs={{0,8},{1,9},{2,10},{3,11},{4,12},{5,13},{6,14},{7,15},{8,0},{9,1},... | collective-permute-start | bytes 141320 | tf_op jit(solution)/shard_map/ppermute | solution.py:150
  79.0 4.6 %collective-permute-start.14 = (bf16[8,2944]{1,0:T(8,128)(2,1)S(1)}, bf16[8,2944]{1,0:T(8,128)(2,1)S(1)}, u32[]{:S(2)}, u32[]{:S(2)}) collective-permute-start(bf16[8,2944]{1,0:T(8,128)(2,1)S(1)} %concatenate.32), channel_id=1, source_target_pairs={{0,12},{1,13},{2,14},{3,15},{4,0},{5,1},{6,2},{7,3},{8,4},{9,5},{1... | collective-permute-start | bytes 141320 | tf_op jit(solution)/shard_map/ppermute | solution.py:136
  80.9 5.0 %collective-permute-start.13 = (bf16[8,2944]{1,0:T(8,128)(2,1)S(1)}, bf16[8,2944]{1,0:T(8,128)(2,1)S(1)}, u32[]{:S(2)}, u32[]{:S(2)}) collective-permute-start(bf16[8,2944]{1,0:T(8,128)(2,1)S(1)} %concatenate.32), channel_id=1, source_target_pairs={{0,8},{1,9},{2,10},{3,11},{4,12},{5,13},{6,14},{7,15},{8,0},{9,1},... | collective-permute-start | bytes 141320 | tf_op jit(solution)/shard_map/ppermute | solution.py:136
  80.9 5.9 %collective-permute-start.12 = (bf16[8,2944]{1,0:T(8,128)(2,1)S(1)}, bf16[8,2944]{1,0:T(8,128)(2,1)S(1)}, u32[]{:S(2)}, u32[]{:S(2)}) collective-permute-start(bf16[8,2944]{1,0:T(8,128)(2,1)S(1)} %concatenate.32), channel_id=1, source_target_pairs={{0,4},{1,5},{2,6},{3,7},{4,8},{5,9},{6,10},{7,11},{8,12},{9,13},{1... | collective-permute-start | bytes 141320 | tf_op jit(solution)/shard_map/ppermute | solution.py:136
  86.8 7.5 %collective-permute-start.15 = (bf16[32,2944]{1,0:T(8,128)(2,1)S(1)}, bf16[32,2944]{1,0:T(8,128)(2,1)S(1)}, u32[]{:S(2)}, u32[]{:S(2)}) collective-permute-start(bf16[32,2944]{1,0:T(8,128)(2,1)S(1)} %pad_maximum_fusion.1), channel_id=1, source_target_pairs={{0,2},{1,17},{2,0},{3,19},{4,6},{5,21},{6,4},{7,23},{8,10},{9,25},... | collective-permute-start | bytes 565256 | tf_op jit(solution)/shard_map/ppermute | solution.py:138
  94.3 7.7 %collective-permute-start.16 = (bf16[64,2944]{1,0:T(8,128)(2,1)S(1)}, bf16[64,2944]{1,0:T(8,128)(2,1)S(1)}, u32[]{:S(2)}, u32[]{:S(2)}) collective-permute-start(bf16[64,2944]{1,0:T(8,128)(2,1)S(1)} %get-tuple-element.22), channel_id=1, source_target_pairs={{0,16},{1,3},{2,18},{3,1},{4,20},{5,7},{6,22},{7,5},{8,24},{9,11},... | collective-permute-start | bytes 1130504 | tf_op jit(solution)/shard_map/ppermute | solution.py:139
  102.0 2.3 %collective-permute-start.17 = (bf16[128,2944]{1,0:T(8,128)(2,1)S(1)}, bf16[128,2944]{1,0:T(8,128)(2,1)S(1)}, u32[]{:S(2)}, u32[]{:S(2)}) collective-permute-start(bf16[128,2944]{1,0:T(8,128)(2,1)S(1)} %constant_dynamic-update-slice_fusion.16.near_ref), channel_id=1, source_target_pairs={{0,1},{1,0},{2,3},{3,2},{4,5},{5,4},{6,7},{7,6},{8,9},{9,8},{10,11... | collective-permute-start | bytes 2261000 | tf_op jit(solution)/shard_map/ppermute | solution.py:140
  104.3 3.5 %copy-start.1 = (bf16[2,1,2880,720]{3,2,1,0:T(8,128)(2,1)S(1)}, bf16[2,1,2880,720]{3,2,1,0:T(8,128)(2,1)}, u32[]{:S(2)}) copy-start(bf16[2,1,2880,720]{3,2,1,0:T(8,128)(2,1)} %copy.14.up_hbm) | copy-start | bytes 24883204
  107.8 3.4 %copy-start.3 = (bf16[2,1,720,2880]{3,2,1,0:T(8,128)(2,1)S(1)}, bf16[2,1,720,2880]{3,2,1,0:T(8,128)(2,1)}, u32[]{:S(2)}) copy-start(bf16[2,1,720,2880]{3,2,1,0:T(8,128)(2,1)} %down_hbm.3) | copy-start | bytes 24883204
  118.2 2.3 %collective-permute-start.18 = (bf16[128,2944]{1,0:T(8,128)(2,1)S(1)}, bf16[128,2944]{1,0:T(8,128)(2,1)S(1)}, u32[]{:S(2)}, u32[]{:S(2)}) collective-permute-start(bf16[128,2944]{1,0:T(8,128)(2,1)S(1)} %get-tuple-element.12), channel_id=1, source_target_pairs={{0,1},{1,0},{2,3},{3,2},{4,5},{5,4},{6,7},{7,6},{8,9},{9,8},{10,11... | collective-permute-start | bytes 2261000 | tf_op jit(solution)/shard_map/ppermute | solution.py:142
  120.8 7.7 %collective-permute-start.19 = (bf16[64,2944]{1,0:T(8,128)(2,1)S(1)}, bf16[64,2944]{1,0:T(8,128)(2,1)S(1)}, u32[]{:S(2)}, u32[]{:S(2)}) collective-permute-start(bf16[64,2944]{1,0:T(8,128)(2,1)S(1)} %slice.164), channel_id=1, source_target_pairs={{0,16},{1,3},{2,18},{3,1},{4,20},{5,7},{6,22},{7,5},{8,24},{9,11},... | collective-permute-start | bytes 1130504 | tf_op jit(solution)/shard_map/ppermute | solution.py:145
  128.5 5.6 %collective-permute-start.20 = (bf16[32,2944]{1,0:T(8,128)(2,1)S(1)}, bf16[32,2944]{1,0:T(8,128)(2,1)S(1)}, u32[]{:S(2)}, u32[]{:S(2)}) collective-permute-start(bf16[32,2944]{1,0:T(8,128)(2,1)S(1)} %slice.166), channel_id=1, source_target_pairs={{0,2},{1,17},{2,0},{3,19},{4,6},{5,21},{6,4},{7,23},{8,10},{9,25},... | collective-permute-start | bytes 565256 | tf_op jit(solution)/shard_map/ppermute | solution.py:145
  134.2 4.6 %collective-permute-start.21 = (bf16[8,2944]{1,0:T(8,128)(2,1)S(1)}, bf16[8,2944]{1,0:T(8,128)(2,1)S(1)}, u32[]{:S(2)}, u32[]{:S(2)}) collective-permute-start(bf16[8,2944]{1,0:T(8,128)(2,1)S(1)} %get-tuple-element.19), channel_id=1, source_target_pairs={{0,12},{1,13},{2,14},{3,15},{4,0},{5,1},{6,2},{7,3},{8,4},{9,5},{1... | collective-permute-start | bytes 141320 | tf_op jit(solution)/shard_map/ppermute | solution.py:150
  135.1 5.9 %collective-permute-start.23 = (bf16[8,2944]{1,0:T(8,128)(2,1)S(1)}, bf16[8,2944]{1,0:T(8,128)(2,1)S(1)}, u32[]{:S(2)}, u32[]{:S(2)}) collective-permute-start(bf16[8,2944]{1,0:T(8,128)(2,1)S(1)} %get-tuple-element.20), channel_id=1, source_target_pairs={{0,4},{1,5},{2,6},{3,7},{4,8},{5,9},{6,10},{7,11},{8,12},{9,13},{1... | collective-permute-start | bytes 141320 | tf_op jit(solution)/shard_map/ppermute | solution.py:150
  136.3 5.7 %collective-permute-start.22 = (bf16[8,2944]{1,0:T(8,128)(2,1)S(1)}, bf16[8,2944]{1,0:T(8,128)(2,1)S(1)}, u32[]{:S(2)}, u32[]{:S(2)}) collective-permute-start(bf16[8,2944]{1,0:T(8,128)(2,1)S(1)} %get-tuple-element.21), channel_id=1, source_target_pairs={{0,8},{1,9},{2,10},{3,11},{4,12},{5,13},{6,14},{7,15},{8,0},{9,1},... | collective-permute-start | bytes 141320 | tf_op jit(solution)/shard_map/ppermute | solution.py:150

commit v2 on v1

--- a/solution.py
+++ b/solution.py
@@ -20,41 +20,72 @@
     return -(-value // unit) * unit
 
 
-def column_blocks(extent, step):
-    return [(start, min(step, extent - start)) for start in range(0, extent, step)]
-
-
-def ffn_kernel(layer, width, up_blocks, down_blocks, ids_ref, near_ref, far_ref, router_ref, up_hbm, down_hbm, near_out, far_out, rows_ref, hidden_ref, *scratch):
-    up_parts, down_parts = scratch[: len(up_blocks)], scratch[len(up_blocks) : -1]
-    sems = scratch[-1]
-    copies = []
-    for index, (start, size) in enumerate(up_blocks):
-        copies.append(pltpu.make_async_copy(up_hbm.at[layer, 0, :, pl.ds(start, size)], up_parts[index], sems.at[index]))
-    for index, (start, size) in enumerate(down_blocks):
-        copies.append(
-            pltpu.make_async_copy(down_hbm.at[layer, 0, :, pl.ds(start, size)], down_parts[index], sems.at[len(up_blocks) + index])
-        )
-    for copy in copies:
-        copy.start()
-    half = near_ref.shape[0]
-    model = router_ref.shape[-1]
+VMEM = pl.BlockSpec(memory_space=pltpu.VMEM)
+SMEM = pl.BlockSpec(memory_space=pltpu.SMEM)
+
+
+def member_tail(layer, shift, lanes, routes_ref, placement_ref):
+    top_k, tok_rows = routes_ref.shape[1:]
+    experts = placement_ref.shape[1]
+    ids = lax.broadcasted_iota(jnp.int32, (experts, tok_rows), 0)
+    named = jnp.zeros((experts, tok_rows), jnp.float32)
+    for choice in range(top_k):
+        named = jnp.where(ids == routes_ref[layer, choice : choice + 1, :], 1.0, named)
+    lane = lax.broadcasted_iota(jnp.int32, (lanes, experts), 0)
+    served = jnp.where(lane == placement_ref[layer : layer + 1, :] + shift, 1.0, 0.0)
+    return lax.dot_general(named, served, (((0,), (1,)), ((), ())), preferred_element_type=jnp.float32)
+
+
+def write_payload(values, tail_rows, model, tail, payload_ref):
+    inverse = lax.rsqrt(jnp.mean(values * values, axis=-1, keepdims=True) + 1e-05)
+    normed = (values * inverse).astype(jnp.bfloat16)
+    payload_ref[:, :tail] = normed[:, :tail]
+    payload_ref[:, tail:] = tail_rows.astype(jnp.bfloat16)
+    if model > tail:
+        payload_ref[:, tail:model] = normed[:, tail:]
+
+
+def first_kernel(model, tail, tokens_ref, routes_ref, placement_ref, payload_ref, tails_ref):
+    lanes = payload_ref.shape[1] - tail
+    for layer in range(routes_ref.shape[0]):
+        tails_ref[layer] = member_tail(layer, model - tail, lanes, routes_ref, placement_ref)
+    write_payload(tokens_ref[...].astype(jnp.float32), tails_ref[0], model, tail, payload_ref)
+
+
+def update_kernel(model, tail, layer, last, own_ref, *refs):
+    pieces, (stream_ref, tails_ref, updated_ref), more = refs[: len(refs) - 3 - (not last)], refs[len(refs) - 3 - (not last) :][:3], refs[len(refs) - (not last) :]
+    total = own_ref[...]
+    for piece in pieces:
+        total = total + piece[...].astype(jnp.float32)
+    denominator = jnp.maximum(jnp.sum(total[:, model:], axis=1, keepdims=True), 0.5)
+    updated = (stream_ref[...].astype(jnp.float32) + total[:, :model] / denominator).astype(jnp.bfloat16)
+    updated_ref[...] = updated
+    if not last:
+        write_payload(updated.astype(jnp.float32), tails_ref[layer + 1], model, tail, more[0])
+
+
+def ffn_kernel(layer, near_ref, far_ref, router_ref, up_ref, down_ref, near_out, far_out, rows_ref, hidden_ref):
+    half, width = near_ref.shape
+    model, units = router_ref.shape[-1], up_ref.shape[2]
     rows_ref[:half, :] = near_ref[...]
     rows_ref[half:, :] = far_ref[...]
-    slot, block = ids_ref[0], ids_ref[1]
+    slot, block = lax.axis_index("expert"), lax.axis_index("dp")
     tail = model // LANES * LANES
     lane = lax.broadcasted_iota(jnp.int32, (2 * half, width - tail), 1)
     here = lane == (model - tail) + slot
     member = jnp.sum(jnp.where(here, rows_ref[:, tail:].astype(jnp.float32), 0.0), axis=1, keepdims=True)
-    router = router_ref[layer].astype(jnp.float32)
-    logits = jnp.sum(rows_ref[:, :model].astype(jnp.float32) * router, axis=1, keepdims=True)
-    gate = jax.nn.sigmoid(logits).astype(jnp.bfloat16).astype(jnp.float32) * member
-    for index, (start, size) in enumerate(up_blocks):
-        copies[index].wait()
-        raw = jnp.dot(rows_ref[:, :model], up_parts[index][...], preferred_element_type=jnp.float32)
+    by_rows = (((1,), (1,)), ((), ()))
+    logits = lax.dot_general(rows_ref[:, :model], router_ref[...], by_rows, preferred_element_type=jnp.float32)
+    gate = jax.nn.sigmoid(logits[:, layer : layer + 1]).astype(jnp.bfloat16).astype(jnp.float32) * member
+    for start in range(0, units, 256):
+        size = min(256, units - start)
+        raw = lax.dot_general(
+            rows_ref[:, :model], up_ref[layer, 0, start : start + size, :], by_rows, preferred_element_type=jnp.float32
+        )
         hidden_ref[:, start : start + size] = jax.nn.silu(raw).astype(jnp.bfloat16)
-    for index, (start, size) in enumerate(down_blocks):
-        copies[len(up_blocks) + index].wait()
-        part = jnp.dot(hidden_ref[...], down_parts[index][...], preferred_element_type=jnp.float32)
+    for start in range(0, model, 768):
+        size = min(768, model - start)
+        part = jnp.dot(hidden_ref[...], down_ref[layer, 0, :, start : start + size], preferred_element_type=jnp.float32)
         weighted = (part.astype(jnp.bfloat16).astype(jnp.float32) * gate).astype(jnp.bfloat16)
         near_out[:, start : start + size] = weighted[:half]
         far_out[:, start : start + size] = weighted[half:]
@@ -63,32 +94,18 @@
     far_out[:, model:] = sent[half:]
 
 
-def expert_ffn(layer, ids, near, far, router, up, down):
+def expert_ffn(layer, near, far, router, up, down):
     half, width = near.shape
-    model, units = up.shape[2], up.shape[3]
-    up_blocks = column_blocks(units, 256)
-    down_blocks = column_blocks(model, 768)
-    scratch = [pltpu.VMEM((2 * half, width), jnp.bfloat16), pltpu.VMEM((2 * half, units), jnp.bfloat16)]
-    scratch += [pltpu.VMEM((model, size), jnp.bfloat16) for _, size in up_blocks]
-    scratch += [pltpu.VMEM((units, size), jnp.bfloat16) for _, size in down_blocks]
-    scratch += [pltpu.SemaphoreType.DMA((len(up_blocks) + len(down_blocks),))]
-    vmem = pl.BlockSpec(memory_space=pltpu.VMEM)
+    units = up.shape[2]
     return pl.pallas_call(
-        functools.partial(ffn_kernel, layer, width, up_blocks, down_blocks),
+        functools.partial(ffn_kernel, layer),
         out_shape=[jax.ShapeDtypeStruct((half, width), jnp.bfloat16)] * 2,
-        in_specs=[
-            pl.BlockSpec(memory_space=pltpu.SMEM),
-            vmem,
-            vmem,
-            vmem,
-            pl.BlockSpec(memory_space=pl.ANY),
-            pl.BlockSpec(memory_space=pl.ANY),
-        ],
-        out_specs=[vmem, vmem],
-        scratch_shapes=scratch,
-        compiler_params=pltpu.CompilerParams(vmem_limit_bytes=32 * 1024 * 1024),
+        in_specs=[VMEM] * 5,
+        out_specs=[VMEM] * 2,
+        scratch_shapes=[pltpu.VMEM((2 * half, width), jnp.bfloat16), pltpu.VMEM((2 * half, units), jnp.bfloat16)],
+        compiler_params=pltpu.CompilerParams(vmem_limit_bytes=16 * 1024 * 1024),
         name=f"ffn_{layer}",
-    )(ids, near, far, router, up, down)
+    )(near, far, router, up, down)
 
 
 def dense_moves(groups, columns):
@@ -121,36 +138,47 @@
     layers, tok_rows, _ = routes.shape
     model = tokens.shape[1]
     width = round_up(model + columns, LANES)
+    tail = model // LANES * LANES
     lengths, shift, first_swap, second_swap, core_swap = dense_moves(groups, columns)
     axes = ("dp", "expert")
-    ids = jnp.stack([lax.axis_index("expert"), lax.axis_index("dp")]).astype(jnp.int32)
-    slots = jnp.arange(columns, dtype=jnp.int32)
+    up_rows, router = jnp.swapaxes(up_weight, 2, 3), router_weight.reshape(layers, model)
+    small = pltpu.CompilerParams(vmem_limit_bytes=4 * 1024 * 1024)
+    payload_shape = jax.ShapeDtypeStruct((tok_rows, width), jnp.bfloat16)
     stream = tokens
+    own, tails = pl.pallas_call(
+        functools.partial(first_kernel, model, tail),
+        out_shape=[payload_shape, jax.ShapeDtypeStruct((layers, tok_rows, width - tail), jnp.float32)],
+        in_specs=[VMEM] * 3,
+        out_specs=[VMEM] * 2,
+        compiler_params=small,
+        cost_estimate=pl.CostEstimate(flops=20_000_000_000, transcendentals=0, bytes_accessed=0),
+        name="first",
+    )(tokens, jnp.swapaxes(routes, 1, 2), placement)
 
     for layer in range(layers):
-        chosen = routes[layer][:, :, None] == slots[None, None, :]
-        target = jnp.sum(jnp.where(chosen, placement[layer][None, None, :], 0), axis=2)
-        member = jnp.any(target[:, :, None] == slots[None, None, :], axis=1).astype(jnp.bfloat16)
-        padding = jnp.zeros((tok_rows, width - model - columns), jnp.bfloat16)
-        own = jnp.concatenate([rms_rows(stream), member, padding], axis=1)
         line = [own] + [lax.ppermute(own, axes, shift(step)) for step in range(1, lengths)]
         rows = jnp.concatenate(line, axis=0)
         rows = jnp.concatenate([rows, lax.ppermute(rows, axes, first_swap)], axis=0)
         near = jnp.concatenate([rows, lax.ppermute(rows, axes, second_swap)], axis=0)
         far = lax.ppermute(near, axes, core_swap)
-        near_out, far_out = expert_ffn(layer, ids, near, far, router_weight, up_weight, down_weight)
+        near_out, far_out = expert_ffn(layer, near, far, router, up_rows, down_weight)
         total = near_out.astype(jnp.float32) + lax.ppermute(far_out, axes, core_swap).astype(jnp.float32)
         for swap in (second_swap, first_swap):
             half = total.shape[0] // 2
             moved = lax.ppermute(total[half:].astype(jnp.bfloat16), axes, swap)
             total = total[:half] + moved.astype(jnp.float32)
         pieces = total.reshape(lengths, tok_rows, width)
-        summed = pieces[0]
-        for step in range(1, lengths):
-            summed = summed + lax.ppermute(pieces[step].astype(jnp.bfloat16), axes, shift(lengths - step)).astype(jnp.float32)
-        denominator = jnp.maximum(jnp.sum(summed[:, model:], axis=1, keepdims=True), 0.5)
-        updated = stream.astype(jnp.float32) + summed[:, :model] / denominator
-        stream = updated.astype(jnp.bfloat16)
+        arrived = [lax.ppermute(pieces[step].astype(jnp.bfloat16), axes, shift(lengths - step)) for step in range(1, lengths)]
+        last = layer + 1 == layers
+        outs = pl.pallas_call(
+            functools.partial(update_kernel, model, tail, layer, last),
+            out_shape=[jax.ShapeDtypeStruct(stream.shape, jnp.bfloat16)] + [payload_shape] * (not last),
+            in_specs=[VMEM] * (len(arrived) + 3),
+            out_specs=[VMEM] * (2 - last),
+            compiler_params=small,
+            name=f"update_{layer}",
+        )(pieces[0], *arrived, stream, tails)
+        stream, own = outs[0], outs[-1]
     return stream
 
 

time: 144 us -> 110 us (0.76)
  local copies, waits for them, and re-layouts: 27.8 us -> 3.59 us
  Pallas kernels: 14.1 us -> 7.62 us
  other arithmetic: 4.34 us -> 0.55 us
  starting transfers between devices: 28.9 us -> 31.3 us
    unnamed x22 -> x30, local copies, waits for them, and re-layouts: 25.8 us -> 3.29 us
    pallas_call x2 -> x5, Pallas kernels: 14.1 us -> 7.62 us  [the longest x2 6.38 us: expert_ffn(): pl.pallas_call(functools.partial(ffn_kernel, layer), out_shape=[jax.Shape...]
    ppermute x6, waiting for transfers between devices: 9.2 us -> 4.96 us  [dense_device(): lax.ppermute(pieces[step].astype(jnp.bfloat16), axes, shift(lengths - step))]
    ppermute x2, waiting for transfers between devices: 2.23 us -> 4.45 us  [dense_device(): far = lax.ppermute(near, axes, core_swap)]
    reduce_sum x5 -> x0, other arithmetic: 1.8 us -> none  [the longest x2 1.15 us: rms_rows(): jnp.mean(values * values, axis=-1, keepdims=True) + 1e-05]
    convert_element_type x5 -> x0, other arithmetic: 1.68 us -> none  [the longest x2 0.95 us: rms_rows(): return (values * inverse).astype(jnp.bfloat16)]
    ppermute x6, starting transfers between devices: 8.62 us -> 10.2 us  [dense_device(): lax.ppermute(own, axes, shift(step))]
    ppermute x6, starting transfers between devices: 6.53 us -> 7.98 us  [dense_device(): lax.ppermute(pieces[step].astype(jnp.bfloat16), axes, shift(lengths - step))]
  transfers between devices with their start and end apart: 24 -> 24, of which waited for: 23 -> 22; matrix products, arithmetic and copies ran while one was open for 9% -> 0% of each run, Pallas kernels for 0% -> 0%
where the time goes in v2:
time: 110 us
  waiting for transfers between devices  66.5 us (60%)
  starting transfers between devices  31.3 us (28%)
  Pallas kernels  7.62 us (7%)
  local copies, waits for them, and re-layouts  3.59 us (3%)
    ppermute x4, waiting for transfers between devices, dense_device(): moved = lax.ppermute(total[half:].astype(jnp.bfloat16), axes, swap)  20.4 us
    ppermute x2, waiting for transfers between devices, dense_device(): lax.ppermute(rows, axes, second_swap)  12.2 us
    ppermute x6, starting transfers between devices, dense_device(): lax.ppermute(own, axes, shift(step))  10.2 us
    ppermute x6, waiting for transfers between devices, dense_device(): lax.ppermute(own, axes, shift(step))  10.2 us
    ppermute x2, waiting for transfers between devices, dense_device(): rows = jnp.concatenate([rows, lax.ppermute(rows, axes, first_swap)], axis=0)  10.1 us
    ppermute x6, starting transfers between devices, dense_device(): lax.ppermute(pieces[step].astype(jnp.bfloat16), axes, shift(lengths - step))  7.98 us
    pallas_call x2, Pallas kernels, expert_ffn(): pl.pallas_call(functools.partial(ffn_kernel, layer), out_shape=[jax.Shape...  6.38 us
    ppermute x4, starting transfers between devices, dense_device(): moved = lax.ppermute(total[half:].astype(jnp.bfloat16), axes, swap)  6.27 us
  transfers between devices with their start and end apart: 24, of which 22 were waited for; matrix products, arithmetic and copies ran while one was open for 0% of the time, Pallas kernels for 0%

profile of v2, /device:TPU:0, one launch (start us, length us, event | category | flops | bytes accessed | tf_op | source)
XLA Modules:
  0.0 109.8 jit_solution(16818171164293567695)
XLA Ops:
  1.0 1.1 %copy-done.3 = s32[2,8,4]{1,2,0:T(4,128)S(1)} copy-done((s32[2,8,4]{1,2,0:T(4,128)S(1)}, s32[2,8,4]{1,2,0:T(4,128)}, u32[]{:S(2)}) %copy-start.3) | copy-done | bytes 280
  3.4 5.1 %collective-permute-start.2 = (bf16[8,2944]{1,0:T(8,128)(2,1)S(1)}, bf16[8,2944]{1,0:T(8,128)(2,1)S(1)}, u32[]{:S(2)}, u32[]{:S(2)}) collective-permute-start(bf16[8,2944]{1,0:T(8,128)(2,1)S(1)} %get-tuple-element.13), channel_id=1, source_target_pairs={{0,12},{1,13},{2,14},{3,15},{4,0},{5,1},{6,2},{7,3},{8,4},{9,5},{1... | collective-permute-start | bytes 141320 | tf_op jit(solution)/shard_map/ppermute | solution.py:159
  10.4 3.0 %collective-permute-done.1 = bf16[8,2944]{1,0:T(8,128)(2,1)S(1)} collective-permute-done((bf16[8,2944]{1,0:T(8,128)(2,1)S(1)}, bf16[8,2944]{1,0:T(8,128)(2,1)S(1)}, u32[]{:S(2)}, u32[]{:S(2)}) %collective-permute-start.1) | collective-permute-done | bytes 47136 | tf_op jit(solution)/shard_map/ppermute | solution.py:159
  14.4 1.6 %collective-permute-start.3 = (bf16[32,2944]{1,0:T(8,128)(2,1)S(1)}, bf16[32,2944]{1,0:T(8,128)(2,1)S(1)}, u32[]{:S(2)}, u32[]{:S(2)}) collective-permute-start(bf16[32,2944]{1,0:T(8,128)(2,1)S(1)} %pad_maximum_fusion), channel_id=1, source_target_pairs={{0,2},{1,17},{2,0},{3,19},{4,6},{5,21},{6,4},{7,23},{8,10},{9,25},... | collective-permute-start | bytes 565256 | tf_op jit(solution)/shard_map/ppermute | solution.py:161
  16.0 4.1 %collective-permute-done.3 = bf16[32,2944]{1,0:T(8,128)(2,1)S(1)} collective-permute-done((bf16[32,2944]{1,0:T(8,128)(2,1)S(1)}, bf16[32,2944]{1,0:T(8,128)(2,1)S(1)}, u32[]{:S(2)}, u32[]{:S(2)}) %collective-permute-start.3) | collective-permute-done | bytes 188448 | tf_op jit(solution)/shard_map/ppermute | solution.py:161
  20.1 1.6 %collective-permute-start.4 = (bf16[64,2944]{1,0:T(8,128)(2,1)S(1)}, bf16[64,2944]{1,0:T(8,128)(2,1)S(1)}, u32[]{:S(2)}, u32[]{:S(2)}) collective-permute-start(bf16[64,2944]{1,0:T(8,128)(2,1)S(1)} %get-tuple-element.33), channel_id=1, source_target_pairs={{0,16},{1,3},{2,18},{3,1},{4,20},{5,7},{6,22},{7,5},{8,24},{9,11},... | collective-permute-start | bytes 1130504 | tf_op jit(solution)/shard_map/ppermute | solution.py:162
  21.7 6.1 %collective-permute-done.4 = bf16[64,2944]{1,0:T(8,128)(2,1)S(1)} collective-permute-done((bf16[64,2944]{1,0:T(8,128)(2,1)S(1)}, bf16[64,2944]{1,0:T(8,128)(2,1)S(1)}, u32[]{:S(2)}, u32[]{:S(2)}) %collective-permute-start.4) | collective-permute-done | bytes 376864 | tf_op jit(solution)/shard_map/ppermute | solution.py:162
  27.9 2.2 %collective-permute-done.5.far_ref = bf16[128,2944]{1,0:T(8,128)(2,1)S(1)} collective-permute-done((bf16[128,2944]{1,0:T(8,128)(2,1)S(1)}, bf16[128,2944]{1,0:T(8,128)(2,1)S(1)}, u32[]{:S(2)}, u32[]{:S(2)}) %collective-permute-start.5) | collective-permute-done | bytes 753696 | tf_op jit(solution)/shard_map/ppermute | solution.py:163
  30.2 3.2 %ffn_0.1 = (bf16[128,2944]{1,0:T(8,128)(2,1)S(1)}, bf16[128,2944]{1,0:T(8,128)(2,1)S(1)}) custom-call(bf16[128,2944]{1,0:T(8,128)(2,1)S(1)} %constant_dynamic-update-slice_fusion.5.near_ref, bf16[128,2944]{1,0:T(8,128)(2,1)S(1)} %collective-permute-done.5.far_ref, bf16[2,2880]{1,0:T(2,128)(2,1)S(1)} %bitcast.9, bf16[2,1,720,2880]{3,2,1,0:T(8,128)(2,1)S(1)} %bitcast.5, ...), custom_call_target="tpu_custom_call" | custom-call | tf_op jit(solution)/shard_map/ffn_0/pallas_call | solution.py:100
  33.6 2.1 %collective-permute-done.6 = bf16[128,2944]{1,0:T(8,128)(2,1)S(1)} collective-permute-done((bf16[128,2944]{1,0:T(8,128)(2,1)S(1)}, bf16[128,2944]{1,0:T(8,128)(2,1)S(1)}, u32[]{:S(2)}, u32[]{:S(2)}) %collective-permute-start.6) | collective-permute-done | bytes 753696 | tf_op jit(solution)/shard_map/ppermute | solution.py:165
  35.9 1.6 %collective-permute-start.7 = (bf16[64,2944]{1,0:T(8,128)(2,1)S(1)}, bf16[64,2944]{1,0:T(8,128)(2,1)S(1)}, u32[]{:S(2)}, u32[]{:S(2)}) collective-permute-start(bf16[64,2944]{1,0:T(8,128)(2,1)S(1)} %slice.107), channel_id=1, source_target_pairs={{0,16},{1,3},{2,18},{3,1},{4,20},{5,7},{6,22},{7,5},{8,24},{9,11},... | collective-permute-start | bytes 1130504 | tf_op jit(solution)/shard_map/ppermute | solution.py:168
  37.5 6.1 %collective-permute-done.7 = bf16[64,2944]{1,0:T(8,128)(2,1)S(1)} collective-permute-done((bf16[64,2944]{1,0:T(8,128)(2,1)S(1)}, bf16[64,2944]{1,0:T(8,128)(2,1)S(1)}, u32[]{:S(2)}, u32[]{:S(2)}) %collective-permute-start.7) | collective-permute-done | bytes 376864 | tf_op jit(solution)/shard_map/ppermute | solution.py:168
  43.6 1.6 %collective-permute-start.8 = (bf16[32,2944]{1,0:T(8,128)(2,1)S(1)}, bf16[32,2944]{1,0:T(8,128)(2,1)S(1)}, u32[]{:S(2)}, u32[]{:S(2)}) collective-permute-start(bf16[32,2944]{1,0:T(8,128)(2,1)S(1)} %slice.109), channel_id=1, source_target_pairs={{0,2},{1,17},{2,0},{3,19},{4,6},{5,21},{6,4},{7,23},{8,10},{9,25},... | collective-permute-start | bytes 565256 | tf_op jit(solution)/shard_map/ppermute | solution.py:168
  45.2 4.1 %collective-permute-done.8 = bf16[32,2944]{1,0:T(8,128)(2,1)S(1)} collective-permute-done((bf16[32,2944]{1,0:T(8,128)(2,1)S(1)}, bf16[32,2944]{1,0:T(8,128)(2,1)S(1)}, u32[]{:S(2)}, u32[]{:S(2)}) %collective-permute-start.8) | collective-permute-done | bytes 188448 | tf_op jit(solution)/shard_map/ppermute | solution.py:168
  49.4 1.6 %collective-permute-start.10 = (bf16[8,2944]{1,0:T(8,128)(2,1)S(1)}, bf16[8,2944]{1,0:T(8,128)(2,1)S(1)}, u32[]{:S(2)}, u32[]{:S(2)}) collective-permute-start(bf16[8,2944]{1,0:T(8,128)(2,1)S(1)} %get-tuple-element.31), channel_id=1, source_target_pairs={{0,8},{1,9},{2,10},{3,11},{4,12},{5,13},{6,14},{7,15},{8,0},{9,1},... | collective-permute-start | bytes 141320 | tf_op jit(solution)/shard_map/ppermute | solution.py:171
  51.1 2.3 %collective-permute-start.9 = (bf16[8,2944]{1,0:T(8,128)(2,1)S(1)}, bf16[8,2944]{1,0:T(8,128)(2,1)S(1)}, u32[]{:S(2)}, u32[]{:S(2)}) collective-permute-start(bf16[8,2944]{1,0:T(8,128)(2,1)S(1)} %get-tuple-element.32), channel_id=1, source_target_pairs={{0,12},{1,13},{2,14},{3,15},{4,0},{5,1},{6,2},{7,3},{8,4},{9,5},{1... | collective-permute-start | bytes 141320 | tf_op jit(solution)/shard_map/ppermute | solution.py:171
  53.4 1.9 %collective-permute-done.11.refs_2_ = bf16[8,2944]{1,0:T(8,128)(2,1)S(1)} collective-permute-done((bf16[8,2944]{1,0:T(8,128)(2,1)S(1)}, bf16[8,2944]{1,0:T(8,128)(2,1)S(1)}, u32[]{:S(2)}, u32[]{:S(2)}) %collective-permute-start.11) | collective-permute-done | bytes 47136 | tf_op jit(solution)/shard_map/ppermute | solution.py:171
  56.1 3.5 %collective-permute-start.14 = (bf16[8,2944]{1,0:T(8,128)(2,1)S(1)}, bf16[8,2944]{1,0:T(8,128)(2,1)S(1)}, u32[]{:S(2)}, u32[]{:S(2)}) collective-permute-start(bf16[8,2944]{1,0:T(8,128)(2,1)S(1)} %get-tuple-element.17), channel_id=1, source_target_pairs={{0,12},{1,13},{2,14},{3,15},{4,0},{5,1},{6,2},{7,3},{8,4},{9,5},{1... | collective-permute-start | bytes 141320 | tf_op jit(solution)/shard_map/ppermute | solution.py:159
  61.3 3.2 %collective-permute-done.13 = bf16[8,2944]{1,0:T(8,128)(2,1)S(1)} collective-permute-done((bf16[8,2944]{1,0:T(8,128)(2,1)S(1)}, bf16[8,2944]{1,0:T(8,128)(2,1)S(1)}, u32[]{:S(2)}, u32[]{:S(2)}) %collective-permute-start.13) | collective-permute-done | bytes 47136 | tf_op jit(solution)/shard_map/ppermute | solution.py:159
  65.7 1.6 %collective-permute-start.15 = (bf16[32,2944]{1,0:T(8,128)(2,1)S(1)}, bf16[32,2944]{1,0:T(8,128)(2,1)S(1)}, u32[]{:S(2)}, u32[]{:S(2)}) collective-permute-start(bf16[32,2944]{1,0:T(8,128)(2,1)S(1)} %pad_maximum_fusion.1), channel_id=1, source_target_pairs={{0,2},{1,17},{2,0},{3,19},{4,6},{5,21},{6,4},{7,23},{8,10},{9,25},... | collective-permute-start | bytes 565256 | tf_op jit(solution)/shard_map/ppermute | solution.py:161
  67.3 6.1 %collective-permute-done.15 = bf16[32,2944]{1,0:T(8,128)(2,1)S(1)} collective-permute-done((bf16[32,2944]{1,0:T(8,128)(2,1)S(1)}, bf16[32,2944]{1,0:T(8,128)(2,1)S(1)}, u32[]{:S(2)}, u32[]{:S(2)}) %collective-permute-start.15) | collective-permute-done | bytes 188448 | tf_op jit(solution)/shard_map/ppermute | solution.py:161
  73.3 1.6 %collective-permute-start.16 = (bf16[64,2944]{1,0:T(8,128)(2,1)S(1)}, bf16[64,2944]{1,0:T(8,128)(2,1)S(1)}, u32[]{:S(2)}, u32[]{:S(2)}) collective-permute-start(bf16[64,2944]{1,0:T(8,128)(2,1)S(1)} %get-tuple-element.28), channel_id=1, source_target_pairs={{0,16},{1,3},{2,18},{3,1},{4,20},{5,7},{6,22},{7,5},{8,24},{9,11},... | collective-permute-start | bytes 1130504 | tf_op jit(solution)/shard_map/ppermute | solution.py:162
  74.9 6.1 %collective-permute-done.16 = bf16[64,2944]{1,0:T(8,128)(2,1)S(1)} collective-permute-done((bf16[64,2944]{1,0:T(8,128)(2,1)S(1)}, bf16[64,2944]{1,0:T(8,128)(2,1)S(1)}, u32[]{:S(2)}, u32[]{:S(2)}) %collective-permute-start.16) | collective-permute-done | bytes 376864 | tf_op jit(solution)/shard_map/ppermute | solution.py:162
  81.1 2.2 %collective-permute-done.17.far_ref = bf16[128,2944]{1,0:T(8,128)(2,1)S(1)} collective-permute-done((bf16[128,2944]{1,0:T(8,128)(2,1)S(1)}, bf16[128,2944]{1,0:T(8,128)(2,1)S(1)}, u32[]{:S(2)}, u32[]{:S(2)}) %collective-permute-start.17) | collective-permute-done | bytes 753696 | tf_op jit(solution)/shard_map/ppermute | solution.py:163
  83.4 3.2 %ffn_1.1 = (bf16[128,2944]{1,0:T(8,128)(2,1)S(1)}, bf16[128,2944]{1,0:T(8,128)(2,1)S(1)}) custom-call(bf16[128,2944]{1,0:T(8,128)(2,1)S(1)} %constant_dynamic-update-slice_fusion.16.near_ref, bf16[128,2944]{1,0:T(8,128)(2,1)S(1)} %collective-permute-done.17.far_ref, bf16[2,2880]{1,0:T(2,128)(2,1)S(1)} %bitcast.10, bf16[2,1,720,2880]{3,2,1,0:T(8,128)(2,1)S(1)} %bitcast.6, ...), custom_call_target="tpu_custom_call" | custom-call | tf_op jit(solution)/shard_map/ffn_1/pallas_call | solution.py:100
  86.7 2.1 %collective-permute-done.18 = bf16[128,2944]{1,0:T(8,128)(2,1)S(1)} collective-permute-done((bf16[128,2944]{1,0:T(8,128)(2,1)S(1)}, bf16[128,2944]{1,0:T(8,128)(2,1)S(1)}, u32[]{:S(2)}, u32[]{:S(2)}) %collective-permute-start.18) | collective-permute-done | bytes 753696 | tf_op jit(solution)/shard_map/ppermute | solution.py:165
  89.0 1.6 %collective-permute-start.19 = (bf16[64,2944]{1,0:T(8,128)(2,1)S(1)}, bf16[64,2944]{1,0:T(8,128)(2,1)S(1)}, u32[]{:S(2)}, u32[]{:S(2)}) collective-permute-start(bf16[64,2944]{1,0:T(8,128)(2,1)S(1)} %slice.106), channel_id=1, source_target_pairs={{0,16},{1,3},{2,18},{3,1},{4,20},{5,7},{6,22},{7,5},{8,24},{9,11},... | collective-permute-start | bytes 1130504 | tf_op jit(solution)/shard_map/ppermute | solution.py:168
  90.6 6.1 %collective-permute-done.19 = bf16[64,2944]{1,0:T(8,128)(2,1)S(1)} collective-permute-done((bf16[64,2944]{1,0:T(8,128)(2,1)S(1)}, bf16[64,2944]{1,0:T(8,128)(2,1)S(1)}, u32[]{:S(2)}, u32[]{:S(2)}) %collective-permute-start.19) | collective-permute-done | bytes 376864 | tf_op jit(solution)/shard_map/ppermute | solution.py:168
  96.8 1.6 %collective-permute-start.20 = (bf16[32,2944]{1,0:T(8,128)(2,1)S(1)}, bf16[32,2944]{1,0:T(8,128)(2,1)S(1)}, u32[]{:S(2)}, u32[]{:S(2)}) collective-permute-start(bf16[32,2944]{1,0:T(8,128)(2,1)S(1)} %slice.108), channel_id=1, source_target_pairs={{0,2},{1,17},{2,0},{3,19},{4,6},{5,21},{6,4},{7,23},{8,10},{9,25},... | collective-permute-start | bytes 565256 | tf_op jit(solution)/shard_map/ppermute | solution.py:168
  98.4 4.1 %collective-permute-done.20 = bf16[32,2944]{1,0:T(8,128)(2,1)S(1)} collective-permute-done((bf16[32,2944]{1,0:T(8,128)(2,1)S(1)}, bf16[32,2944]{1,0:T(8,128)(2,1)S(1)}, u32[]{:S(2)}, u32[]{:S(2)}) %collective-permute-start.20) | collective-permute-done | bytes 188448 | tf_op jit(solution)/shard_map/ppermute | solution.py:168
  103.6 2.8 %collective-permute-start.21 = (bf16[8,2944]{1,0:T(8,128)(2,1)S(1)}, bf16[8,2944]{1,0:T(8,128)(2,1)S(1)}, u32[]{:S(2)}, u32[]{:S(2)}) collective-permute-start(bf16[8,2944]{1,0:T(8,128)(2,1)S(1)} %get-tuple-element.27), channel_id=1, source_target_pairs={{0,12},{1,13},{2,14},{3,15},{4,0},{5,1},{6,2},{7,3},{8,4},{9,5},{1... | collective-permute-start | bytes 141320 | tf_op jit(solution)/shard_map/ppermute | solution.py:171
  106.5 2.0 %collective-permute-done.23.refs_2_ = bf16[8,2944]{1,0:T(8,128)(2,1)S(1)} collective-permute-done((bf16[8,2944]{1,0:T(8,128)(2,1)S(1)}, bf16[8,2944]{1,0:T(8,128)(2,1)S(1)}, u32[]{:S(2)}, u32[]{:S(2)}) %collective-permute-start.23) | collective-permute-done | bytes 47136 | tf_op jit(solution)/shard_map/ppermute | solution.py:171
  (73 shorter events, 12.7 us)
Async XLA Ops:
  0.0 30.1 %slice-start = ((s8[8478720]{0:T(1024)(128)(4,1)}), s8[4194304]{0:T(1024)(128)(4,1)S(1)}, s32[]{:S(2)}) async-start(s8[8478720]{0:T(1024)(128)(4,1)} %bitcast.3), calls=%async_computation | async-start | bytes 8388608
  0.0 30.1 %slice-start.3 = ((s8[8478720]{0:T(1024)(128)(4,1)}), s8[4194304]{0:T(1024)(128)(4,1)S(1)}, s32[]{:S(2)}) async-start(s8[8478720]{0:T(1024)(128)(4,1)} %bitcast.7), calls=%async_computation.3 | async-start | bytes 8388608
  3.2 26.9 %slice-start.1 = ((s8[8478720]{0:T(1024)(128)(4,1)}), s8[4194304]{0:T(1024)(128)(4,1)S(1)}, s32[]{:S(2)}) async-start(s8[8478720]{0:T(1024)(128)(4,1)} %bitcast.3), calls=%async_computation.1 | async-start | bytes 8388608
  3.2 26.9 %slice-start.2 = ((s8[8478720]{0:T(1024)(128)(4,1)}), s8[90112]{0:T(1024)(128)(4,1)S(1)}, s32[]{:S(2)}) async-start(s8[8478720]{0:T(1024)(128)(4,1)} %bitcast.3), calls=%async_computation.2 | async-start | bytes 180224
  3.2 26.9 %slice-start.4 = ((s8[8478720]{0:T(1024)(128)(4,1)}), s8[4194304]{0:T(1024)(128)(4,1)S(1)}, s32[]{:S(2)}) async-start(s8[8478720]{0:T(1024)(128)(4,1)} %bitcast.7), calls=%async_computation.4 | async-start | bytes 8388608
  3.2 26.9 %slice-start.5 = ((s8[8478720]{0:T(1024)(128)(4,1)}), s8[90112]{0:T(1024)(128)(4,1)S(1)}, s32[]{:S(2)}) async-start(s8[8478720]{0:T(1024)(128)(4,1)} %bitcast.7), calls=%async_computation.5 | async-start | bytes 180224
  3.4 26.8 %copy-start = (bf16[2,1,2880]{2,0,1:T(2,128)(2,1)S(1)}, bf16[2,1,2880]{2,0,1:T(2,128)(2,1)}, u32[]{:S(2)}) copy-start(bf16[2,1,2880]{2,0,1:T(2,128)(2,1)} %param.11) | copy-start | bytes 34564
  3.4 7.1 %collective-permute-start.2 = (bf16[8,2944]{1,0:T(8,128)(2,1)S(1)}, bf16[8,2944]{1,0:T(8,128)(2,1)S(1)}, u32[]{:S(2)}, u32[]{:S(2)}) collective-permute-start(bf16[8,2944]{1,0:T(8,128)(2,1)S(1)} %get-tuple-element.13), channel_id=1, source_target_pairs={{0,12},{1,13},{2,14},{3,15},{4,0},{5,1},{6,2},{7,3},{8,4},{9,5},{1... | collective-permute-start | bytes 141320 | tf_op jit(solution)/shard_map/ppermute | solution.py:159
  8.5 5.0 %collective-permute-start.1 = (bf16[8,2944]{1,0:T(8,128)(2,1)S(1)}, bf16[8,2944]{1,0:T(8,128)(2,1)S(1)}, u32[]{:S(2)}, u32[]{:S(2)}) collective-permute-start(bf16[8,2944]{1,0:T(8,128)(2,1)S(1)} %get-tuple-element.13), channel_id=1, source_target_pairs={{0,8},{1,9},{2,10},{3,11},{4,12},{5,13},{6,14},{7,15},{8,0},{9,1},... | collective-permute-start | bytes 141320 | tf_op jit(solution)/shard_map/ppermute | solution.py:159
  8.5 5.9 %collective-permute-start = (bf16[8,2944]{1,0:T(8,128)(2,1)S(1)}, bf16[8,2944]{1,0:T(8,128)(2,1)S(1)}, u32[]{:S(2)}, u32[]{:S(2)}) collective-permute-start(bf16[8,2944]{1,0:T(8,128)(2,1)S(1)} %get-tuple-element.13), channel_id=1, source_target_pairs={{0,4},{1,5},{2,6},{3,7},{4,8},{5,9},{6,10},{7,11},{8,12},{9,13},{1... | collective-permute-start | bytes 141320 | tf_op jit(solution)/shard_map/ppermute | solution.py:159
  14.4 5.7 %collective-permute-start.3 = (bf16[32,2944]{1,0:T(8,128)(2,1)S(1)}, bf16[32,2944]{1,0:T(8,128)(2,1)S(1)}, u32[]{:S(2)}, u32[]{:S(2)}) collective-permute-start(bf16[32,2944]{1,0:T(8,128)(2,1)S(1)} %pad_maximum_fusion), channel_id=1, source_target_pairs={{0,2},{1,17},{2,0},{3,19},{4,6},{5,21},{6,4},{7,23},{8,10},{9,25},... | collective-permute-start | bytes 565256 | tf_op jit(solution)/shard_map/ppermute | solution.py:161
  20.1 7.7 %collective-permute-start.4 = (bf16[64,2944]{1,0:T(8,128)(2,1)S(1)}, bf16[64,2944]{1,0:T(8,128)(2,1)S(1)}, u32[]{:S(2)}, u32[]{:S(2)}) collective-permute-start(bf16[64,2944]{1,0:T(8,128)(2,1)S(1)} %get-tuple-element.33), channel_id=1, source_target_pairs={{0,16},{1,3},{2,18},{3,1},{4,20},{5,7},{6,22},{7,5},{8,24},{9,11},... | collective-permute-start | bytes 1130504 | tf_op jit(solution)/shard_map/ppermute | solution.py:162
  27.8 2.3 %collective-permute-start.5 = (bf16[128,2944]{1,0:T(8,128)(2,1)S(1)}, bf16[128,2944]{1,0:T(8,128)(2,1)S(1)}, u32[]{:S(2)}, u32[]{:S(2)}) collective-permute-start(bf16[128,2944]{1,0:T(8,128)(2,1)S(1)} %constant_dynamic-update-slice_fusion.5.near_ref), channel_id=1, source_target_pairs={{0,1},{1,0},{2,3},{3,2},{4,5},{5,4},{6,7},{7,6},{8,9},{9,8},{10,11... | collective-permute-start | bytes 2261000 | tf_op jit(solution)/shard_map/ppermute | solution.py:163
  33.4 2.3 %collective-permute-start.6 = (bf16[128,2944]{1,0:T(8,128)(2,1)S(1)}, bf16[128,2944]{1,0:T(8,128)(2,1)S(1)}, u32[]{:S(2)}, u32[]{:S(2)}) collective-permute-start(bf16[128,2944]{1,0:T(8,128)(2,1)S(1)} %get-tuple-element.15), channel_id=1, source_target_pairs={{0,1},{1,0},{2,3},{3,2},{4,5},{5,4},{6,7},{7,6},{8,9},{9,8},{10,11... | collective-permute-start | bytes 2261000 | tf_op jit(solution)/shard_map/ppermute | solution.py:165
  35.9 20.0 %copy-start.2 = (bf16[8,2880]{1,0:T(8,128)(2,1)S(1)}, bf16[8,2880]{1,0:T(8,128)(2,1)}, u32[]{:S(2)}) copy-start(bf16[8,2880]{1,0:T(8,128)(2,1)} %refs_3_.1) | copy-start | bytes 138244
  35.9 7.7 %collective-permute-start.7 = (bf16[64,2944]{1,0:T(8,128)(2,1)S(1)}, bf16[64,2944]{1,0:T(8,128)(2,1)S(1)}, u32[]{:S(2)}, u32[]{:S(2)}) collective-permute-start(bf16[64,2944]{1,0:T(8,128)(2,1)S(1)} %slice.107), channel_id=1, source_target_pairs={{0,16},{1,3},{2,18},{3,1},{4,20},{5,7},{6,22},{7,5},{8,24},{9,11},... | collective-permute-start | bytes 1130504 | tf_op jit(solution)/shard_map/ppermute | solution.py:168
  43.6 5.6 %collective-permute-start.8 = (bf16[32,2944]{1,0:T(8,128)(2,1)S(1)}, bf16[32,2944]{1,0:T(8,128)(2,1)S(1)}, u32[]{:S(2)}, u32[]{:S(2)}) collective-permute-start(bf16[32,2944]{1,0:T(8,128)(2,1)S(1)} %slice.109), channel_id=1, source_target_pairs={{0,2},{1,17},{2,0},{3,19},{4,6},{5,21},{6,4},{7,23},{8,10},{9,25},... | collective-permute-start | bytes 565256 | tf_op jit(solution)/shard_map/ppermute | solution.py:168
  49.4 5.9 %collective-permute-start.11 = (bf16[8,2944]{1,0:T(8,128)(2,1)S(1)}, bf16[8,2944]{1,0:T(8,128)(2,1)S(1)}, u32[]{:S(2)}, u32[]{:S(2)}) collective-permute-start(bf16[8,2944]{1,0:T(8,128)(2,1)S(1)} %get-tuple-element.30), channel_id=1, source_target_pairs={{0,4},{1,5},{2,6},{3,7},{4,8},{5,9},{6,10},{7,11},{8,12},{9,13},{1... | collective-permute-start | bytes 141320 | tf_op jit(solution)/shard_map/ppermute | solution.py:171
  49.4 5.9 %collective-permute-start.10 = (bf16[8,2944]{1,0:T(8,128)(2,1)S(1)}, bf16[8,2944]{1,0:T(8,128)(2,1)S(1)}, u32[]{:S(2)}, u32[]{:S(2)}) collective-permute-start(bf16[8,2944]{1,0:T(8,128)(2,1)S(1)} %get-tuple-element.31), channel_id=1, source_target_pairs={{0,8},{1,9},{2,10},{3,11},{4,12},{5,13},{6,14},{7,15},{8,0},{9,1},... | collective-permute-start | bytes 141320 | tf_op jit(solution)/shard_map/ppermute | solution.py:171
  51.1 4.8 %collective-permute-start.9 = (bf16[8,2944]{1,0:T(8,128)(2,1)S(1)}, bf16[8,2944]{1,0:T(8,128)(2,1)S(1)}, u32[]{:S(2)}, u32[]{:S(2)}) collective-permute-start(bf16[8,2944]{1,0:T(8,128)(2,1)S(1)} %get-tuple-element.32), channel_id=1, source_target_pairs={{0,12},{1,13},{2,14},{3,15},{4,0},{5,1},{6,2},{7,3},{8,4},{9,5},{1... | collective-permute-start | bytes 141320 | tf_op jit(solution)/shard_map/ppermute | solution.py:171
  56.1 5.2 %collective-permute-start.14 = (bf16[8,2944]{1,0:T(8,128)(2,1)S(1)}, bf16[8,2944]{1,0:T(8,128)(2,1)S(1)}, u32[]{:S(2)}, u32[]{:S(2)}) collective-permute-start(bf16[8,2944]{1,0:T(8,128)(2,1)S(1)} %get-tuple-element.17), channel_id=1, source_target_pairs={{0,12},{1,13},{2,14},{3,15},{4,0},{5,1},{6,2},{7,3},{8,4},{9,5},{1... | collective-permute-start | bytes 141320 | tf_op jit(solution)/shard_map/ppermute | solution.py:159
  59.6 5.0 %collective-permute-start.13 = (bf16[8,2944]{1,0:T(8,128)(2,1)S(1)}, bf16[8,2944]{1,0:T(8,128)(2,1)S(1)}, u32[]{:S(2)}, u32[]{:S(2)}) collective-permute-start(bf16[8,2944]{1,0:T(8,128)(2,1)S(1)} %get-tuple-element.17), channel_id=1, source_target_pairs={{0,8},{1,9},{2,10},{3,11},{4,12},{5,13},{6,14},{7,15},{8,0},{9,1},... | collective-permute-start | bytes 141320 | tf_op jit(solution)/shard_map/ppermute | solution.py:159
  59.8 5.9 %collective-permute-start.12 = (bf16[8,2944]{1,0:T(8,128)(2,1)S(1)}, bf16[8,2944]{1,0:T(8,128)(2,1)S(1)}, u32[]{:S(2)}, u32[]{:S(2)}) collective-permute-start(bf16[8,2944]{1,0:T(8,128)(2,1)S(1)} %get-tuple-element.17), channel_id=1, source_target_pairs={{0,4},{1,5},{2,6},{3,7},{4,8},{5,9},{6,10},{7,11},{8,12},{9,13},{1... | collective-permute-start | bytes 141320 | tf_op jit(solution)/shard_map/ppermute | solution.py:159
  65.7 7.7 %collective-permute-start.15 = (bf16[32,2944]{1,0:T(8,128)(2,1)S(1)}, bf16[32,2944]{1,0:T(8,128)(2,1)S(1)}, u32[]{:S(2)}, u32[]{:S(2)}) collective-permute-start(bf16[32,2944]{1,0:T(8,128)(2,1)S(1)} %pad_maximum_fusion.1), channel_id=1, source_target_pairs={{0,2},{1,17},{2,0},{3,19},{4,6},{5,21},{6,4},{7,23},{8,10},{9,25},... | collective-permute-start | bytes 565256 | tf_op jit(solution)/shard_map/ppermute | solution.py:161
  73.3 7.7 %collective-permute-start.16 = (bf16[64,2944]{1,0:T(8,128)(2,1)S(1)}, bf16[64,2944]{1,0:T(8,128)(2,1)S(1)}, u32[]{:S(2)}, u32[]{:S(2)}) collective-permute-start(bf16[64,2944]{1,0:T(8,128)(2,1)S(1)} %get-tuple-element.28), channel_id=1, source_target_pairs={{0,16},{1,3},{2,18},{3,1},{4,20},{5,7},{6,22},{7,5},{8,24},{9,11},... | collective-permute-start | bytes 1130504 | tf_op jit(solution)/shard_map/ppermute | solution.py:162
  81.0 2.3 %collective-permute-start.17 = (bf16[128,2944]{1,0:T(8,128)(2,1)S(1)}, bf16[128,2944]{1,0:T(8,128)(2,1)S(1)}, u32[]{:S(2)}, u32[]{:S(2)}) collective-permute-start(bf16[128,2944]{1,0:T(8,128)(2,1)S(1)} %constant_dynamic-update-slice_fusion.16.near_ref), channel_id=1, source_target_pairs={{0,1},{1,0},{2,3},{3,2},{4,5},{5,4},{6,7},{7,6},{8,9},{9,8},{10,11... | collective-permute-start | bytes 2261000 | tf_op jit(solution)/shard_map/ppermute | solution.py:163
  86.5 2.3 %collective-permute-start.18 = (bf16[128,2944]{1,0:T(8,128)(2,1)S(1)}, bf16[128,2944]{1,0:T(8,128)(2,1)S(1)}, u32[]{:S(2)}, u32[]{:S(2)}) collective-permute-start(bf16[128,2944]{1,0:T(8,128)(2,1)S(1)} %get-tuple-element.19), channel_id=1, source_target_pairs={{0,1},{1,0},{2,3},{3,2},{4,5},{5,4},{6,7},{7,6},{8,9},{9,8},{10,11... | collective-permute-start | bytes 2261000 | tf_op jit(solution)/shard_map/ppermute | solution.py:165
  89.0 7.7 %collective-permute-start.19 = (bf16[64,2944]{1,0:T(8,128)(2,1)S(1)}, bf16[64,2944]{1,0:T(8,128)(2,1)S(1)}, u32[]{:S(2)}, u32[]{:S(2)}) collective-permute-start(bf16[64,2944]{1,0:T(8,128)(2,1)S(1)} %slice.106), channel_id=1, source_target_pairs={{0,16},{1,3},{2,18},{3,1},{4,20},{5,7},{6,22},{7,5},{8,24},{9,11},... | collective-permute-start | bytes 1130504 | tf_op jit(solution)/shard_map/ppermute | solution.py:168
  96.8 5.6 %collective-permute-start.20 = (bf16[32,2944]{1,0:T(8,128)(2,1)S(1)}, bf16[32,2944]{1,0:T(8,128)(2,1)S(1)}, u32[]{:S(2)}, u32[]{:S(2)}) collective-permute-start(bf16[32,2944]{1,0:T(8,128)(2,1)S(1)} %slice.108), channel_id=1, source_target_pairs={{0,2},{1,17},{2,0},{3,19},{4,6},{5,21},{6,4},{7,23},{8,10},{9,25},... | collective-permute-start | bytes 565256 | tf_op jit(solution)/shard_map/ppermute | solution.py:168
  102.5 5.9 %collective-permute-start.23 = (bf16[8,2944]{1,0:T(8,128)(2,1)S(1)}, bf16[8,2944]{1,0:T(8,128)(2,1)S(1)}, u32[]{:S(2)}, u32[]{:S(2)}) collective-permute-start(bf16[8,2944]{1,0:T(8,128)(2,1)S(1)} %get-tuple-element.25), channel_id=1, source_target_pairs={{0,4},{1,5},{2,6},{3,7},{4,8},{5,9},{6,10},{7,11},{8,12},{9,13},{1... | collective-permute-start | bytes 141320 | tf_op jit(solution)/shard_map/ppermute | solution.py:171
  102.6 5.9 %collective-permute-start.22 = (bf16[8,2944]{1,0:T(8,128)(2,1)S(1)}, bf16[8,2944]{1,0:T(8,128)(2,1)S(1)}, u32[]{:S(2)}, u32[]{:S(2)}) collective-permute-start(bf16[8,2944]{1,0:T(8,128)(2,1)S(1)} %get-tuple-element.26), channel_id=1, source_target_pairs={{0,8},{1,9},{2,10},{3,11},{4,12},{5,13},{6,14},{7,15},{8,0},{9,1},... | collective-permute-start | bytes 141320 | tf_op jit(solution)/shard_map/ppermute | solution.py:171
  103.6 5.4 %collective-permute-start.21 = (bf16[8,2944]{1,0:T(8,128)(2,1)S(1)}, bf16[8,2944]{1,0:T(8,128)(2,1)S(1)}, u32[]{:S(2)}, u32[]{:S(2)}) collective-permute-start(bf16[8,2944]{1,0:T(8,128)(2,1)S(1)} %get-tuple-element.27), channel_id=1, source_target_pairs={{0,12},{1,13},{2,14},{3,15},{4,0},{5,1},{6,2},{7,3},{8,4},{9,5},{1... | collective-permute-start | bytes 141320 | tf_op jit(solution)/shard_map/ppermute | solution.py:171
  (3 other events, 3.2 us)

commit v3 on v2

--- a/solution.py
+++ b/solution.py
@@ -64,48 +64,46 @@
         write_payload(updated.astype(jnp.float32), tails_ref[layer + 1], model, tail, more[0])
 
 
-def ffn_kernel(layer, near_ref, far_ref, router_ref, up_ref, down_ref, near_out, far_out, rows_ref, hidden_ref):
-    half, width = near_ref.shape
+def ffn_kernel(layer, count, *refs):
+    pieces, (router_ref, up_ref, down_ref), outs, (rows_ref, hidden_ref) = refs[:count], refs[count : count + 3], refs[count + 3 : -2], refs[-2:]
+    size, width = pieces[0].shape
     model, units = router_ref.shape[-1], up_ref.shape[2]
-    rows_ref[:half, :] = near_ref[...]
-    rows_ref[half:, :] = far_ref[...]
+    for index, piece in enumerate(pieces):
+        rows_ref[index * size : (index + 1) * size, :] = piece[...]
     slot, block = lax.axis_index("expert"), lax.axis_index("dp")
     tail = model // LANES * LANES
-    lane = lax.broadcasted_iota(jnp.int32, (2 * half, width - tail), 1)
+    lane = lax.broadcasted_iota(jnp.int32, (count * size, width - tail), 1)
     here = lane == (model - tail) + slot
     member = jnp.sum(jnp.where(here, rows_ref[:, tail:].astype(jnp.float32), 0.0), axis=1, keepdims=True)
     by_rows = (((1,), (1,)), ((), ()))
     logits = lax.dot_general(rows_ref[:, :model], router_ref[...], by_rows, preferred_element_type=jnp.float32)
     gate = jax.nn.sigmoid(logits[:, layer : layer + 1]).astype(jnp.bfloat16).astype(jnp.float32) * member
     for start in range(0, units, 256):
-        size = min(256, units - start)
-        raw = lax.dot_general(
-            rows_ref[:, :model], up_ref[layer, 0, start : start + size, :], by_rows, preferred_element_type=jnp.float32
-        )
-        hidden_ref[:, start : start + size] = jax.nn.silu(raw).astype(jnp.bfloat16)
+        stop = min(start + 256, units)
+        raw = lax.dot_general(rows_ref[:, :model], up_ref[layer, 0, start:stop, :], by_rows, preferred_element_type=jnp.float32)
+        hidden_ref[:, start:stop] = jax.nn.silu(raw).astype(jnp.bfloat16)
     for start in range(0, model, 768):
-        size = min(768, model - start)
-        part = jnp.dot(hidden_ref[...], down_ref[layer, 0, :, start : start + size], preferred_element_type=jnp.float32)
+        stop = min(start + 768, model)
+        part = jnp.dot(hidden_ref[...], down_ref[layer, 0, :, start:stop], preferred_element_type=jnp.float32)
         weighted = (part.astype(jnp.bfloat16).astype(jnp.float32) * gate).astype(jnp.bfloat16)
-        near_out[:, start : start + size] = weighted[:half]
-        far_out[:, start : start + size] = weighted[half:]
+        for index, out in enumerate(outs):
+            out[:, start:stop] = weighted[index * size : (index + 1) * size]
     sent = jnp.where(here & (block == 0), gate, 0.0)[:, model - tail :].astype(jnp.bfloat16)
-    near_out[:, model:] = sent[:half]
-    far_out[:, model:] = sent[half:]
-
-
-def expert_ffn(layer, near, far, router, up, down):
-    half, width = near.shape
-    units = up.shape[2]
+    for index, out in enumerate(outs):
+        out[:, model:] = sent[index * size : (index + 1) * size]
+
+
+def expert_ffn(layer, pieces, router, up, down):
+    count, (size, width), units = len(pieces), pieces[0].shape, up.shape[2]
     return pl.pallas_call(
-        functools.partial(ffn_kernel, layer),
-        out_shape=[jax.ShapeDtypeStruct((half, width), jnp.bfloat16)] * 2,
-        in_specs=[VMEM] * 5,
-        out_specs=[VMEM] * 2,
-        scratch_shapes=[pltpu.VMEM((2 * half, width), jnp.bfloat16), pltpu.VMEM((2 * half, units), jnp.bfloat16)],
+        functools.partial(ffn_kernel, layer, count),
+        out_shape=[jax.ShapeDtypeStruct((size, width), jnp.bfloat16)] * count,
+        in_specs=[VMEM] * (count + 3),
+        out_specs=[VMEM] * count,
+        scratch_shapes=[pltpu.VMEM((count * size, width), jnp.bfloat16), pltpu.VMEM((count * size, units), jnp.bfloat16)],
         compiler_params=pltpu.CompilerParams(vmem_limit_bytes=16 * 1024 * 1024),
         name=f"ffn_{layer}",
-    )(near, far, router, up, down)
+    )(*pieces, router, up, down)
 
 
 def dense_moves(groups, columns):
@@ -128,7 +126,7 @@
         return pairs(move)
 
     def shift(amount):
-        return pairs(lambda group, far, side, core: (group, (far + amount) % lengths, side, core))
+        return pairs(lambda group, far, side, core: (group, far ^ amount, side, core))
 
     return lengths, shift, axis_swap(0), axis_swap(1), pairs(lambda group, far, side, core: (group, far, side, 1 - core))
 
@@ -155,20 +153,25 @@
         name="first",
     )(tokens, jnp.swapaxes(routes, 1, 2), placement)
 
+    def move(value, pairs):
+        return lax.ppermute(value, axes, pairs)
+
     for layer in range(layers):
-        line = [own] + [lax.ppermute(own, axes, shift(step)) for step in range(1, lengths)]
-        rows = jnp.concatenate(line, axis=0)
-        rows = jnp.concatenate([rows, lax.ppermute(rows, axes, first_swap)], axis=0)
-        near = jnp.concatenate([rows, lax.ppermute(rows, axes, second_swap)], axis=0)
-        far = lax.ppermute(near, axes, core_swap)
-        near_out, far_out = expert_ffn(layer, near, far, router, up_rows, down_weight)
-        total = near_out.astype(jnp.float32) + lax.ppermute(far_out, axes, core_swap).astype(jnp.float32)
-        for swap in (second_swap, first_swap):
-            half = total.shape[0] // 2
-            moved = lax.ppermute(total[half:].astype(jnp.bfloat16), axes, swap)
-            total = total[:half] + moved.astype(jnp.float32)
-        pieces = total.reshape(lengths, tok_rows, width)
-        arrived = [lax.ppermute(pieces[step].astype(jnp.bfloat16), axes, shift(lengths - step)) for step in range(1, lengths)]
+        here = jnp.concatenate([own] + [move(own, shift(step)) for step in range(1, lengths)], axis=0)
+        first = move(here, first_swap)
+        second = move(here, second_swap)
+        across = move(first, second_swap)
+        near = [here, second, first, across]
+        outs = expert_ffn(layer, near + [move(piece, core_swap) for piece in near], router, up_rows, down_weight)
+        wide = [value.astype(jnp.float32) for value in outs[:4]]
+        here, second, first, across = [
+            mine + move(theirs, core_swap).astype(jnp.float32) for mine, theirs in zip(wide, outs[4:])
+        ]
+        first = first + move(across.astype(jnp.bfloat16), second_swap).astype(jnp.float32)
+        here = here + move(second.astype(jnp.bfloat16), second_swap).astype(jnp.float32)
+        here = here + move(first.astype(jnp.bfloat16), first_swap).astype(jnp.float32)
+        pieces = here.reshape(lengths, tok_rows, width)
+        arrived = [move(pieces[step].astype(jnp.bfloat16), shift(step)) for step in range(1, lengths)]
         last = layer + 1 == layers
         outs = pl.pallas_call(
             functools.partial(update_kernel, model, tail, layer, last),
@@ -269,7 +272,8 @@
     groups, columns = lax.axis_size("dp"), lax.axis_size("expert")
     tok_rows, top_k = tokens.shape[0], routes.shape[2]
     capacity = 2 * tok_rows * top_k // columns
-    dense = groups == 2 and columns % 4 == 0 and tok_rows <= 2 * capacity
+    lengths = columns // 4
+    dense = groups == 2 and columns == 4 * lengths and lengths & (lengths - 1) == 0 and tok_rows <= 2 * capacity
     plan = dense_device if dense else dispatch_device
     return plan(tokens, routes, placement, up_weight, down_weight, router_weight)
 

time: 110 us -> 96.3 us (0.88)
  waiting for transfers between devices: 66.5 us -> 50.8 us
  starting transfers between devices: 31.3 us -> 34.8 us
  local copies, waits for them, and re-layouts: 3.59 us -> 2.28 us
    ppermute x24 -> x40, waiting for transfers between devices: 66.5 us -> 50.8 us  [move(): return lax.ppermute(value, axes, pairs)]
    ppermute x24 -> x40, starting transfers between devices: 31.3 us -> 34.8 us  [move(): return lax.ppermute(value, axes, pairs)]
    unnamed x30 -> x20, local copies, waits for them, and re-layouts: 3.29 us -> 2.22 us
  transfers between devices with their start and end apart: 24 -> 40, of which waited for: 22 -> 24; matrix products, arithmetic and copies ran while one was open for 0% -> 0% of each run, Pallas kernels for 0% -> 0%
where the time goes in v3:
time: 96.3 us; the launch traced here: 96.1 us
  waiting for transfers between devices  50.8 us (53%)
  starting transfers between devices  34.8 us (36%)
  Pallas kernels  7.63 us (8%)
  local copies, waits for them, and re-layouts  2.28 us (2%)
    ppermute x40, waiting for transfers between devices, move(): return lax.ppermute(value, axes, pairs)  50.8 us
    ppermute x40, starting transfers between devices, move(): return lax.ppermute(value, axes, pairs)  34.8 us
    pallas_call x2, Pallas kernels, expert_ffn(): pl.pallas_call(functools.partial(ffn_kernel, layer, count), out_shape=[ja...  6.39 us
    unnamed x20, local copies, waits for them, and re-layouts  2.22 us
  transfers between devices with their start and end apart: 40, of which 24 were waited for; matrix products, arithmetic and copies ran while one was open for 0% of the time, Pallas kernels for 0%

profile of v3, /device:TPU:0, one launch (start us, length us, event | category | flops | bytes accessed | tf_op | source)
XLA Modules:
  0.0 96.1 jit_solution(18113976912011283298)
XLA Ops:
  2.4 5.1 %collective-permute-start.2 = (bf16[8,2944]{1,0:T(8,128)(2,1)S(1)}, bf16[8,2944]{1,0:T(8,128)(2,1)S(1)}, u32[]{:S(2)}, u32[]{:S(2)}) collective-permute-start(bf16[8,2944]{1,0:T(8,128)(2,1)S(1)} %get-tuple-element.25), channel_id=1, source_target_pairs={{0,12},{1,13},{2,14},{3,15},{4,8},{5,9},{6,10},{7,11},{8,4},{9,5},... | collective-permute-start | bytes 141320 | tf_op jit(solution)/shard_map/ppermute | solution.py:157
  8.1 3.4 %collective-permute-done = bf16[8,2944]{1,0:T(8,128)(2,1)S(1)} collective-permute-done((bf16[8,2944]{1,0:T(8,128)(2,1)S(1)}, bf16[8,2944]{1,0:T(8,128)(2,1)S(1)}, u32[]{:S(2)}, u32[]{:S(2)}) %collective-permute-start) | collective-permute-done | bytes 47136 | tf_op jit(solution)/shard_map/ppermute | solution.py:157
  12.4 1.6 %collective-permute-start.4 = (bf16[32,2944]{1,0:T(8,128)(2,1)S(1)}, bf16[32,2944]{1,0:T(8,128)(2,1)S(1)}, u32[]{:S(2)}, u32[]{:S(2)}) collective-permute-start(bf16[32,2944]{1,0:T(8,128)(2,1)S(1)} %constant_dynamic-update-slice_fusion.refs_0_), channel_id=1, source_target_pairs={{0,2},{1,17},{2,0},{3,19},{4,6},{5,21},{6,4},{7,23},{8,10},{9,25},... | collective-permute-start | bytes 565256 | tf_op jit(solution)/shard_map/ppermute | solution.py:157
  14.0 1.5 %collective-permute-start.3 = (bf16[32,2944]{1,0:T(8,128)(2,1)S(1)}, bf16[32,2944]{1,0:T(8,128)(2,1)S(1)}, u32[]{:S(2)}, u32[]{:S(2)}) collective-permute-start(bf16[32,2944]{1,0:T(8,128)(2,1)S(1)} %constant_dynamic-update-slice_fusion.refs_0_), channel_id=1, source_target_pairs={{0,16},{1,3},{2,18},{3,1},{4,20},{5,7},{6,22},{7,5},{8,24},{9,11},... | collective-permute-start | bytes 565256 | tf_op jit(solution)/shard_map/ppermute | solution.py:157
  15.5 4.1 %collective-permute-done.4.refs_2_ = bf16[32,2944]{1,0:T(8,128)(2,1)S(1)} collective-permute-done((bf16[32,2944]{1,0:T(8,128)(2,1)S(1)}, bf16[32,2944]{1,0:T(8,128)(2,1)S(1)}, u32[]{:S(2)}, u32[]{:S(2)}) %collective-permute-start.4) | collective-permute-done | bytes 188448 | tf_op jit(solution)/shard_map/ppermute | solution.py:157
  20.3 5.0 %collective-permute-done.5.refs_3_ = bf16[32,2944]{1,0:T(8,128)(2,1)S(1)} collective-permute-done((bf16[32,2944]{1,0:T(8,128)(2,1)S(1)}, bf16[32,2944]{1,0:T(8,128)(2,1)S(1)}, u32[]{:S(2)}, u32[]{:S(2)}) %collective-permute-start.5) | collective-permute-done | bytes 188448 | tf_op jit(solution)/shard_map/ppermute | solution.py:157
  25.2 1.4 %collective-permute-done.9.refs_7_ = bf16[32,2944]{1,0:T(8,128)(2,1)S(1)} collective-permute-done((bf16[32,2944]{1,0:T(8,128)(2,1)S(1)}, bf16[32,2944]{1,0:T(8,128)(2,1)S(1)}, u32[]{:S(2)}, u32[]{:S(2)}) %collective-permute-start.9) | collective-permute-done | bytes 188448 | tf_op jit(solution)/shard_map/ppermute | solution.py:157
  26.7 3.2 %ffn_0.1 = (bf16[32,2944]{1,0:T(8,128)(2,1)S(1)}, bf16[32,2944]{1,0:T(8,128)(2,1)S(1)}, bf16[32,2944]{1,0:T(8,128)(2,1)S(1)}, bf16[32,2944]{1,0:T(8,128)(2,1)S(1...) custom-call(bf16[32,2944]{1,0:T(8,128)(2,1)S(1)} %constant_dynamic-u, ...), custom_call_target="tpu_custom_call" | custom-call | tf_op jit(solution)/shard_map/ffn_0/pallas_call | solution.py:98
  32.0 1.7 %collective-permute-start.12 = (bf16[32,2944]{1,0:T(8,128)(2,1)S(1)}, bf16[32,2944]{1,0:T(8,128)(2,1)S(1)}, u32[]{:S(2)}, u32[]{:S(2)}) collective-permute-start(bf16[32,2944]{1,0:T(8,128)(2,1)S(1)} %add_convert_fusion.5), channel_id=1, source_target_pairs={{0,16},{1,3},{2,18},{3,1},{4,20},{5,7},{6,22},{7,5},{8,24},{9,11},... | collective-permute-start | bytes 565256 | tf_op jit(solution)/shard_map/ppermute | solution.py:157
  33.6 3.4 %collective-permute-done.15 = bf16[32,2944]{1,0:T(8,128)(2,1)S(1)} collective-permute-done((bf16[32,2944]{1,0:T(8,128)(2,1)S(1)}, bf16[32,2944]{1,0:T(8,128)(2,1)S(1)}, u32[]{:S(2)}, u32[]{:S(2)}) %collective-permute-start.15) | collective-permute-done | bytes 188448 | tf_op jit(solution)/shard_map/ppermute | solution.py:157
  37.2 1.6 %collective-permute-start.16 = (bf16[32,2944]{1,0:T(8,128)(2,1)S(1)}, bf16[32,2944]{1,0:T(8,128)(2,1)S(1)}, u32[]{:S(2)}, u32[]{:S(2)}) collective-permute-start(bf16[32,2944]{1,0:T(8,128)(2,1)S(1)} %add_convert_fusion.3), channel_id=1, source_target_pairs={{0,2},{1,17},{2,0},{3,19},{4,6},{5,21},{6,4},{7,23},{8,10},{9,25},... | collective-permute-start | bytes 565256 | tf_op jit(solution)/shard_map/ppermute | solution.py:157
  39.1 3.7 %collective-permute-done.16 = bf16[32,2944]{1,0:T(8,128)(2,1)S(1)} collective-permute-done((bf16[32,2944]{1,0:T(8,128)(2,1)S(1)}, bf16[32,2944]{1,0:T(8,128)(2,1)S(1)}, u32[]{:S(2)}, u32[]{:S(2)}) %collective-permute-start.16) | collective-permute-done | bytes 188448 | tf_op jit(solution)/shard_map/ppermute | solution.py:157
  42.9 2.2 %collective-permute-start.19 = (bf16[8,2944]{1,0:T(8,128)(2,1)S(1)}, bf16[8,2944]{1,0:T(8,128)(2,1)S(1)}, u32[]{:S(2)}, u32[]{:S(2)}) collective-permute-start(bf16[8,2944]{1,0:T(8,128)(2,1)S(1)} %get-tuple-element.52), channel_id=1, source_target_pairs={{0,12},{1,13},{2,14},{3,15},{4,8},{5,9},{6,10},{7,11},{8,4},{9,5},... | collective-permute-start | bytes 141320 | tf_op jit(solution)/shard_map/ppermute | solution.py:157
  45.3 2.0 %collective-permute-start.17 = (bf16[8,2944]{1,0:T(8,128)(2,1)S(1)}, bf16[8,2944]{1,0:T(8,128)(2,1)S(1)}, u32[]{:S(2)}, u32[]{:S(2)}) collective-permute-start(bf16[8,2944]{1,0:T(8,128)(2,1)S(1)} %get-tuple-element.54), channel_id=1, source_target_pairs={{0,4},{1,5},{2,6},{3,7},{4,0},{5,1},{6,2},{7,3},{8,12},{9,13},{10,... | collective-permute-start | bytes 141320 | tf_op jit(solution)/shard_map/ppermute | solution.py:157
  47.4 1.6 %collective-permute-done.19.refs_2_ = bf16[8,2944]{1,0:T(8,128)(2,1)S(1)} collective-permute-done((bf16[8,2944]{1,0:T(8,128)(2,1)S(1)}, bf16[8,2944]{1,0:T(8,128)(2,1)S(1)}, u32[]{:S(2)}, u32[]{:S(2)}) %collective-permute-start.19) | collective-permute-done | bytes 47136 | tf_op jit(solution)/shard_map/ppermute | solution.py:157
  49.0 1.3 %collective-permute-done.18.refs_1_ = bf16[8,2944]{1,0:T(8,128)(2,1)S(1)} collective-permute-done((bf16[8,2944]{1,0:T(8,128)(2,1)S(1)}, bf16[8,2944]{1,0:T(8,128)(2,1)S(1)}, u32[]{:S(2)}, u32[]{:S(2)}) %collective-permute-start.18) | collective-permute-done | bytes 47136 | tf_op jit(solution)/shard_map/ppermute | solution.py:157
  50.5 2.1 %collective-permute-start.22 = (bf16[8,2944]{1,0:T(8,128)(2,1)S(1)}, bf16[8,2944]{1,0:T(8,128)(2,1)S(1)}, u32[]{:S(2)}, u32[]{:S(2)}) collective-permute-start(bf16[8,2944]{1,0:T(8,128)(2,1)S(1)} %get-tuple-element.35), channel_id=1, source_target_pairs={{0,12},{1,13},{2,14},{3,15},{4,8},{5,9},{6,10},{7,11},{8,4},{9,5},... | collective-permute-start | bytes 141320 | tf_op jit(solution)/shard_map/ppermute | solution.py:157
  53.3 1.7 %collective-permute-start.20 = (bf16[8,2944]{1,0:T(8,128)(2,1)S(1)}, bf16[8,2944]{1,0:T(8,128)(2,1)S(1)}, u32[]{:S(2)}, u32[]{:S(2)}) collective-permute-start(bf16[8,2944]{1,0:T(8,128)(2,1)S(1)} %get-tuple-element.35), channel_id=1, source_target_pairs={{0,4},{1,5},{2,6},{3,7},{4,0},{5,1},{6,2},{7,3},{8,12},{9,13},{10,... | collective-permute-start | bytes 141320 | tf_op jit(solution)/shard_map/ppermute | solution.py:157
  55.0 2.4 %collective-permute-done.20 = bf16[8,2944]{1,0:T(8,128)(2,1)S(1)} collective-permute-done((bf16[8,2944]{1,0:T(8,128)(2,1)S(1)}, bf16[8,2944]{1,0:T(8,128)(2,1)S(1)}, u32[]{:S(2)}, u32[]{:S(2)}) %collective-permute-start.20) | collective-permute-done | bytes 47136 | tf_op jit(solution)/shard_map/ppermute | solution.py:157
  58.0 1.6 %collective-permute-start.24 = (bf16[32,2944]{1,0:T(8,128)(2,1)S(1)}, bf16[32,2944]{1,0:T(8,128)(2,1)S(1)}, u32[]{:S(2)}, u32[]{:S(2)}) collective-permute-start(bf16[32,2944]{1,0:T(8,128)(2,1)S(1)} %constant_dynamic-update-slice_fusion.4.refs_0_), channel_id=1, source_target_pairs={{0,2},{1,17},{2,0},{3,19},{4,6},{5,21},{6,4},{7,23},{8,10},{9,25},... | collective-permute-start | bytes 565256 | tf_op jit(solution)/shard_map/ppermute | solution.py:157
  59.5 5.4 %collective-permute-done.24.refs_2_ = bf16[32,2944]{1,0:T(8,128)(2,1)S(1)} collective-permute-done((bf16[32,2944]{1,0:T(8,128)(2,1)S(1)}, bf16[32,2944]{1,0:T(8,128)(2,1)S(1)}, u32[]{:S(2)}, u32[]{:S(2)}) %collective-permute-start.24) | collective-permute-done | bytes 188448 | tf_op jit(solution)/shard_map/ppermute | solution.py:157
  66.1 4.5 %collective-permute-done.25.refs_3_ = bf16[32,2944]{1,0:T(8,128)(2,1)S(1)} collective-permute-done((bf16[32,2944]{1,0:T(8,128)(2,1)S(1)}, bf16[32,2944]{1,0:T(8,128)(2,1)S(1)}, u32[]{:S(2)}, u32[]{:S(2)}) %collective-permute-start.25) | collective-permute-done | bytes 188448 | tf_op jit(solution)/shard_map/ppermute | solution.py:157
  70.6 1.4 %collective-permute-done.29.refs_7_ = bf16[32,2944]{1,0:T(8,128)(2,1)S(1)} collective-permute-done((bf16[32,2944]{1,0:T(8,128)(2,1)S(1)}, bf16[32,2944]{1,0:T(8,128)(2,1)S(1)}, u32[]{:S(2)}, u32[]{:S(2)}) %collective-permute-start.29) | collective-permute-done | bytes 188448 | tf_op jit(solution)/shard_map/ppermute | solution.py:157
  72.0 3.2 %ffn_1.1 = (bf16[32,2944]{1,0:T(8,128)(2,1)S(1)}, bf16[32,2944]{1,0:T(8,128)(2,1)S(1)}, bf16[32,2944]{1,0:T(8,128)(2,1)S(1)}, bf16[32,2944]{1,0:T(8,128)(2,1)S(1...) custom-call(bf16[32,2944]{1,0:T(8,128)(2,1)S(1)} %constant_dynamic-u, ...), custom_call_target="tpu_custom_call" | custom-call | tf_op jit(solution)/shard_map/ffn_1/pallas_call | solution.py:98
  77.4 1.5 %collective-permute-start.32 = (bf16[32,2944]{1,0:T(8,128)(2,1)S(1)}, bf16[32,2944]{1,0:T(8,128)(2,1)S(1)}, u32[]{:S(2)}, u32[]{:S(2)}) collective-permute-start(bf16[32,2944]{1,0:T(8,128)(2,1)S(1)} %add_convert_fusion.2), channel_id=1, source_target_pairs={{0,16},{1,3},{2,18},{3,1},{4,20},{5,7},{6,22},{7,5},{8,24},{9,11},... | collective-permute-start | bytes 565256 | tf_op jit(solution)/shard_map/ppermute | solution.py:157
  78.9 3.4 %collective-permute-done.35 = bf16[32,2944]{1,0:T(8,128)(2,1)S(1)} collective-permute-done((bf16[32,2944]{1,0:T(8,128)(2,1)S(1)}, bf16[32,2944]{1,0:T(8,128)(2,1)S(1)}, u32[]{:S(2)}, u32[]{:S(2)}) %collective-permute-start.35) | collective-permute-done | bytes 188448 | tf_op jit(solution)/shard_map/ppermute | solution.py:157
  82.4 1.5 %collective-permute-start.36 = (bf16[32,2944]{1,0:T(8,128)(2,1)S(1)}, bf16[32,2944]{1,0:T(8,128)(2,1)S(1)}, u32[]{:S(2)}, u32[]{:S(2)}) collective-permute-start(bf16[32,2944]{1,0:T(8,128)(2,1)S(1)} %add_convert_fusion), channel_id=1, source_target_pairs={{0,2},{1,17},{2,0},{3,19},{4,6},{5,21},{6,4},{7,23},{8,10},{9,25},... | collective-permute-start | bytes 565256 | tf_op jit(solution)/shard_map/ppermute | solution.py:157
  84.4 3.7 %collective-permute-done.36 = bf16[32,2944]{1,0:T(8,128)(2,1)S(1)} collective-permute-done((bf16[32,2944]{1,0:T(8,128)(2,1)S(1)}, bf16[32,2944]{1,0:T(8,128)(2,1)S(1)}, u32[]{:S(2)}, u32[]{:S(2)}) %collective-permute-start.36) | collective-permute-done | bytes 188448 | tf_op jit(solution)/shard_map/ppermute | solution.py:157
  88.2 1.9 %collective-permute-start.39 = (bf16[8,2944]{1,0:T(8,128)(2,1)S(1)}, bf16[8,2944]{1,0:T(8,128)(2,1)S(1)}, u32[]{:S(2)}, u32[]{:S(2)}) collective-permute-start(bf16[8,2944]{1,0:T(8,128)(2,1)S(1)} %get-tuple-element.49), channel_id=1, source_target_pairs={{0,12},{1,13},{2,14},{3,15},{4,8},{5,9},{6,10},{7,11},{8,4},{9,5},... | collective-permute-start | bytes 141320 | tf_op jit(solution)/shard_map/ppermute | solution.py:157
  90.8 1.9 %collective-permute-start.37 = (bf16[8,2944]{1,0:T(8,128)(2,1)S(1)}, bf16[8,2944]{1,0:T(8,128)(2,1)S(1)}, u32[]{:S(2)}, u32[]{:S(2)}) collective-permute-start(bf16[8,2944]{1,0:T(8,128)(2,1)S(1)} %get-tuple-element.51), channel_id=1, source_target_pairs={{0,4},{1,5},{2,6},{3,7},{4,0},{5,1},{6,2},{7,3},{8,12},{9,13},{10,... | collective-permute-start | bytes 141320 | tf_op jit(solution)/shard_map/ppermute | solution.py:157
  92.7 1.5 %collective-permute-done.39.refs_2_ = bf16[8,2944]{1,0:T(8,128)(2,1)S(1)} collective-permute-done((bf16[8,2944]{1,0:T(8,128)(2,1)S(1)}, bf16[8,2944]{1,0:T(8,128)(2,1)S(1)}, u32[]{:S(2)}, u32[]{:S(2)}) %collective-permute-start.39) | collective-permute-done | bytes 47136 | tf_op jit(solution)/shard_map/ppermute | solution.py:157
  94.1 1.1 %collective-permute-done.38.refs_1_ = bf16[8,2944]{1,0:T(8,128)(2,1)S(1)} collective-permute-done((bf16[8,2944]{1,0:T(8,128)(2,1)S(1)}, bf16[8,2944]{1,0:T(8,128)(2,1)S(1)}, u32[]{:S(2)}, u32[]{:S(2)}) %collective-permute-start.38) | collective-permute-done | bytes 47136 | tf_op jit(solution)/shard_map/ppermute | solution.py:157
  (87 shorter events, 14.5 us)
Async XLA Ops:
  2.4 10.1 %collective-permute-start.2 = (bf16[8,2944]{1,0:T(8,128)(2,1)S(1)}, bf16[8,2944]{1,0:T(8,128)(2,1)S(1)}, u32[]{:S(2)}, u32[]{:S(2)}) collective-permute-start(bf16[8,2944]{1,0:T(8,128)(2,1)S(1)} %get-tuple-element.25), channel_id=1, source_target_pairs={{0,12},{1,13},{2,14},{3,15},{4,8},{5,9},{6,10},{7,11},{8,4},{9,5},... | collective-permute-start | bytes 141320 | tf_op jit(solution)/shard_map/ppermute | solution.py:157
  7.5 5.0 %collective-permute-start.1 = (bf16[8,2944]{1,0:T(8,128)(2,1)S(1)}, bf16[8,2944]{1,0:T(8,128)(2,1)S(1)}, u32[]{:S(2)}, u32[]{:S(2)}) collective-permute-start(bf16[8,2944]{1,0:T(8,128)(2,1)S(1)} %get-tuple-element.25), channel_id=1, source_target_pairs={{0,8},{1,9},{2,10},{3,11},{4,12},{5,13},{6,14},{7,15},{8,0},{9,1},... | collective-permute-start | bytes 141320 | tf_op jit(solution)/shard_map/ppermute | solution.py:157
  7.5 4.1 %collective-permute-start = (bf16[8,2944]{1,0:T(8,128)(2,1)S(1)}, bf16[8,2944]{1,0:T(8,128)(2,1)S(1)}, u32[]{:S(2)}, u32[]{:S(2)}) collective-permute-start(bf16[8,2944]{1,0:T(8,128)(2,1)S(1)} %get-tuple-element.25), channel_id=1, source_target_pairs={{0,4},{1,5},{2,6},{3,7},{4,0},{5,1},{6,2},{7,3},{8,12},{9,13},{10,... | collective-permute-start | bytes 141320 | tf_op jit(solution)/shard_map/ppermute | solution.py:157
  12.4 7.2 %collective-permute-start.4 = (bf16[32,2944]{1,0:T(8,128)(2,1)S(1)}, bf16[32,2944]{1,0:T(8,128)(2,1)S(1)}, u32[]{:S(2)}, u32[]{:S(2)}) collective-permute-start(bf16[32,2944]{1,0:T(8,128)(2,1)S(1)} %constant_dynamic-update-slice_fusion.refs_0_), channel_id=1, source_target_pairs={{0,2},{1,17},{2,0},{3,19},{4,6},{5,21},{6,4},{7,23},{8,10},{9,25},... | collective-permute-start | bytes 565256 | tf_op jit(solution)/shard_map/ppermute | solution.py:157
  14.0 6.3 %collective-permute-start.3 = (bf16[32,2944]{1,0:T(8,128)(2,1)S(1)}, bf16[32,2944]{1,0:T(8,128)(2,1)S(1)}, u32[]{:S(2)}, u32[]{:S(2)}) collective-permute-start(bf16[32,2944]{1,0:T(8,128)(2,1)S(1)} %constant_dynamic-update-slice_fusion.refs_0_), channel_id=1, source_target_pairs={{0,16},{1,3},{2,18},{3,1},{4,20},{5,7},{6,22},{7,5},{8,24},{9,11},... | collective-permute-start | bytes 565256 | tf_op jit(solution)/shard_map/ppermute | solution.py:157
  19.6 5.6 %collective-permute-start.5 = (bf16[32,2944]{1,0:T(8,128)(2,1)S(1)}, bf16[32,2944]{1,0:T(8,128)(2,1)S(1)}, u32[]{:S(2)}, u32[]{:S(2)}) collective-permute-start(bf16[32,2944]{1,0:T(8,128)(2,1)S(1)} %collective-permute-done.4.refs_2_), channel_id=1, source_target_pairs={{0,16},{1,3},{2,18},{3,1},{4,20},{5,7},{6,22},{7,5},{8,24},{9,11},... | collective-permute-start | bytes 565256 | tf_op jit(solution)/shard_map/ppermute | solution.py:157
  19.8 5.5 %collective-permute-start.6 = (bf16[32,2944]{1,0:T(8,128)(2,1)S(1)}, bf16[32,2944]{1,0:T(8,128)(2,1)S(1)}, u32[]{:S(2)}, u32[]{:S(2)}) collective-permute-start(bf16[32,2944]{1,0:T(8,128)(2,1)S(1)} %constant_dynamic-update-slice_fusion.refs_0_), channel_id=1, source_target_pairs={{0,1},{1,0},{2,3},{3,2},{4,5},{5,4},{6,7},{7,6},{8,9},{9,8},{10,11... | collective-permute-start | bytes 565256 | tf_op jit(solution)/shard_map/ppermute | solution.py:157
  19.8 5.5 %collective-permute-start.8 = (bf16[32,2944]{1,0:T(8,128)(2,1)S(1)}, bf16[32,2944]{1,0:T(8,128)(2,1)S(1)}, u32[]{:S(2)}, u32[]{:S(2)}) collective-permute-start(bf16[32,2944]{1,0:T(8,128)(2,1)S(1)} %collective-permute-done.4.refs_2_), channel_id=1, source_target_pairs={{0,1},{1,0},{2,3},{3,2},{4,5},{5,4},{6,7},{7,6},{8,9},{9,8},{10,11... | collective-permute-start | bytes 565256 | tf_op jit(solution)/shard_map/ppermute | solution.py:157
  20.3 5.0 %collective-permute-start.7 = (bf16[32,2944]{1,0:T(8,128)(2,1)S(1)}, bf16[32,2944]{1,0:T(8,128)(2,1)S(1)}, u32[]{:S(2)}, u32[]{:S(2)}) collective-permute-start(bf16[32,2944]{1,0:T(8,128)(2,1)S(1)} %collective-permute-done.3.refs_1_), channel_id=1, source_target_pairs={{0,1},{1,0},{2,3},{3,2},{4,5},{5,4},{6,7},{7,6},{8,9},{9,8},{10,11... | collective-permute-start | bytes 565256 | tf_op jit(solution)/shard_map/ppermute | solution.py:157
  30.1 8.6 %collective-permute-start.10 = (bf16[32,2944]{1,0:T(8,128)(2,1)S(1)}, bf16[32,2944]{1,0:T(8,128)(2,1)S(1)}, u32[]{:S(2)}, u32[]{:S(2)}) collective-permute-start(bf16[32,2944]{1,0:T(8,128)(2,1)S(1)} %get-tuple-element.27), channel_id=1, source_target_pairs={{0,1},{1,0},{2,3},{3,2},{4,5},{5,4},{6,7},{7,6},{8,9},{9,8},{10,11... | collective-permute-start | bytes 565256 | tf_op jit(solution)/shard_map/ppermute | solution.py:157
  31.4 5.6 %collective-permute-start.15 = (bf16[32,2944]{1,0:T(8,128)(2,1)S(1)}, bf16[32,2944]{1,0:T(8,128)(2,1)S(1)}, u32[]{:S(2)}, u32[]{:S(2)}) collective-permute-start(bf16[32,2944]{1,0:T(8,128)(2,1)S(1)} %add_convert_fusion.4), channel_id=1, source_target_pairs={{0,16},{1,3},{2,18},{3,1},{4,20},{5,7},{6,22},{7,5},{8,24},{9,11},... | collective-permute-start | bytes 565256 | tf_op jit(solution)/shard_map/ppermute | solution.py:157
  32.0 7.1 %collective-permute-start.12 = (bf16[32,2944]{1,0:T(8,128)(2,1)S(1)}, bf16[32,2944]{1,0:T(8,128)(2,1)S(1)}, u32[]{:S(2)}, u32[]{:S(2)}) collective-permute-start(bf16[32,2944]{1,0:T(8,128)(2,1)S(1)} %add_convert_fusion.5), channel_id=1, source_target_pairs={{0,16},{1,3},{2,18},{3,1},{4,20},{5,7},{6,22},{7,5},{8,24},{9,11},... | collective-permute-start | bytes 565256 | tf_op jit(solution)/shard_map/ppermute | solution.py:157
  37.2 5.6 %collective-permute-start.16 = (bf16[32,2944]{1,0:T(8,128)(2,1)S(1)}, bf16[32,2944]{1,0:T(8,128)(2,1)S(1)}, u32[]{:S(2)}, u32[]{:S(2)}) collective-permute-start(bf16[32,2944]{1,0:T(8,128)(2,1)S(1)} %add_convert_fusion.3), channel_id=1, source_target_pairs={{0,2},{1,17},{2,0},{3,19},{4,6},{5,21},{6,4},{7,23},{8,10},{9,25},... | collective-permute-start | bytes 565256 | tf_op jit(solution)/shard_map/ppermute | solution.py:157
  42.9 6.0 %collective-permute-start.19 = (bf16[8,2944]{1,0:T(8,128)(2,1)S(1)}, bf16[8,2944]{1,0:T(8,128)(2,1)S(1)}, u32[]{:S(2)}, u32[]{:S(2)}) collective-permute-start(bf16[8,2944]{1,0:T(8,128)(2,1)S(1)} %get-tuple-element.52), channel_id=1, source_target_pairs={{0,12},{1,13},{2,14},{3,15},{4,8},{5,9},{6,10},{7,11},{8,4},{9,5},... | collective-permute-start | bytes 141320 | tf_op jit(solution)/shard_map/ppermute | solution.py:157
  45.1 5.1 %collective-permute-start.18 = (bf16[8,2944]{1,0:T(8,128)(2,1)S(1)}, bf16[8,2944]{1,0:T(8,128)(2,1)S(1)}, u32[]{:S(2)}, u32[]{:S(2)}) collective-permute-start(bf16[8,2944]{1,0:T(8,128)(2,1)S(1)} %get-tuple-element.53), channel_id=1, source_target_pairs={{0,8},{1,9},{2,10},{3,11},{4,12},{5,13},{6,14},{7,15},{8,0},{9,1},... | collective-permute-start | bytes 141320 | tf_op jit(solution)/shard_map/ppermute | solution.py:157
  45.3 4.9 %collective-permute-start.17 = (bf16[8,2944]{1,0:T(8,128)(2,1)S(1)}, bf16[8,2944]{1,0:T(8,128)(2,1)S(1)}, u32[]{:S(2)}, u32[]{:S(2)}) collective-permute-start(bf16[8,2944]{1,0:T(8,128)(2,1)S(1)} %get-tuple-element.54), channel_id=1, source_target_pairs={{0,4},{1,5},{2,6},{3,7},{4,0},{5,1},{6,2},{7,3},{8,12},{9,13},{10,... | collective-permute-start | bytes 141320 | tf_op jit(solution)/shard_map/ppermute | solution.py:157
  50.5 7.4 %collective-permute-start.22 = (bf16[8,2944]{1,0:T(8,128)(2,1)S(1)}, bf16[8,2944]{1,0:T(8,128)(2,1)S(1)}, u32[]{:S(2)}, u32[]{:S(2)}) collective-permute-start(bf16[8,2944]{1,0:T(8,128)(2,1)S(1)} %get-tuple-element.35), channel_id=1, source_target_pairs={{0,12},{1,13},{2,14},{3,15},{4,8},{5,9},{6,10},{7,11},{8,4},{9,5},... | collective-permute-start | bytes 141320 | tf_op jit(solution)/shard_map/ppermute | solution.py:157
  52.6 5.3 %collective-permute-start.21 = (bf16[8,2944]{1,0:T(8,128)(2,1)S(1)}, bf16[8,2944]{1,0:T(8,128)(2,1)S(1)}, u32[]{:S(2)}, u32[]{:S(2)}) collective-permute-start(bf16[8,2944]{1,0:T(8,128)(2,1)S(1)} %get-tuple-element.35), channel_id=1, source_target_pairs={{0,8},{1,9},{2,10},{3,11},{4,12},{5,13},{6,14},{7,15},{8,0},{9,1},... | collective-permute-start | bytes 141320 | tf_op jit(solution)/shard_map/ppermute | solution.py:157
  53.3 4.1 %collective-permute-start.20 = (bf16[8,2944]{1,0:T(8,128)(2,1)S(1)}, bf16[8,2944]{1,0:T(8,128)(2,1)S(1)}, u32[]{:S(2)}, u32[]{:S(2)}) collective-permute-start(bf16[8,2944]{1,0:T(8,128)(2,1)S(1)} %get-tuple-element.35), channel_id=1, source_target_pairs={{0,4},{1,5},{2,6},{3,7},{4,0},{5,1},{6,2},{7,3},{8,12},{9,13},{10,... | collective-permute-start | bytes 141320 | tf_op jit(solution)/shard_map/ppermute | solution.py:157
  58.0 7.0 %collective-permute-start.24 = (bf16[32,2944]{1,0:T(8,128)(2,1)S(1)}, bf16[32,2944]{1,0:T(8,128)(2,1)S(1)}, u32[]{:S(2)}, u32[]{:S(2)}) collective-permute-start(bf16[32,2944]{1,0:T(8,128)(2,1)S(1)} %constant_dynamic-update-slice_fusion.4.refs_0_), channel_id=1, source_target_pairs={{0,2},{1,17},{2,0},{3,19},{4,6},{5,21},{6,4},{7,23},{8,10},{9,25},... | collective-permute-start | bytes 565256 | tf_op jit(solution)/shard_map/ppermute | solution.py:157
  59.5 6.6 %collective-permute-start.23 = (bf16[32,2944]{1,0:T(8,128)(2,1)S(1)}, bf16[32,2944]{1,0:T(8,128)(2,1)S(1)}, u32[]{:S(2)}, u32[]{:S(2)}) collective-permute-start(bf16[32,2944]{1,0:T(8,128)(2,1)S(1)} %constant_dynamic-update-slice_fusion.4.refs_0_), channel_id=1, source_target_pairs={{0,16},{1,3},{2,18},{3,1},{4,20},{5,7},{6,22},{7,5},{8,24},{9,11},... | collective-permute-start | bytes 565256 | tf_op jit(solution)/shard_map/ppermute | solution.py:157
  65.0 5.6 %collective-permute-start.25 = (bf16[32,2944]{1,0:T(8,128)(2,1)S(1)}, bf16[32,2944]{1,0:T(8,128)(2,1)S(1)}, u32[]{:S(2)}, u32[]{:S(2)}) collective-permute-start(bf16[32,2944]{1,0:T(8,128)(2,1)S(1)} %collective-permute-done.24.refs_2_), channel_id=1, source_target_pairs={{0,16},{1,3},{2,18},{3,1},{4,20},{5,7},{6,22},{7,5},{8,24},{9,11},... | collective-permute-start | bytes 565256 | tf_op jit(solution)/shard_map/ppermute | solution.py:157
  65.6 5.0 %collective-permute-start.26 = (bf16[32,2944]{1,0:T(8,128)(2,1)S(1)}, bf16[32,2944]{1,0:T(8,128)(2,1)S(1)}, u32[]{:S(2)}, u32[]{:S(2)}) collective-permute-start(bf16[32,2944]{1,0:T(8,128)(2,1)S(1)} %constant_dynamic-update-slice_fusion.4.refs_0_), channel_id=1, source_target_pairs={{0,1},{1,0},{2,3},{3,2},{4,5},{5,4},{6,7},{7,6},{8,9},{9,8},{10,11... | collective-permute-start | bytes 565256 | tf_op jit(solution)/shard_map/ppermute | solution.py:157
  65.6 5.0 %collective-permute-start.28 = (bf16[32,2944]{1,0:T(8,128)(2,1)S(1)}, bf16[32,2944]{1,0:T(8,128)(2,1)S(1)}, u32[]{:S(2)}, u32[]{:S(2)}) collective-permute-start(bf16[32,2944]{1,0:T(8,128)(2,1)S(1)} %collective-permute-done.24.refs_2_), channel_id=1, source_target_pairs={{0,1},{1,0},{2,3},{3,2},{4,5},{5,4},{6,7},{7,6},{8,9},{9,8},{10,11... | collective-permute-start | bytes 565256 | tf_op jit(solution)/shard_map/ppermute | solution.py:157
  66.1 4.5 %collective-permute-start.27 = (bf16[32,2944]{1,0:T(8,128)(2,1)S(1)}, bf16[32,2944]{1,0:T(8,128)(2,1)S(1)}, u32[]{:S(2)}, u32[]{:S(2)}) collective-permute-start(bf16[32,2944]{1,0:T(8,128)(2,1)S(1)} %collective-permute-done.23.refs_1_), channel_id=1, source_target_pairs={{0,1},{1,0},{2,3},{3,2},{4,5},{5,4},{6,7},{7,6},{8,9},{9,8},{10,11... | collective-permute-start | bytes 565256 | tf_op jit(solution)/shard_map/ppermute | solution.py:157
  75.4 8.6 %collective-permute-start.30 = (bf16[32,2944]{1,0:T(8,128)(2,1)S(1)}, bf16[32,2944]{1,0:T(8,128)(2,1)S(1)}, u32[]{:S(2)}, u32[]{:S(2)}) collective-permute-start(bf16[32,2944]{1,0:T(8,128)(2,1)S(1)} %get-tuple-element.37), channel_id=1, source_target_pairs={{0,1},{1,0},{2,3},{3,2},{4,5},{5,4},{6,7},{7,6},{8,9},{9,8},{10,11... | collective-permute-start | bytes 565256 | tf_op jit(solution)/shard_map/ppermute | solution.py:157
  76.7 5.6 %collective-permute-start.35 = (bf16[32,2944]{1,0:T(8,128)(2,1)S(1)}, bf16[32,2944]{1,0:T(8,128)(2,1)S(1)}, u32[]{:S(2)}, u32[]{:S(2)}) collective-permute-start(bf16[32,2944]{1,0:T(8,128)(2,1)S(1)} %add_convert_fusion.1), channel_id=1, source_target_pairs={{0,16},{1,3},{2,18},{3,1},{4,20},{5,7},{6,22},{7,5},{8,24},{9,11},... | collective-permute-start | bytes 565256 | tf_op jit(solution)/shard_map/ppermute | solution.py:157
  77.4 7.0 %collective-permute-start.32 = (bf16[32,2944]{1,0:T(8,128)(2,1)S(1)}, bf16[32,2944]{1,0:T(8,128)(2,1)S(1)}, u32[]{:S(2)}, u32[]{:S(2)}) collective-permute-start(bf16[32,2944]{1,0:T(8,128)(2,1)S(1)} %add_convert_fusion.2), channel_id=1, source_target_pairs={{0,16},{1,3},{2,18},{3,1},{4,20},{5,7},{6,22},{7,5},{8,24},{9,11},... | collective-permute-start | bytes 565256 | tf_op jit(solution)/shard_map/ppermute | solution.py:157
  82.4 5.6 %collective-permute-start.36 = (bf16[32,2944]{1,0:T(8,128)(2,1)S(1)}, bf16[32,2944]{1,0:T(8,128)(2,1)S(1)}, u32[]{:S(2)}, u32[]{:S(2)}) collective-permute-start(bf16[32,2944]{1,0:T(8,128)(2,1)S(1)} %add_convert_fusion), channel_id=1, source_target_pairs={{0,2},{1,17},{2,0},{3,19},{4,6},{5,21},{6,4},{7,23},{8,10},{9,25},... | collective-permute-start | bytes 565256 | tf_op jit(solution)/shard_map/ppermute | solution.py:157
  88.2 5.9 %collective-permute-start.39 = (bf16[8,2944]{1,0:T(8,128)(2,1)S(1)}, bf16[8,2944]{1,0:T(8,128)(2,1)S(1)}, u32[]{:S(2)}, u32[]{:S(2)}) collective-permute-start(bf16[8,2944]{1,0:T(8,128)(2,1)S(1)} %get-tuple-element.49), channel_id=1, source_target_pairs={{0,12},{1,13},{2,14},{3,15},{4,8},{5,9},{6,10},{7,11},{8,4},{9,5},... | collective-permute-start | bytes 141320 | tf_op jit(solution)/shard_map/ppermute | solution.py:157
  90.1 5.2 %collective-permute-start.38 = (bf16[8,2944]{1,0:T(8,128)(2,1)S(1)}, bf16[8,2944]{1,0:T(8,128)(2,1)S(1)}, u32[]{:S(2)}, u32[]{:S(2)}) collective-permute-start(bf16[8,2944]{1,0:T(8,128)(2,1)S(1)} %get-tuple-element.50), channel_id=1, source_target_pairs={{0,8},{1,9},{2,10},{3,11},{4,12},{5,13},{6,14},{7,15},{8,0},{9,1},... | collective-permute-start | bytes 141320 | tf_op jit(solution)/shard_map/ppermute | solution.py:157
  90.8 4.6 %collective-permute-start.37 = (bf16[8,2944]{1,0:T(8,128)(2,1)S(1)}, bf16[8,2944]{1,0:T(8,128)(2,1)S(1)}, u32[]{:S(2)}, u32[]{:S(2)}) collective-permute-start(bf16[8,2944]{1,0:T(8,128)(2,1)S(1)} %get-tuple-element.51), channel_id=1, source_target_pairs={{0,4},{1,5},{2,6},{3,7},{4,0},{5,1},{6,2},{7,3},{8,12},{9,13},{10,... | collective-permute-start | bytes 141320 | tf_op jit(solution)/shard_map/ppermute | solution.py:157
  (15 other events, 114.2 us)

commit v4 on v3

--- a/solution.py
+++ b/solution.py
@@ -8,6 +8,7 @@
 from jax.sharding import PartitionSpec as P
 
 LANES = 128
+WAVES = 2
 
 
 def rms_rows(stream):
@@ -24,15 +25,14 @@
 SMEM = pl.BlockSpec(memory_space=pltpu.SMEM)
 
 
-def member_tail(layer, shift, lanes, routes_ref, placement_ref):
-    top_k, tok_rows = routes_ref.shape[1:]
-    experts = placement_ref.shape[1]
+def member_tail(layer, shift, lanes, tok_rows, experts, table_ref):
+    top_k = table_ref.shape[1] - 1
     ids = lax.broadcasted_iota(jnp.int32, (experts, tok_rows), 0)
     named = jnp.zeros((experts, tok_rows), jnp.float32)
     for choice in range(top_k):
-        named = jnp.where(ids == routes_ref[layer, choice : choice + 1, :], 1.0, named)
+        named = jnp.where(ids == table_ref[layer, choice : choice + 1, :tok_rows], 1.0, named)
     lane = lax.broadcasted_iota(jnp.int32, (lanes, experts), 0)
-    served = jnp.where(lane == placement_ref[layer : layer + 1, :] + shift, 1.0, 0.0)
+    served = jnp.where(lane == table_ref[layer, top_k : top_k + 1, :experts] + shift, 1.0, 0.0)
     return lax.dot_general(named, served, (((0,), (1,)), ((), ())), preferred_element_type=jnp.float32)
 
 
@@ -45,10 +45,10 @@
         payload_ref[:, tail:model] = normed[:, tail:]
 
 
-def first_kernel(model, tail, tokens_ref, routes_ref, placement_ref, payload_ref, tails_ref):
+def first_kernel(model, tail, experts, tokens_ref, table_ref, payload_ref, tails_ref):
     lanes = payload_ref.shape[1] - tail
-    for layer in range(routes_ref.shape[0]):
-        tails_ref[layer] = member_tail(layer, model - tail, lanes, routes_ref, placement_ref)
+    for layer in range(table_ref.shape[0]):
+        tails_ref[layer] = member_tail(layer, model - tail, lanes, tokens_ref.shape[0], experts, table_ref)
     write_payload(tokens_ref[...].astype(jnp.float32), tails_ref[0], model, tail, payload_ref)
 
 
@@ -66,13 +66,15 @@
 
 def ffn_kernel(layer, count, *refs):
     pieces, (router_ref, up_ref, down_ref), outs, (rows_ref, hidden_ref) = refs[:count], refs[count : count + 3], refs[count + 3 : -2], refs[-2:]
-    size, width = pieces[0].shape
+    total, width = rows_ref.shape
     model, units = router_ref.shape[-1], up_ref.shape[2]
-    for index, piece in enumerate(pieces):
-        rows_ref[index * size : (index + 1) * size, :] = piece[...]
+    size, filled = outs[0].shape[0], 0
+    for piece in pieces:
+        rows_ref[filled : filled + piece.shape[0], :] = piece[...]
+        filled += piece.shape[0]
     slot, block = lax.axis_index("expert"), lax.axis_index("dp")
     tail = model // LANES * LANES
-    lane = lax.broadcasted_iota(jnp.int32, (count * size, width - tail), 1)
+    lane = lax.broadcasted_iota(jnp.int32, (total, width - tail), 1)
     here = lane == (model - tail) + slot
     member = jnp.sum(jnp.where(here, rows_ref[:, tail:].astype(jnp.float32), 0.0), axis=1, keepdims=True)
     by_rows = (((1,), (1,)), ((), ()))
@@ -94,13 +96,14 @@
 
 
 def expert_ffn(layer, pieces, router, up, down):
-    count, (size, width), units = len(pieces), pieces[0].shape, up.shape[2]
+    count, width, units = len(pieces), pieces[0].shape[1], up.shape[2]
+    total = sum(piece.shape[0] for piece in pieces)
     return pl.pallas_call(
         functools.partial(ffn_kernel, layer, count),
-        out_shape=[jax.ShapeDtypeStruct((size, width), jnp.bfloat16)] * count,
+        out_shape=[jax.ShapeDtypeStruct((total // 8, width), jnp.bfloat16)] * 8,
         in_specs=[VMEM] * (count + 3),
-        out_specs=[VMEM] * count,
-        scratch_shapes=[pltpu.VMEM((count * size, width), jnp.bfloat16), pltpu.VMEM((count * size, units), jnp.bfloat16)],
+        out_specs=[VMEM] * 8,
+        scratch_shapes=[pltpu.VMEM((total, width), jnp.bfloat16), pltpu.VMEM((total, units), jnp.bfloat16)],
         compiler_params=pltpu.CompilerParams(vmem_limit_bytes=16 * 1024 * 1024),
         name=f"ffn_{layer}",
     )(*pieces, router, up, down)
@@ -142,30 +145,38 @@
     up_rows, router = jnp.swapaxes(up_weight, 2, 3), router_weight.reshape(layers, model)
     small = pltpu.CompilerParams(vmem_limit_bytes=4 * 1024 * 1024)
     payload_shape = jax.ShapeDtypeStruct((tok_rows, width), jnp.bfloat16)
+    top_k, experts = routes.shape[2], placement.shape[1]
+    lanes = max(tok_rows, experts)
+    table = lax.pad(jnp.swapaxes(routes, 1, 2), 0, [(0, 0, 0), (0, 1, 0), (0, lanes - tok_rows, 0)]) + lax.pad(
+        placement[:, None, :], 0, [(0, 0, 0), (top_k, 0, 0), (0, lanes - experts, 0)]
+    )
     stream = tokens
     own, tails = pl.pallas_call(
-        functools.partial(first_kernel, model, tail),
+        functools.partial(first_kernel, model, tail, experts),
         out_shape=[payload_shape, jax.ShapeDtypeStruct((layers, tok_rows, width - tail), jnp.float32)],
-        in_specs=[VMEM] * 3,
+        in_specs=[VMEM] * 2,
         out_specs=[VMEM] * 2,
         compiler_params=small,
         cost_estimate=pl.CostEstimate(flops=20_000_000_000, transcendentals=0, bytes_accessed=0),
         name="first",
-    )(tokens, jnp.swapaxes(routes, 1, 2), placement)
+    )(tokens, table)
+
+    wave = lengths // WAVES
 
     def move(value, pairs):
         return lax.ppermute(value, axes, pairs)
 
     for layer in range(layers):
-        here = jnp.concatenate([own] + [move(own, shift(step)) for step in range(1, lengths)], axis=0)
-        first = move(here, first_swap)
+        line = [own] + [move(own, shift(step)) for step in range(1, lengths)]
+        parts = [jnp.concatenate(line[start : start + wave], axis=0) for start in range(0, lengths, wave)]
+        here = jnp.concatenate(line, axis=0)
+        firsts = [move(part, first_swap) for part in parts]
         second = move(here, second_swap)
-        across = move(first, second_swap)
-        near = [here, second, first, across]
+        acrosses = [move(part, second_swap) for part in firsts]
+        near = [here, second] + firsts + acrosses
         outs = expert_ffn(layer, near + [move(piece, core_swap) for piece in near], router, up_rows, down_weight)
-        wide = [value.astype(jnp.float32) for value in outs[:4]]
         here, second, first, across = [
-            mine + move(theirs, core_swap).astype(jnp.float32) for mine, theirs in zip(wide, outs[4:])
+            mine.astype(jnp.float32) + move(theirs, core_swap).astype(jnp.float32) for mine, theirs in zip(outs[:4], outs[4:])
         ]
         first = first + move(across.astype(jnp.bfloat16), second_swap).astype(jnp.float32)
         here = here + move(second.astype(jnp.bfloat16), second_swap).astype(jnp.float32)

time: 96.3 us -> 93.3 us (0.969)
  waiting for transfers between devices: 50.8 us -> 44.8 us
  starting transfers between devices: 34.8 us -> 38.3 us
  local copies, waits for them, and re-layouts: 2.28 us -> 0.92 us
    ppermute x40 -> x48, waiting for transfers between devices: 50.8 us -> 44.8 us  [move(): return lax.ppermute(value, axes, pairs)]
    ppermute x40 -> x48, starting transfers between devices: 34.8 us -> 38.3 us  [move(): return lax.ppermute(value, axes, pairs)]
    unnamed x20 -> x16, local copies, waits for them, and re-layouts: 2.22 us -> 0.86 us
  transfers between devices with their start and end apart: 40 -> 48, of which waited for: 24 -> 26; matrix products, arithmetic and copies ran while one was open for 0% -> 0% of each run, Pallas kernels for 0% -> 0%
where the time goes in v4:
time: 93.3 us; the launch traced here: 93.1 us
  waiting for transfers between devices  44.8 us (48%)
  starting transfers between devices  38.3 us (41%)
  Pallas kernels  7.62 us (8%)
  other arithmetic  1.28 us (1%)
    ppermute x48, waiting for transfers between devices, move(): return lax.ppermute(value, axes, pairs)  44.8 us
    ppermute x48, starting transfers between devices, move(): return lax.ppermute(value, axes, pairs)  38.3 us
    pallas_call x2, Pallas kernels, expert_ffn(): pl.pallas_call(functools.partial(ffn_kernel, layer, count), out_shape=[ja...  6.38 us
  transfers between devices with their start and end apart: 48, of which 26 were waited for; matrix products, arithmetic and copies ran while one was open for 0% of the time, Pallas kernels for 0%

profile of v4, /device:TPU:0, one launch (start us, length us, event | category | flops | bytes accessed | tf_op | source)
XLA Modules:
  0.0 93.1 jit_solution(14179784588928372260)
XLA Ops:
  1.7 5.1 %collective-permute-start.2 = (bf16[8,2944]{1,0:T(8,128)(2,1)S(1)}, bf16[8,2944]{1,0:T(8,128)(2,1)S(1)}, u32[]{:S(2)}, u32[]{:S(2)}) collective-permute-start(bf16[8,2944]{1,0:T(8,128)(2,1)S(1)} %get-tuple-element.25), channel_id=1, source_target_pairs={{0,12},{1,13},{2,14},{3,15},{4,8},{5,9},{6,10},{7,11},{8,4},{9,5},... | collective-permute-start | bytes 141320 | tf_op jit(solution)/shard_map/ppermute | solution.py:167
  7.4 1.4 %collective-permute-done.2 = bf16[8,2944]{1,0:T(8,128)(2,1)S(1)} collective-permute-done((bf16[8,2944]{1,0:T(8,128)(2,1)S(1)}, bf16[8,2944]{1,0:T(8,128)(2,1)S(1)}, u32[]{:S(2)}, u32[]{:S(2)}) %collective-permute-start.2) | collective-permute-done | bytes 47136 | tf_op jit(solution)/shard_map/ppermute | solution.py:167
  8.9 2.9 %collective-permute-done.1 = bf16[8,2944]{1,0:T(8,128)(2,1)S(1)} collective-permute-done((bf16[8,2944]{1,0:T(8,128)(2,1)S(1)}, bf16[8,2944]{1,0:T(8,128)(2,1)S(1)}, u32[]{:S(2)}, u32[]{:S(2)}) %collective-permute-start.1) | collective-permute-done | bytes 47136 | tf_op jit(solution)/shard_map/ppermute | solution.py:167
  11.8 1.6 %collective-permute-start.5 = (bf16[16,2944]{1,0:T(8,128)(2,1)S(1)}, bf16[16,2944]{1,0:T(8,128)(2,1)S(1)}, u32[]{:S(2)}, u32[]{:S(2)}) collective-permute-start(bf16[16,2944]{1,0:T(8,128)(2,1)S(1)} %pad_maximum_fusion.1), channel_id=1, source_target_pairs={{0,2},{1,17},{2,0},{3,19},{4,6},{5,21},{6,4},{7,23},{8,10},{9,25},... | collective-permute-start | bytes 282632 | tf_op jit(solution)/shard_map/ppermute | solution.py:167
  13.4 1.6 %collective-permute-start.3 = (bf16[32,2944]{1,0:T(8,128)(2,1)S(1)}, bf16[32,2944]{1,0:T(8,128)(2,1)S(1)}, u32[]{:S(2)}, u32[]{:S(2)}) collective-permute-start(bf16[32,2944]{1,0:T(8,128)(2,1)S(1)} %constant_dynamic-update-slice_fusion.refs_0_), channel_id=1, source_target_pairs={{0,16},{1,3},{2,18},{3,1},{4,20},{5,7},{6,22},{7,5},{8,24},{9,11},... | collective-permute-start | bytes 565256 | tf_op jit(solution)/shard_map/ppermute | solution.py:167
  15.6 1.7 %collective-permute-done.5.refs_3_ = bf16[16,2944]{1,0:T(8,128)(2,1)S(1)} collective-permute-done((bf16[16,2944]{1,0:T(8,128)(2,1)S(1)}, bf16[16,2944]{1,0:T(8,128)(2,1)S(1)}, u32[]{:S(2)}, u32[]{:S(2)}) %collective-permute-start.5) | collective-permute-done | bytes 94240 | tf_op jit(solution)/shard_map/ppermute | solution.py:167
  18.4 1.2 %collective-permute-done.4.refs_2_ = bf16[16,2944]{1,0:T(8,128)(2,1)S(1)} collective-permute-done((bf16[16,2944]{1,0:T(8,128)(2,1)S(1)}, bf16[16,2944]{1,0:T(8,128)(2,1)S(1)}, u32[]{:S(2)}, u32[]{:S(2)}) %collective-permute-start.4) | collective-permute-done | bytes 94240 | tf_op jit(solution)/shard_map/ppermute | solution.py:167
  20.6 1.7 %collective-permute-done.7.refs_5_ = bf16[16,2944]{1,0:T(8,128)(2,1)S(1)} collective-permute-done((bf16[16,2944]{1,0:T(8,128)(2,1)S(1)}, bf16[16,2944]{1,0:T(8,128)(2,1)S(1)}, u32[]{:S(2)}, u32[]{:S(2)}) %collective-permute-start.7) | collective-permute-done | bytes 94240 | tf_op jit(solution)/shard_map/ppermute | solution.py:167
  22.3 1.9 %collective-permute-done.6.refs_4_ = bf16[16,2944]{1,0:T(8,128)(2,1)S(1)} collective-permute-done((bf16[16,2944]{1,0:T(8,128)(2,1)S(1)}, bf16[16,2944]{1,0:T(8,128)(2,1)S(1)}, u32[]{:S(2)}, u32[]{:S(2)}) %collective-permute-start.6) | collective-permute-done | bytes 94240 | tf_op jit(solution)/shard_map/ppermute | solution.py:167
  24.2 1.3 %collective-permute-done.12.refs_10_ = bf16[16,2944]{1,0:T(8,128)(2,1)S(1)} collective-permute-done((bf16[16,2944]{1,0:T(8,128)(2,1)S(1)}, bf16[16,2944]{1,0:T(8,128)(2,1)S(1)}, u32[]{:S(2)}, u32[]{:S(2)}) %collective-permute-start.12) | collective-permute-done | bytes 94240 | tf_op jit(solution)/shard_map/ppermute | solution.py:167
  25.5 3.2 %ffn_0.1 = (bf16[32,2944]{1,0:T(8,128)(2,1)S(1)}, bf16[32,2944]{1,0:T(8,128)(2,1)S(1)}, bf16[32,2944]{1,0:T(8,128)(2,1)S(1)}, bf16[32,2944]{1,0:T(8,128)(2,1)S(1...) custom-call(bf16[32,2944]{1,0:T(8,128)(2,1)S(1)} %constant_dynamic-u, ...), custom_call_target="tpu_custom_call" | custom-call | tf_op jit(solution)/shard_map/ffn_0/pallas_call | solution.py:101
  30.9 1.6 %collective-permute-start.16 = (bf16[32,2944]{1,0:T(8,128)(2,1)S(1)}, bf16[32,2944]{1,0:T(8,128)(2,1)S(1)}, u32[]{:S(2)}, u32[]{:S(2)}) collective-permute-start(bf16[32,2944]{1,0:T(8,128)(2,1)S(1)} %add_convert_fusion.5), channel_id=1, source_target_pairs={{0,16},{1,3},{2,18},{3,1},{4,20},{5,7},{6,22},{7,5},{8,24},{9,11},... | collective-permute-start | bytes 565256 | tf_op jit(solution)/shard_map/ppermute | solution.py:167
  32.5 3.4 %collective-permute-done.19 = bf16[32,2944]{1,0:T(8,128)(2,1)S(1)} collective-permute-done((bf16[32,2944]{1,0:T(8,128)(2,1)S(1)}, bf16[32,2944]{1,0:T(8,128)(2,1)S(1)}, u32[]{:S(2)}, u32[]{:S(2)}) %collective-permute-start.19) | collective-permute-done | bytes 188448 | tf_op jit(solution)/shard_map/ppermute | solution.py:167
  36.7 1.2 %collective-permute-done.16 = bf16[32,2944]{1,0:T(8,128)(2,1)S(1)} collective-permute-done((bf16[32,2944]{1,0:T(8,128)(2,1)S(1)}, bf16[32,2944]{1,0:T(8,128)(2,1)S(1)}, u32[]{:S(2)}, u32[]{:S(2)}) %collective-permute-start.16) | collective-permute-done | bytes 188448 | tf_op jit(solution)/shard_map/ppermute | solution.py:167
  37.9 3.7 %collective-permute-done.20 = bf16[32,2944]{1,0:T(8,128)(2,1)S(1)} collective-permute-done((bf16[32,2944]{1,0:T(8,128)(2,1)S(1)}, bf16[32,2944]{1,0:T(8,128)(2,1)S(1)}, u32[]{:S(2)}, u32[]{:S(2)}) %collective-permute-start.20) | collective-permute-done | bytes 188448 | tf_op jit(solution)/shard_map/ppermute | solution.py:167
  41.7 2.0 %collective-permute-start.23 = (bf16[8,2944]{1,0:T(8,128)(2,1)S(1)}, bf16[8,2944]{1,0:T(8,128)(2,1)S(1)}, u32[]{:S(2)}, u32[]{:S(2)}) collective-permute-start(bf16[8,2944]{1,0:T(8,128)(2,1)S(1)} %get-tuple-element.52), channel_id=1, source_target_pairs={{0,12},{1,13},{2,14},{3,15},{4,8},{5,9},{6,10},{7,11},{8,4},{9,5},... | collective-permute-start | bytes 141320 | tf_op jit(solution)/shard_map/ppermute | solution.py:167
  43.8 2.4 %collective-permute-start.21 = (bf16[8,2944]{1,0:T(8,128)(2,1)S(1)}, bf16[8,2944]{1,0:T(8,128)(2,1)S(1)}, u32[]{:S(2)}, u32[]{:S(2)}) collective-permute-start(bf16[8,2944]{1,0:T(8,128)(2,1)S(1)} %get-tuple-element.54), channel_id=1, source_target_pairs={{0,4},{1,5},{2,6},{3,7},{4,0},{5,1},{6,2},{7,3},{8,12},{9,13},{10,... | collective-permute-start | bytes 141320 | tf_op jit(solution)/shard_map/ppermute | solution.py:167
  46.2 1.5 %collective-permute-done.23.refs_2_ = bf16[8,2944]{1,0:T(8,128)(2,1)S(1)} collective-permute-done((bf16[8,2944]{1,0:T(8,128)(2,1)S(1)}, bf16[8,2944]{1,0:T(8,128)(2,1)S(1)}, u32[]{:S(2)}, u32[]{:S(2)}) %collective-permute-start.23) | collective-permute-done | bytes 47136 | tf_op jit(solution)/shard_map/ppermute | solution.py:167
  49.0 2.0 %collective-permute-start.26 = (bf16[8,2944]{1,0:T(8,128)(2,1)S(1)}, bf16[8,2944]{1,0:T(8,128)(2,1)S(1)}, u32[]{:S(2)}, u32[]{:S(2)}) collective-permute-start(bf16[8,2944]{1,0:T(8,128)(2,1)S(1)} %get-tuple-element.35), channel_id=1, source_target_pairs={{0,12},{1,13},{2,14},{3,15},{4,8},{5,9},{6,10},{7,11},{8,4},{9,5},... | collective-permute-start | bytes 141320 | tf_op jit(solution)/shard_map/ppermute | solution.py:167
  52.1 1.4 %collective-permute-start.24 = (bf16[8,2944]{1,0:T(8,128)(2,1)S(1)}, bf16[8,2944]{1,0:T(8,128)(2,1)S(1)}, u32[]{:S(2)}, u32[]{:S(2)}) collective-permute-start(bf16[8,2944]{1,0:T(8,128)(2,1)S(1)} %get-tuple-element.35), channel_id=1, source_target_pairs={{0,4},{1,5},{2,6},{3,7},{4,0},{5,1},{6,2},{7,3},{8,12},{9,13},{10,... | collective-permute-start | bytes 141320 | tf_op jit(solution)/shard_map/ppermute | solution.py:167
  53.5 1.5 %collective-permute-done.26 = bf16[8,2944]{1,0:T(8,128)(2,1)S(1)} collective-permute-done((bf16[8,2944]{1,0:T(8,128)(2,1)S(1)}, bf16[8,2944]{1,0:T(8,128)(2,1)S(1)}, u32[]{:S(2)}, u32[]{:S(2)}) %collective-permute-start.26) | collective-permute-done | bytes 47136 | tf_op jit(solution)/shard_map/ppermute | solution.py:167
  55.0 1.6 %collective-permute-done.25 = bf16[8,2944]{1,0:T(8,128)(2,1)S(1)} collective-permute-done((bf16[8,2944]{1,0:T(8,128)(2,1)S(1)}, bf16[8,2944]{1,0:T(8,128)(2,1)S(1)}, u32[]{:S(2)}, u32[]{:S(2)}) %collective-permute-start.25) | collective-permute-done | bytes 47136 | tf_op jit(solution)/shard_map/ppermute | solution.py:167
  59.3 1.9 %collective-permute-done.29.refs_3_ = bf16[16,2944]{1,0:T(8,128)(2,1)S(1)} collective-permute-done((bf16[16,2944]{1,0:T(8,128)(2,1)S(1)}, bf16[16,2944]{1,0:T(8,128)(2,1)S(1)}, u32[]{:S(2)}, u32[]{:S(2)}) %collective-permute-start.29) | collective-permute-done | bytes 94240 | tf_op jit(solution)/shard_map/ppermute | solution.py:167
  64.7 1.6 %collective-permute-done.31.refs_5_ = bf16[16,2944]{1,0:T(8,128)(2,1)S(1)} collective-permute-done((bf16[16,2944]{1,0:T(8,128)(2,1)S(1)}, bf16[16,2944]{1,0:T(8,128)(2,1)S(1)}, u32[]{:S(2)}, u32[]{:S(2)}) %collective-permute-start.31) | collective-permute-done | bytes 94240 | tf_op jit(solution)/shard_map/ppermute | solution.py:167
  66.3 1.5 %collective-permute-done.30.refs_4_ = bf16[16,2944]{1,0:T(8,128)(2,1)S(1)} collective-permute-done((bf16[16,2944]{1,0:T(8,128)(2,1)S(1)}, bf16[16,2944]{1,0:T(8,128)(2,1)S(1)}, u32[]{:S(2)}, u32[]{:S(2)}) %collective-permute-start.30) | collective-permute-done | bytes 94240 | tf_op jit(solution)/shard_map/ppermute | solution.py:167
  67.8 1.3 %collective-permute-done.36.refs_10_ = bf16[16,2944]{1,0:T(8,128)(2,1)S(1)} collective-permute-done((bf16[16,2944]{1,0:T(8,128)(2,1)S(1)}, bf16[16,2944]{1,0:T(8,128)(2,1)S(1)}, u32[]{:S(2)}, u32[]{:S(2)}) %collective-permute-start.36) | collective-permute-done | bytes 94240 | tf_op jit(solution)/shard_map/ppermute | solution.py:167
  69.1 3.2 %ffn_1.1 = (bf16[32,2944]{1,0:T(8,128)(2,1)S(1)}, bf16[32,2944]{1,0:T(8,128)(2,1)S(1)}, bf16[32,2944]{1,0:T(8,128)(2,1)S(1)}, bf16[32,2944]{1,0:T(8,128)(2,1)S(1...) custom-call(bf16[32,2944]{1,0:T(8,128)(2,1)S(1)} %constant_dynamic-u, ...), custom_call_target="tpu_custom_call" | custom-call | tf_op jit(solution)/shard_map/ffn_1/pallas_call | solution.py:101
  76.0 3.4 %collective-permute-done.43 = bf16[32,2944]{1,0:T(8,128)(2,1)S(1)} collective-permute-done((bf16[32,2944]{1,0:T(8,128)(2,1)S(1)}, bf16[32,2944]{1,0:T(8,128)(2,1)S(1)}, u32[]{:S(2)}, u32[]{:S(2)}) %collective-permute-start.43) | collective-permute-done | bytes 188448 | tf_op jit(solution)/shard_map/ppermute | solution.py:167
  81.5 3.7 %collective-permute-done.44 = bf16[32,2944]{1,0:T(8,128)(2,1)S(1)} collective-permute-done((bf16[32,2944]{1,0:T(8,128)(2,1)S(1)}, bf16[32,2944]{1,0:T(8,128)(2,1)S(1)}, u32[]{:S(2)}, u32[]{:S(2)}) %collective-permute-start.44) | collective-permute-done | bytes 188448 | tf_op jit(solution)/shard_map/ppermute | solution.py:167
  85.3 1.9 %collective-permute-start.47 = (bf16[8,2944]{1,0:T(8,128)(2,1)S(1)}, bf16[8,2944]{1,0:T(8,128)(2,1)S(1)}, u32[]{:S(2)}, u32[]{:S(2)}) collective-permute-start(bf16[8,2944]{1,0:T(8,128)(2,1)S(1)} %get-tuple-element.49), channel_id=1, source_target_pairs={{0,12},{1,13},{2,14},{3,15},{4,8},{5,9},{6,10},{7,11},{8,4},{9,5},... | collective-permute-start | bytes 141320 | tf_op jit(solution)/shard_map/ppermute | solution.py:167
  87.2 2.5 %collective-permute-start.45 = (bf16[8,2944]{1,0:T(8,128)(2,1)S(1)}, bf16[8,2944]{1,0:T(8,128)(2,1)S(1)}, u32[]{:S(2)}, u32[]{:S(2)}) collective-permute-start(bf16[8,2944]{1,0:T(8,128)(2,1)S(1)} %get-tuple-element.51), channel_id=1, source_target_pairs={{0,4},{1,5},{2,6},{3,7},{4,0},{5,1},{6,2},{7,3},{8,12},{9,13},{10,... | collective-permute-start | bytes 141320 | tf_op jit(solution)/shard_map/ppermute | solution.py:167
  89.7 1.5 %collective-permute-done.47.refs_2_ = bf16[8,2944]{1,0:T(8,128)(2,1)S(1)} collective-permute-done((bf16[8,2944]{1,0:T(8,128)(2,1)S(1)}, bf16[8,2944]{1,0:T(8,128)(2,1)S(1)}, u32[]{:S(2)}, u32[]{:S(2)}) %collective-permute-start.47) | collective-permute-done | bytes 47136 | tf_op jit(solution)/shard_map/ppermute | solution.py:167
  (104 shorter events, 24.7 us)
Async XLA Ops:
  1.7 7.2 %collective-permute-start.2 = (bf16[8,2944]{1,0:T(8,128)(2,1)S(1)}, bf16[8,2944]{1,0:T(8,128)(2,1)S(1)}, u32[]{:S(2)}, u32[]{:S(2)}) collective-permute-start(bf16[8,2944]{1,0:T(8,128)(2,1)S(1)} %get-tuple-element.25), channel_id=1, source_target_pairs={{0,12},{1,13},{2,14},{3,15},{4,8},{5,9},{6,10},{7,11},{8,4},{9,5},... | collective-permute-start | bytes 141320 | tf_op jit(solution)/shard_map/ppermute | solution.py:167
  6.8 5.0 %collective-permute-start.1 = (bf16[8,2944]{1,0:T(8,128)(2,1)S(1)}, bf16[8,2944]{1,0:T(8,128)(2,1)S(1)}, u32[]{:S(2)}, u32[]{:S(2)}) collective-permute-start(bf16[8,2944]{1,0:T(8,128)(2,1)S(1)} %get-tuple-element.25), channel_id=1, source_target_pairs={{0,8},{1,9},{2,10},{3,11},{4,12},{5,13},{6,14},{7,15},{8,0},{9,1},... | collective-permute-start | bytes 141320 | tf_op jit(solution)/shard_map/ppermute | solution.py:167
  6.8 6.5 %collective-permute-start = (bf16[8,2944]{1,0:T(8,128)(2,1)S(1)}, bf16[8,2944]{1,0:T(8,128)(2,1)S(1)}, u32[]{:S(2)}, u32[]{:S(2)}) collective-permute-start(bf16[8,2944]{1,0:T(8,128)(2,1)S(1)} %get-tuple-element.25), channel_id=1, source_target_pairs={{0,4},{1,5},{2,6},{3,7},{4,0},{5,1},{6,2},{7,3},{8,12},{9,13},{10,... | collective-permute-start | bytes 141320 | tf_op jit(solution)/shard_map/ppermute | solution.py:167
  11.8 5.4 %collective-permute-start.5 = (bf16[16,2944]{1,0:T(8,128)(2,1)S(1)}, bf16[16,2944]{1,0:T(8,128)(2,1)S(1)}, u32[]{:S(2)}, u32[]{:S(2)}) collective-permute-start(bf16[16,2944]{1,0:T(8,128)(2,1)S(1)} %pad_maximum_fusion.1), channel_id=1, source_target_pairs={{0,2},{1,17},{2,0},{3,19},{4,6},{5,21},{6,4},{7,23},{8,10},{9,25},... | collective-permute-start | bytes 282632 | tf_op jit(solution)/shard_map/ppermute | solution.py:167
  13.4 6.7 %collective-permute-start.3 = (bf16[32,2944]{1,0:T(8,128)(2,1)S(1)}, bf16[32,2944]{1,0:T(8,128)(2,1)S(1)}, u32[]{:S(2)}, u32[]{:S(2)}) collective-permute-start(bf16[32,2944]{1,0:T(8,128)(2,1)S(1)} %constant_dynamic-update-slice_fusion.refs_0_), channel_id=1, source_target_pairs={{0,16},{1,3},{2,18},{3,1},{4,20},{5,7},{6,22},{7,5},{8,24},{9,11},... | collective-permute-start | bytes 565256 | tf_op jit(solution)/shard_map/ppermute | solution.py:167
  15.0 4.6 %collective-permute-start.4 = (bf16[16,2944]{1,0:T(8,128)(2,1)S(1)}, bf16[16,2944]{1,0:T(8,128)(2,1)S(1)}, u32[]{:S(2)}, u32[]{:S(2)}) collective-permute-start(bf16[16,2944]{1,0:T(8,128)(2,1)S(1)} %pad_maximum_fusion), channel_id=1, source_target_pairs={{0,2},{1,17},{2,0},{3,19},{4,6},{5,21},{6,4},{7,23},{8,10},{9,25},... | collective-permute-start | bytes 282632 | tf_op jit(solution)/shard_map/ppermute | solution.py:167
  17.2 7.0 %collective-permute-start.8 = (bf16[32,2944]{1,0:T(8,128)(2,1)S(1)}, bf16[32,2944]{1,0:T(8,128)(2,1)S(1)}, u32[]{:S(2)}, u32[]{:S(2)}) collective-permute-start(bf16[32,2944]{1,0:T(8,128)(2,1)S(1)} %constant_dynamic-update-slice_fusion.refs_0_), channel_id=1, source_target_pairs={{0,1},{1,0},{2,3},{3,2},{4,5},{5,4},{6,7},{7,6},{8,9},{9,8},{10,11... | collective-permute-start | bytes 565256 | tf_op jit(solution)/shard_map/ppermute | solution.py:167
  17.7 4.6 %collective-permute-start.7 = (bf16[16,2944]{1,0:T(8,128)(2,1)S(1)}, bf16[16,2944]{1,0:T(8,128)(2,1)S(1)}, u32[]{:S(2)}, u32[]{:S(2)}) collective-permute-start(bf16[16,2944]{1,0:T(8,128)(2,1)S(1)} %collective-permute-done.5.refs_3_), channel_id=1, source_target_pairs={{0,16},{1,3},{2,18},{3,1},{4,20},{5,7},{6,22},{7,5},{8,24},{9,11},... | collective-permute-start | bytes 282632 | tf_op jit(solution)/shard_map/ppermute | solution.py:167
  19.6 4.6 %collective-permute-start.6 = (bf16[16,2944]{1,0:T(8,128)(2,1)S(1)}, bf16[16,2944]{1,0:T(8,128)(2,1)S(1)}, u32[]{:S(2)}, u32[]{:S(2)}) collective-permute-start(bf16[16,2944]{1,0:T(8,128)(2,1)S(1)} %collective-permute-done.4.refs_2_), channel_id=1, source_target_pairs={{0,16},{1,3},{2,18},{3,1},{4,20},{5,7},{6,22},{7,5},{8,24},{9,11},... | collective-permute-start | bytes 282632 | tf_op jit(solution)/shard_map/ppermute | solution.py:167
  20.1 5.4 %collective-permute-start.9 = (bf16[32,2944]{1,0:T(8,128)(2,1)S(1)}, bf16[32,2944]{1,0:T(8,128)(2,1)S(1)}, u32[]{:S(2)}, u32[]{:S(2)}) collective-permute-start(bf16[32,2944]{1,0:T(8,128)(2,1)S(1)} %collective-permute-done.3.refs_1_), channel_id=1, source_target_pairs={{0,1},{1,0},{2,3},{3,2},{4,5},{5,4},{6,7},{7,6},{8,9},{9,8},{10,11... | collective-permute-start | bytes 565256 | tf_op jit(solution)/shard_map/ppermute | solution.py:167
  28.9 7.8 %collective-permute-start.14 = (bf16[32,2944]{1,0:T(8,128)(2,1)S(1)}, bf16[32,2944]{1,0:T(8,128)(2,1)S(1)}, u32[]{:S(2)}, u32[]{:S(2)}) collective-permute-start(bf16[32,2944]{1,0:T(8,128)(2,1)S(1)} %get-tuple-element.27), channel_id=1, source_target_pairs={{0,1},{1,0},{2,3},{3,2},{4,5},{5,4},{6,7},{7,6},{8,9},{9,8},{10,11... | collective-permute-start | bytes 565256 | tf_op jit(solution)/shard_map/ppermute | solution.py:167
  30.3 5.6 %collective-permute-start.19 = (bf16[32,2944]{1,0:T(8,128)(2,1)S(1)}, bf16[32,2944]{1,0:T(8,128)(2,1)S(1)}, u32[]{:S(2)}, u32[]{:S(2)}) collective-permute-start(bf16[32,2944]{1,0:T(8,128)(2,1)S(1)} %add_convert_fusion.4), channel_id=1, source_target_pairs={{0,16},{1,3},{2,18},{3,1},{4,20},{5,7},{6,22},{7,5},{8,24},{9,11},... | collective-permute-start | bytes 565256 | tf_op jit(solution)/shard_map/ppermute | solution.py:167
  30.9 7.0 %collective-permute-start.16 = (bf16[32,2944]{1,0:T(8,128)(2,1)S(1)}, bf16[32,2944]{1,0:T(8,128)(2,1)S(1)}, u32[]{:S(2)}, u32[]{:S(2)}) collective-permute-start(bf16[32,2944]{1,0:T(8,128)(2,1)S(1)} %add_convert_fusion.5), channel_id=1, source_target_pairs={{0,16},{1,3},{2,18},{3,1},{4,20},{5,7},{6,22},{7,5},{8,24},{9,11},... | collective-permute-start | bytes 565256 | tf_op jit(solution)/shard_map/ppermute | solution.py:167
  36.0 5.6 %collective-permute-start.20 = (bf16[32,2944]{1,0:T(8,128)(2,1)S(1)}, bf16[32,2944]{1,0:T(8,128)(2,1)S(1)}, u32[]{:S(2)}, u32[]{:S(2)}) collective-permute-start(bf16[32,2944]{1,0:T(8,128)(2,1)S(1)} %add_convert_fusion.3), channel_id=1, source_target_pairs={{0,2},{1,17},{2,0},{3,19},{4,6},{5,21},{6,4},{7,23},{8,10},{9,25},... | collective-permute-start | bytes 565256 | tf_op jit(solution)/shard_map/ppermute | solution.py:167
  41.7 5.9 %collective-permute-start.23 = (bf16[8,2944]{1,0:T(8,128)(2,1)S(1)}, bf16[8,2944]{1,0:T(8,128)(2,1)S(1)}, u32[]{:S(2)}, u32[]{:S(2)}) collective-permute-start(bf16[8,2944]{1,0:T(8,128)(2,1)S(1)} %get-tuple-element.52), channel_id=1, source_target_pairs={{0,12},{1,13},{2,14},{3,15},{4,8},{5,9},{6,10},{7,11},{8,4},{9,5},... | collective-permute-start | bytes 141320 | tf_op jit(solution)/shard_map/ppermute | solution.py:167
  43.8 5.0 %collective-permute-start.22 = (bf16[8,2944]{1,0:T(8,128)(2,1)S(1)}, bf16[8,2944]{1,0:T(8,128)(2,1)S(1)}, u32[]{:S(2)}, u32[]{:S(2)}) collective-permute-start(bf16[8,2944]{1,0:T(8,128)(2,1)S(1)} %get-tuple-element.53), channel_id=1, source_target_pairs={{0,8},{1,9},{2,10},{3,11},{4,12},{5,13},{6,14},{7,15},{8,0},{9,1},... | collective-permute-start | bytes 141320 | tf_op jit(solution)/shard_map/ppermute | solution.py:167
  43.8 5.0 %collective-permute-start.21 = (bf16[8,2944]{1,0:T(8,128)(2,1)S(1)}, bf16[8,2944]{1,0:T(8,128)(2,1)S(1)}, u32[]{:S(2)}, u32[]{:S(2)}) collective-permute-start(bf16[8,2944]{1,0:T(8,128)(2,1)S(1)} %get-tuple-element.54), channel_id=1, source_target_pairs={{0,4},{1,5},{2,6},{3,7},{4,0},{5,1},{6,2},{7,3},{8,12},{9,13},{10,... | collective-permute-start | bytes 141320 | tf_op jit(solution)/shard_map/ppermute | solution.py:167
  49.0 5.9 %collective-permute-start.26 = (bf16[8,2944]{1,0:T(8,128)(2,1)S(1)}, bf16[8,2944]{1,0:T(8,128)(2,1)S(1)}, u32[]{:S(2)}, u32[]{:S(2)}) collective-permute-start(bf16[8,2944]{1,0:T(8,128)(2,1)S(1)} %get-tuple-element.35), channel_id=1, source_target_pairs={{0,12},{1,13},{2,14},{3,15},{4,8},{5,9},{6,10},{7,11},{8,4},{9,5},... | collective-permute-start | bytes 141320 | tf_op jit(solution)/shard_map/ppermute | solution.py:167
  51.1 5.5 %collective-permute-start.25 = (bf16[8,2944]{1,0:T(8,128)(2,1)S(1)}, bf16[8,2944]{1,0:T(8,128)(2,1)S(1)}, u32[]{:S(2)}, u32[]{:S(2)}) collective-permute-start(bf16[8,2944]{1,0:T(8,128)(2,1)S(1)} %get-tuple-element.35), channel_id=1, source_target_pairs={{0,8},{1,9},{2,10},{3,11},{4,12},{5,13},{6,14},{7,15},{8,0},{9,1},... | collective-permute-start | bytes 141320 | tf_op jit(solution)/shard_map/ppermute | solution.py:167
  52.1 5.3 %collective-permute-start.24 = (bf16[8,2944]{1,0:T(8,128)(2,1)S(1)}, bf16[8,2944]{1,0:T(8,128)(2,1)S(1)}, u32[]{:S(2)}, u32[]{:S(2)}) collective-permute-start(bf16[8,2944]{1,0:T(8,128)(2,1)S(1)} %get-tuple-element.35), channel_id=1, source_target_pairs={{0,4},{1,5},{2,6},{3,7},{4,0},{5,1},{6,2},{7,3},{8,12},{9,13},{10,... | collective-permute-start | bytes 141320 | tf_op jit(solution)/shard_map/ppermute | solution.py:167
  56.6 4.6 %collective-permute-start.29 = (bf16[16,2944]{1,0:T(8,128)(2,1)S(1)}, bf16[16,2944]{1,0:T(8,128)(2,1)S(1)}, u32[]{:S(2)}, u32[]{:S(2)}) collective-permute-start(bf16[16,2944]{1,0:T(8,128)(2,1)S(1)} %pad_maximum_fusion.3), channel_id=1, source_target_pairs={{0,2},{1,17},{2,0},{3,19},{4,6},{5,21},{6,4},{7,23},{8,10},{9,25},... | collective-permute-start | bytes 282632 | tf_op jit(solution)/shard_map/ppermute | solution.py:167
  57.5 6.7 %collective-permute-start.27 = (bf16[32,2944]{1,0:T(8,128)(2,1)S(1)}, bf16[32,2944]{1,0:T(8,128)(2,1)S(1)}, u32[]{:S(2)}, u32[]{:S(2)}) collective-permute-start(bf16[32,2944]{1,0:T(8,128)(2,1)S(1)} %constant_dynamic-update-slice_fusion.4.refs_0_), channel_id=1, source_target_pairs={{0,16},{1,3},{2,18},{3,1},{4,20},{5,7},{6,22},{7,5},{8,24},{9,11},... | collective-permute-start | bytes 565256 | tf_op jit(solution)/shard_map/ppermute | solution.py:167
  58.6 4.6 %collective-permute-start.28 = (bf16[16,2944]{1,0:T(8,128)(2,1)S(1)}, bf16[16,2944]{1,0:T(8,128)(2,1)S(1)}, u32[]{:S(2)}, u32[]{:S(2)}) collective-permute-start(bf16[16,2944]{1,0:T(8,128)(2,1)S(1)} %pad_maximum_fusion.2), channel_id=1, source_target_pairs={{0,2},{1,17},{2,0},{3,19},{4,6},{5,21},{6,4},{7,23},{8,10},{9,25},... | collective-permute-start | bytes 282632 | tf_op jit(solution)/shard_map/ppermute | solution.py:167
  61.2 6.6 %collective-permute-start.32 = (bf16[32,2944]{1,0:T(8,128)(2,1)S(1)}, bf16[32,2944]{1,0:T(8,128)(2,1)S(1)}, u32[]{:S(2)}, u32[]{:S(2)}) collective-permute-start(bf16[32,2944]{1,0:T(8,128)(2,1)S(1)} %constant_dynamic-update-slice_fusion.4.refs_0_), channel_id=1, source_target_pairs={{0,1},{1,0},{2,3},{3,2},{4,5},{5,4},{6,7},{7,6},{8,9},{9,8},{10,11... | collective-permute-start | bytes 565256 | tf_op jit(solution)/shard_map/ppermute | solution.py:167
  64.2 4.9 %collective-permute-start.33 = (bf16[32,2944]{1,0:T(8,128)(2,1)S(1)}, bf16[32,2944]{1,0:T(8,128)(2,1)S(1)}, u32[]{:S(2)}, u32[]{:S(2)}) collective-permute-start(bf16[32,2944]{1,0:T(8,128)(2,1)S(1)} %collective-permute-done.27.refs_1_), channel_id=1, source_target_pairs={{0,1},{1,0},{2,3},{3,2},{4,5},{5,4},{6,7},{7,6},{8,9},{9,8},{10,11... | collective-permute-start | bytes 565256 | tf_op jit(solution)/shard_map/ppermute | solution.py:167
  72.5 7.8 %collective-permute-start.38 = (bf16[32,2944]{1,0:T(8,128)(2,1)S(1)}, bf16[32,2944]{1,0:T(8,128)(2,1)S(1)}, u32[]{:S(2)}, u32[]{:S(2)}) collective-permute-start(bf16[32,2944]{1,0:T(8,128)(2,1)S(1)} %get-tuple-element.37), channel_id=1, source_target_pairs={{0,1},{1,0},{2,3},{3,2},{4,5},{5,4},{6,7},{7,6},{8,9},{9,8},{10,11... | collective-permute-start | bytes 565256 | tf_op jit(solution)/shard_map/ppermute | solution.py:167
  73.8 5.6 %collective-permute-start.43 = (bf16[32,2944]{1,0:T(8,128)(2,1)S(1)}, bf16[32,2944]{1,0:T(8,128)(2,1)S(1)}, u32[]{:S(2)}, u32[]{:S(2)}) collective-permute-start(bf16[32,2944]{1,0:T(8,128)(2,1)S(1)} %add_convert_fusion.1), channel_id=1, source_target_pairs={{0,16},{1,3},{2,18},{3,1},{4,20},{5,7},{6,22},{7,5},{8,24},{9,11},... | collective-permute-start | bytes 565256 | tf_op jit(solution)/shard_map/ppermute | solution.py:167
  74.9 6.5 %collective-permute-start.40 = (bf16[32,2944]{1,0:T(8,128)(2,1)S(1)}, bf16[32,2944]{1,0:T(8,128)(2,1)S(1)}, u32[]{:S(2)}, u32[]{:S(2)}) collective-permute-start(bf16[32,2944]{1,0:T(8,128)(2,1)S(1)} %add_convert_fusion.2), channel_id=1, source_target_pairs={{0,16},{1,3},{2,18},{3,1},{4,20},{5,7},{6,22},{7,5},{8,24},{9,11},... | collective-permute-start | bytes 565256 | tf_op jit(solution)/shard_map/ppermute | solution.py:167
  79.5 5.6 %collective-permute-start.44 = (bf16[32,2944]{1,0:T(8,128)(2,1)S(1)}, bf16[32,2944]{1,0:T(8,128)(2,1)S(1)}, u32[]{:S(2)}, u32[]{:S(2)}) collective-permute-start(bf16[32,2944]{1,0:T(8,128)(2,1)S(1)} %add_convert_fusion), channel_id=1, source_target_pairs={{0,2},{1,17},{2,0},{3,19},{4,6},{5,21},{6,4},{7,23},{8,10},{9,25},... | collective-permute-start | bytes 565256 | tf_op jit(solution)/shard_map/ppermute | solution.py:167
  85.3 5.9 %collective-permute-start.47 = (bf16[8,2944]{1,0:T(8,128)(2,1)S(1)}, bf16[8,2944]{1,0:T(8,128)(2,1)S(1)}, u32[]{:S(2)}, u32[]{:S(2)}) collective-permute-start(bf16[8,2944]{1,0:T(8,128)(2,1)S(1)} %get-tuple-element.49), channel_id=1, source_target_pairs={{0,12},{1,13},{2,14},{3,15},{4,8},{5,9},{6,10},{7,11},{8,4},{9,5},... | collective-permute-start | bytes 141320 | tf_op jit(solution)/shard_map/ppermute | solution.py:167
  87.2 5.1 %collective-permute-start.46 = (bf16[8,2944]{1,0:T(8,128)(2,1)S(1)}, bf16[8,2944]{1,0:T(8,128)(2,1)S(1)}, u32[]{:S(2)}, u32[]{:S(2)}) collective-permute-start(bf16[8,2944]{1,0:T(8,128)(2,1)S(1)} %get-tuple-element.50), channel_id=1, source_target_pairs={{0,8},{1,9},{2,10},{3,11},{4,12},{5,13},{6,14},{7,15},{8,0},{9,1},... | collective-permute-start | bytes 141320 | tf_op jit(solution)/shard_map/ppermute | solution.py:167
  87.2 5.1 %collective-permute-start.45 = (bf16[8,2944]{1,0:T(8,128)(2,1)S(1)}, bf16[8,2944]{1,0:T(8,128)(2,1)S(1)}, u32[]{:S(2)}, u32[]{:S(2)}) collective-permute-start(bf16[8,2944]{1,0:T(8,128)(2,1)S(1)} %get-tuple-element.51), channel_id=1, source_target_pairs={{0,4},{1,5},{2,6},{3,7},{4,0},{5,1},{6,2},{7,3},{8,12},{9,13},{10,... | collective-permute-start | bytes 141320 | tf_op jit(solution)/shard_map/ppermute | solution.py:167
  (21 other events, 137.2 us)

commit v5 on v4

--- a/solution.py
+++ b/solution.py
@@ -162,12 +162,14 @@
     )(tokens, table)
 
     wave = lengths // WAVES
+    sequence = sorted(range(lengths), key=lambda step: (step % WAVES, step))
 
     def move(value, pairs):
         return lax.ppermute(value, axes, pairs)
 
     for layer in range(layers):
         line = [own] + [move(own, shift(step)) for step in range(1, lengths)]
+        line = [line[step] for step in sequence]
         parts = [jnp.concatenate(line[start : start + wave], axis=0) for start in range(0, lengths, wave)]
         here = jnp.concatenate(line, axis=0)
         firsts = [move(part, first_swap) for part in parts]
@@ -182,6 +184,7 @@
         here = here + move(second.astype(jnp.bfloat16), second_swap).astype(jnp.float32)
         here = here + move(first.astype(jnp.bfloat16), first_swap).astype(jnp.float32)
         pieces = here.reshape(lengths, tok_rows, width)
+        pieces = [pieces[sequence.index(step)] for step in range(lengths)]
         arrived = [move(pieces[step].astype(jnp.bfloat16), shift(step)) for step in range(1, lengths)]
         last = layer + 1 == layers
         outs = pl.pallas_call(
@@ -284,7 +287,7 @@
     tok_rows, top_k = tokens.shape[0], routes.shape[2]
     capacity = 2 * tok_rows * top_k // columns
     lengths = columns // 4
-    dense = groups == 2 and columns == 4 * lengths and lengths & (lengths - 1) == 0 and tok_rows <= 2 * capacity
+    dense = groups == 2 and columns == 4 * lengths and lengths & (lengths - 1) == 0 and lengths % WAVES == 0 and tok_rows <= 2 * capacity
     plan = dense_device if dense else dispatch_device
     return plan(tokens, routes, placement, up_weight, down_weight, router_weight)
 

time: 93.3 us -> 91.9 us (0.985)
  waiting for transfers between devices: 44.8 us -> 42 us
  starting transfers between devices: 38.3 us -> 39.7 us
    ppermute x48, waiting for transfers between devices: 44.8 us -> 42 us  [move(): return lax.ppermute(value, axes, pairs)]
    ppermute x48, starting transfers between devices: 38.3 us -> 39.7 us  [move(): return lax.ppermute(value, axes, pairs)]
  transfers between devices with their start and end apart: 48 -> 48, of which waited for: 26 -> 27; matrix products, arithmetic and copies ran while one was open for 0% -> 0% of each run, Pallas kernels for 0% -> 0%
where the time goes in v5:
time: 91.9 us; the launch traced here: 91.7 us
  waiting for transfers between devices  42 us (46%)
  starting transfers between devices  39.7 us (43%)
  Pallas kernels  7.62 us (8%)
  other arithmetic  1.28 us (1%)
  local copies, waits for them, and re-layouts  0.92 us (1%)
    ppermute x48, waiting for transfers between devices, move(): return lax.ppermute(value, axes, pairs)  42 us
    ppermute x48, starting transfers between devices, move(): return lax.ppermute(value, axes, pairs)  39.7 us
    pallas_call x2, Pallas kernels, expert_ffn(): pl.pallas_call(functools.partial(ffn_kernel, layer, count), out_shape=[ja...  6.38 us
  transfers between devices with their start and end apart: 48, of which 27 were waited for; matrix products, arithmetic and copies ran while one was open for 0% of the time, Pallas kernels for 0%

profile of v5, /device:TPU:0, one launch (start us, length us, event | category | flops | bytes accessed | tf_op | source)
XLA Modules:
  0.0 91.7 jit_solution(9496655056151606292)
XLA Ops:
  1.7 5.1 %collective-permute-start.2 = (bf16[8,2944]{1,0:T(8,128)(2,1)S(1)}, bf16[8,2944]{1,0:T(8,128)(2,1)S(1)}, u32[]{:S(2)}, u32[]{:S(2)}) collective-permute-start(bf16[8,2944]{1,0:T(8,128)(2,1)S(1)} %get-tuple-element.25), channel_id=1, source_target_pairs={{0,12},{1,13},{2,14},{3,15},{4,8},{5,9},{6,10},{7,11},{8,4},{9,5},... | collective-permute-start | bytes 141320 | tf_op jit(solution)/shard_map/ppermute | solution.py:168
  7.4 1.6 %collective-permute-done.2 = bf16[8,2944]{1,0:T(8,128)(2,1)S(1)} collective-permute-done((bf16[8,2944]{1,0:T(8,128)(2,1)S(1)}, bf16[8,2944]{1,0:T(8,128)(2,1)S(1)}, u32[]{:S(2)}, u32[]{:S(2)}) %collective-permute-start.2) | collective-permute-done | bytes 47136 | tf_op jit(solution)/shard_map/ppermute | solution.py:168
  9.0 1.9 %collective-permute-done.1 = bf16[8,2944]{1,0:T(8,128)(2,1)S(1)} collective-permute-done((bf16[8,2944]{1,0:T(8,128)(2,1)S(1)}, bf16[8,2944]{1,0:T(8,128)(2,1)S(1)}, u32[]{:S(2)}, u32[]{:S(2)}) %collective-permute-start.1) | collective-permute-done | bytes 47136 | tf_op jit(solution)/shard_map/ppermute | solution.py:168
  10.9 1.6 %collective-permute-start.5 = (bf16[16,2944]{1,0:T(8,128)(2,1)S(1)}, bf16[16,2944]{1,0:T(8,128)(2,1)S(1)}, u32[]{:S(2)}, u32[]{:S(2)}) collective-permute-start(bf16[16,2944]{1,0:T(8,128)(2,1)S(1)} %pad_maximum_fusion.1), channel_id=1, source_target_pairs={{0,2},{1,17},{2,0},{3,19},{4,6},{5,21},{6,4},{7,23},{8,10},{9,25},... | collective-permute-start | bytes 282632 | tf_op jit(solution)/shard_map/ppermute | solution.py:168
  12.5 1.6 %collective-permute-start.3 = (bf16[32,2944]{1,0:T(8,128)(2,1)S(1)}, bf16[32,2944]{1,0:T(8,128)(2,1)S(1)}, u32[]{:S(2)}, u32[]{:S(2)}) collective-permute-start(bf16[32,2944]{1,0:T(8,128)(2,1)S(1)} %constant_dynamic-update-slice_fusion.refs_0_), channel_id=1, source_target_pairs={{0,16},{1,3},{2,18},{3,1},{4,20},{5,7},{6,22},{7,5},{8,24},{9,11},... | collective-permute-start | bytes 565256 | tf_op jit(solution)/shard_map/ppermute | solution.py:168
  15.2 1.2 %collective-permute-done.5.refs_3_ = bf16[16,2944]{1,0:T(8,128)(2,1)S(1)} collective-permute-done((bf16[16,2944]{1,0:T(8,128)(2,1)S(1)}, bf16[16,2944]{1,0:T(8,128)(2,1)S(1)}, u32[]{:S(2)}, u32[]{:S(2)}) %collective-permute-start.5) | collective-permute-done | bytes 94240 | tf_op jit(solution)/shard_map/ppermute | solution.py:168
  19.7 1.8 %collective-permute-done.7.refs_5_ = bf16[16,2944]{1,0:T(8,128)(2,1)S(1)} collective-permute-done((bf16[16,2944]{1,0:T(8,128)(2,1)S(1)}, bf16[16,2944]{1,0:T(8,128)(2,1)S(1)}, u32[]{:S(2)}, u32[]{:S(2)}) %collective-permute-start.7) | collective-permute-done | bytes 94240 | tf_op jit(solution)/shard_map/ppermute | solution.py:168
  21.5 1.8 %collective-permute-done.6.refs_4_ = bf16[16,2944]{1,0:T(8,128)(2,1)S(1)} collective-permute-done((bf16[16,2944]{1,0:T(8,128)(2,1)S(1)}, bf16[16,2944]{1,0:T(8,128)(2,1)S(1)}, u32[]{:S(2)}, u32[]{:S(2)}) %collective-permute-start.6) | collective-permute-done | bytes 94240 | tf_op jit(solution)/shard_map/ppermute | solution.py:168
  23.3 1.3 %collective-permute-done.12.refs_10_ = bf16[16,2944]{1,0:T(8,128)(2,1)S(1)} collective-permute-done((bf16[16,2944]{1,0:T(8,128)(2,1)S(1)}, bf16[16,2944]{1,0:T(8,128)(2,1)S(1)}, u32[]{:S(2)}, u32[]{:S(2)}) %collective-permute-start.12) | collective-permute-done | bytes 94240 | tf_op jit(solution)/shard_map/ppermute | solution.py:168
  24.6 3.2 %ffn_0.1 = (bf16[32,2944]{1,0:T(8,128)(2,1)S(1)}, bf16[32,2944]{1,0:T(8,128)(2,1)S(1)}, bf16[32,2944]{1,0:T(8,128)(2,1)S(1)}, bf16[32,2944]{1,0:T(8,128)(2,1)S(1...) custom-call(bf16[32,2944]{1,0:T(8,128)(2,1)S(1)} %constant_dynamic-u, ...), custom_call_target="tpu_custom_call" | custom-call | tf_op jit(solution)/shard_map/ffn_0/pallas_call | solution.py:101
  30.0 1.6 %collective-permute-start.16 = (bf16[32,2944]{1,0:T(8,128)(2,1)S(1)}, bf16[32,2944]{1,0:T(8,128)(2,1)S(1)}, u32[]{:S(2)}, u32[]{:S(2)}) collective-permute-start(bf16[32,2944]{1,0:T(8,128)(2,1)S(1)} %add_convert_fusion.5), channel_id=1, source_target_pairs={{0,16},{1,3},{2,18},{3,1},{4,20},{5,7},{6,22},{7,5},{8,24},{9,11},... | collective-permute-start | bytes 565256 | tf_op jit(solution)/shard_map/ppermute | solution.py:168
  31.6 3.4 %collective-permute-done.19 = bf16[32,2944]{1,0:T(8,128)(2,1)S(1)} collective-permute-done((bf16[32,2944]{1,0:T(8,128)(2,1)S(1)}, bf16[32,2944]{1,0:T(8,128)(2,1)S(1)}, u32[]{:S(2)}, u32[]{:S(2)}) %collective-permute-start.19) | collective-permute-done | bytes 188448 | tf_op jit(solution)/shard_map/ppermute | solution.py:168
  37.0 3.7 %collective-permute-done.20 = bf16[32,2944]{1,0:T(8,128)(2,1)S(1)} collective-permute-done((bf16[32,2944]{1,0:T(8,128)(2,1)S(1)}, bf16[32,2944]{1,0:T(8,128)(2,1)S(1)}, u32[]{:S(2)}, u32[]{:S(2)}) %collective-permute-start.20) | collective-permute-done | bytes 188448 | tf_op jit(solution)/shard_map/ppermute | solution.py:168
  40.8 2.3 %collective-permute-start.23 = (bf16[8,2944]{1,0:T(8,128)(2,1)S(1)}, bf16[8,2944]{1,0:T(8,128)(2,1)S(1)}, u32[]{:S(2)}, u32[]{:S(2)}) collective-permute-start(bf16[8,2944]{1,0:T(8,128)(2,1)S(1)} %get-tuple-element.52), channel_id=1, source_target_pairs={{0,12},{1,13},{2,14},{3,15},{4,8},{5,9},{6,10},{7,11},{8,4},{9,5},... | collective-permute-start | bytes 141320 | tf_op jit(solution)/shard_map/ppermute | solution.py:168
  43.7 1.6 %collective-permute-start.21 = (bf16[8,2944]{1,0:T(8,128)(2,1)S(1)}, bf16[8,2944]{1,0:T(8,128)(2,1)S(1)}, u32[]{:S(2)}, u32[]{:S(2)}) collective-permute-start(bf16[8,2944]{1,0:T(8,128)(2,1)S(1)} %get-tuple-element.54), channel_id=1, source_target_pairs={{0,4},{1,5},{2,6},{3,7},{4,0},{5,1},{6,2},{7,3},{8,12},{9,13},{10,... | collective-permute-start | bytes 141320 | tf_op jit(solution)/shard_map/ppermute | solution.py:168
  45.3 1.7 %collective-permute-done.23.refs_2_ = bf16[8,2944]{1,0:T(8,128)(2,1)S(1)} collective-permute-done((bf16[8,2944]{1,0:T(8,128)(2,1)S(1)}, bf16[8,2944]{1,0:T(8,128)(2,1)S(1)}, u32[]{:S(2)}, u32[]{:S(2)}) %collective-permute-start.23) | collective-permute-done | bytes 47136 | tf_op jit(solution)/shard_map/ppermute | solution.py:168
  47.0 1.2 %collective-permute-done.22.refs_1_ = bf16[8,2944]{1,0:T(8,128)(2,1)S(1)} collective-permute-done((bf16[8,2944]{1,0:T(8,128)(2,1)S(1)}, bf16[8,2944]{1,0:T(8,128)(2,1)S(1)}, u32[]{:S(2)}, u32[]{:S(2)}) %collective-permute-start.22) | collective-permute-done | bytes 47136 | tf_op jit(solution)/shard_map/ppermute | solution.py:168
  48.6 1.9 %collective-permute-start.26 = (bf16[8,2944]{1,0:T(8,128)(2,1)S(1)}, bf16[8,2944]{1,0:T(8,128)(2,1)S(1)}, u32[]{:S(2)}, u32[]{:S(2)}) collective-permute-start(bf16[8,2944]{1,0:T(8,128)(2,1)S(1)} %get-tuple-element.35), channel_id=1, source_target_pairs={{0,12},{1,13},{2,14},{3,15},{4,8},{5,9},{6,10},{7,11},{8,4},{9,5},... | collective-permute-start | bytes 141320 | tf_op jit(solution)/shard_map/ppermute | solution.py:168
  51.0 2.0 %collective-permute-start.24 = (bf16[8,2944]{1,0:T(8,128)(2,1)S(1)}, bf16[8,2944]{1,0:T(8,128)(2,1)S(1)}, u32[]{:S(2)}, u32[]{:S(2)}) collective-permute-start(bf16[8,2944]{1,0:T(8,128)(2,1)S(1)} %get-tuple-element.35), channel_id=1, source_target_pairs={{0,8},{1,9},{2,10},{3,11},{4,12},{5,13},{6,14},{7,15},{8,0},{9,1},... | collective-permute-start | bytes 141320 | tf_op jit(solution)/shard_map/ppermute | solution.py:168
  53.0 1.5 %collective-permute-done.26 = bf16[8,2944]{1,0:T(8,128)(2,1)S(1)} collective-permute-done((bf16[8,2944]{1,0:T(8,128)(2,1)S(1)}, bf16[8,2944]{1,0:T(8,128)(2,1)S(1)}, u32[]{:S(2)}, u32[]{:S(2)}) %collective-permute-start.26) | collective-permute-done | bytes 47136 | tf_op jit(solution)/shard_map/ppermute | solution.py:168
  57.8 1.9 %collective-permute-done.29.refs_3_ = bf16[16,2944]{1,0:T(8,128)(2,1)S(1)} collective-permute-done((bf16[16,2944]{1,0:T(8,128)(2,1)S(1)}, bf16[16,2944]{1,0:T(8,128)(2,1)S(1)}, u32[]{:S(2)}, u32[]{:S(2)}) %collective-permute-start.29) | collective-permute-done | bytes 94240 | tf_op jit(solution)/shard_map/ppermute | solution.py:168
  63.4 1.3 %collective-permute-done.31.refs_5_ = bf16[16,2944]{1,0:T(8,128)(2,1)S(1)} collective-permute-done((bf16[16,2944]{1,0:T(8,128)(2,1)S(1)}, bf16[16,2944]{1,0:T(8,128)(2,1)S(1)}, u32[]{:S(2)}, u32[]{:S(2)}) %collective-permute-start.31) | collective-permute-done | bytes 94240 | tf_op jit(solution)/shard_map/ppermute | solution.py:168
  64.7 1.5 %collective-permute-done.30.refs_4_ = bf16[16,2944]{1,0:T(8,128)(2,1)S(1)} collective-permute-done((bf16[16,2944]{1,0:T(8,128)(2,1)S(1)}, bf16[16,2944]{1,0:T(8,128)(2,1)S(1)}, u32[]{:S(2)}, u32[]{:S(2)}) %collective-permute-start.30) | collective-permute-done | bytes 94240 | tf_op jit(solution)/shard_map/ppermute | solution.py:168
  66.3 1.3 %collective-permute-done.36.refs_10_ = bf16[16,2944]{1,0:T(8,128)(2,1)S(1)} collective-permute-done((bf16[16,2944]{1,0:T(8,128)(2,1)S(1)}, bf16[16,2944]{1,0:T(8,128)(2,1)S(1)}, u32[]{:S(2)}, u32[]{:S(2)}) %collective-permute-start.36) | collective-permute-done | bytes 94240 | tf_op jit(solution)/shard_map/ppermute | solution.py:168
  67.6 3.2 %ffn_1.1 = (bf16[32,2944]{1,0:T(8,128)(2,1)S(1)}, bf16[32,2944]{1,0:T(8,128)(2,1)S(1)}, bf16[32,2944]{1,0:T(8,128)(2,1)S(1)}, bf16[32,2944]{1,0:T(8,128)(2,1)S(1...) custom-call(bf16[32,2944]{1,0:T(8,128)(2,1)S(1)} %constant_dynamic-u, ...), custom_call_target="tpu_custom_call" | custom-call | tf_op jit(solution)/shard_map/ffn_1/pallas_call | solution.py:101
  72.3 1.3 %collective-permute-start.43 = (bf16[32,2944]{1,0:T(8,128)(2,1)S(1)}, bf16[32,2944]{1,0:T(8,128)(2,1)S(1)}, u32[]{:S(2)}, u32[]{:S(2)}) collective-permute-start(bf16[32,2944]{1,0:T(8,128)(2,1)S(1)} %add_convert_fusion.1), channel_id=1, source_target_pairs={{0,16},{1,3},{2,18},{3,1},{4,20},{5,7},{6,22},{7,5},{8,24},{9,11},... | collective-permute-start | bytes 565256 | tf_op jit(solution)/shard_map/ppermute | solution.py:168
  74.5 3.4 %collective-permute-done.43 = bf16[32,2944]{1,0:T(8,128)(2,1)S(1)} collective-permute-done((bf16[32,2944]{1,0:T(8,128)(2,1)S(1)}, bf16[32,2944]{1,0:T(8,128)(2,1)S(1)}, u32[]{:S(2)}, u32[]{:S(2)}) %collective-permute-start.43) | collective-permute-done | bytes 188448 | tf_op jit(solution)/shard_map/ppermute | solution.py:168
  78.8 1.2 %collective-permute-done.40 = bf16[32,2944]{1,0:T(8,128)(2,1)S(1)} collective-permute-done((bf16[32,2944]{1,0:T(8,128)(2,1)S(1)}, bf16[32,2944]{1,0:T(8,128)(2,1)S(1)}, u32[]{:S(2)}, u32[]{:S(2)}) %collective-permute-start.40) | collective-permute-done | bytes 188448 | tf_op jit(solution)/shard_map/ppermute | solution.py:168
  80.0 3.7 %collective-permute-done.44 = bf16[32,2944]{1,0:T(8,128)(2,1)S(1)} collective-permute-done((bf16[32,2944]{1,0:T(8,128)(2,1)S(1)}, bf16[32,2944]{1,0:T(8,128)(2,1)S(1)}, u32[]{:S(2)}, u32[]{:S(2)}) %collective-permute-start.44) | collective-permute-done | bytes 188448 | tf_op jit(solution)/shard_map/ppermute | solution.py:168
  83.8 1.9 %collective-permute-start.47 = (bf16[8,2944]{1,0:T(8,128)(2,1)S(1)}, bf16[8,2944]{1,0:T(8,128)(2,1)S(1)}, u32[]{:S(2)}, u32[]{:S(2)}) collective-permute-start(bf16[8,2944]{1,0:T(8,128)(2,1)S(1)} %get-tuple-element.49), channel_id=1, source_target_pairs={{0,12},{1,13},{2,14},{3,15},{4,8},{5,9},{6,10},{7,11},{8,4},{9,5},... | collective-permute-start | bytes 141320 | tf_op jit(solution)/shard_map/ppermute | solution.py:168
  86.3 2.0 %collective-permute-start.45 = (bf16[8,2944]{1,0:T(8,128)(2,1)S(1)}, bf16[8,2944]{1,0:T(8,128)(2,1)S(1)}, u32[]{:S(2)}, u32[]{:S(2)}) collective-permute-start(bf16[8,2944]{1,0:T(8,128)(2,1)S(1)} %get-tuple-element.51), channel_id=1, source_target_pairs={{0,4},{1,5},{2,6},{3,7},{4,0},{5,1},{6,2},{7,3},{8,12},{9,13},{10,... | collective-permute-start | bytes 141320 | tf_op jit(solution)/shard_map/ppermute | solution.py:168
  88.3 1.5 %collective-permute-done.47.refs_2_ = bf16[8,2944]{1,0:T(8,128)(2,1)S(1)} collective-permute-done((bf16[8,2944]{1,0:T(8,128)(2,1)S(1)}, bf16[8,2944]{1,0:T(8,128)(2,1)S(1)}, u32[]{:S(2)}, u32[]{:S(2)}) %collective-permute-start.47) | collective-permute-done | bytes 47136 | tf_op jit(solution)/shard_map/ppermute | solution.py:168
  (104 shorter events, 25.6 us)
Async XLA Ops:
  1.7 7.3 %collective-permute-start.2 = (bf16[8,2944]{1,0:T(8,128)(2,1)S(1)}, bf16[8,2944]{1,0:T(8,128)(2,1)S(1)}, u32[]{:S(2)}, u32[]{:S(2)}) collective-permute-start(bf16[8,2944]{1,0:T(8,128)(2,1)S(1)} %get-tuple-element.25), channel_id=1, source_target_pairs={{0,12},{1,13},{2,14},{3,15},{4,8},{5,9},{6,10},{7,11},{8,4},{9,5},... | collective-permute-start | bytes 141320 | tf_op jit(solution)/shard_map/ppermute | solution.py:168
  6.8 5.6 %collective-permute-start = (bf16[8,2944]{1,0:T(8,128)(2,1)S(1)}, bf16[8,2944]{1,0:T(8,128)(2,1)S(1)}, u32[]{:S(2)}, u32[]{:S(2)}) collective-permute-start(bf16[8,2944]{1,0:T(8,128)(2,1)S(1)} %get-tuple-element.25), channel_id=1, source_target_pairs={{0,8},{1,9},{2,10},{3,11},{4,12},{5,13},{6,14},{7,15},{8,0},{9,1},... | collective-permute-start | bytes 141320 | tf_op jit(solution)/shard_map/ppermute | solution.py:168
  10.9 5.6 %collective-permute-start.5 = (bf16[16,2944]{1,0:T(8,128)(2,1)S(1)}, bf16[16,2944]{1,0:T(8,128)(2,1)S(1)}, u32[]{:S(2)}, u32[]{:S(2)}) collective-permute-start(bf16[16,2944]{1,0:T(8,128)(2,1)S(1)} %pad_maximum_fusion.1), channel_id=1, source_target_pairs={{0,2},{1,17},{2,0},{3,19},{4,6},{5,21},{6,4},{7,23},{8,10},{9,25},... | collective-permute-start | bytes 282632 | tf_op jit(solution)/shard_map/ppermute | solution.py:168
  12.5 6.7 %collective-permute-start.3 = (bf16[32,2944]{1,0:T(8,128)(2,1)S(1)}, bf16[32,2944]{1,0:T(8,128)(2,1)S(1)}, u32[]{:S(2)}, u32[]{:S(2)}) collective-permute-start(bf16[32,2944]{1,0:T(8,128)(2,1)S(1)} %constant_dynamic-update-slice_fusion.refs_0_), channel_id=1, source_target_pairs={{0,16},{1,3},{2,18},{3,1},{4,20},{5,7},{6,22},{7,5},{8,24},{9,11},... | collective-permute-start | bytes 565256 | tf_op jit(solution)/shard_map/ppermute | solution.py:168
  14.1 4.6 %collective-permute-start.4 = (bf16[16,2944]{1,0:T(8,128)(2,1)S(1)}, bf16[16,2944]{1,0:T(8,128)(2,1)S(1)}, u32[]{:S(2)}, u32[]{:S(2)}) collective-permute-start(bf16[16,2944]{1,0:T(8,128)(2,1)S(1)} %pad_maximum_fusion), channel_id=1, source_target_pairs={{0,2},{1,17},{2,0},{3,19},{4,6},{5,21},{6,4},{7,23},{8,10},{9,25},... | collective-permute-start | bytes 282632 | tf_op jit(solution)/shard_map/ppermute | solution.py:168
  16.4 6.8 %collective-permute-start.8 = (bf16[32,2944]{1,0:T(8,128)(2,1)S(1)}, bf16[32,2944]{1,0:T(8,128)(2,1)S(1)}, u32[]{:S(2)}, u32[]{:S(2)}) collective-permute-start(bf16[32,2944]{1,0:T(8,128)(2,1)S(1)} %constant_dynamic-update-slice_fusion.refs_0_), channel_id=1, source_target_pairs={{0,1},{1,0},{2,3},{3,2},{4,5},{5,4},{6,7},{7,6},{8,9},{9,8},{10,11... | collective-permute-start | bytes 565256 | tf_op jit(solution)/shard_map/ppermute | solution.py:168
  16.9 4.6 %collective-permute-start.7 = (bf16[16,2944]{1,0:T(8,128)(2,1)S(1)}, bf16[16,2944]{1,0:T(8,128)(2,1)S(1)}, u32[]{:S(2)}, u32[]{:S(2)}) collective-permute-start(bf16[16,2944]{1,0:T(8,128)(2,1)S(1)} %collective-permute-done.5.refs_3_), channel_id=1, source_target_pairs={{0,16},{1,3},{2,18},{3,1},{4,20},{5,7},{6,22},{7,5},{8,24},{9,11},... | collective-permute-start | bytes 282632 | tf_op jit(solution)/shard_map/ppermute | solution.py:168
  18.7 4.6 %collective-permute-start.6 = (bf16[16,2944]{1,0:T(8,128)(2,1)S(1)}, bf16[16,2944]{1,0:T(8,128)(2,1)S(1)}, u32[]{:S(2)}, u32[]{:S(2)}) collective-permute-start(bf16[16,2944]{1,0:T(8,128)(2,1)S(1)} %collective-permute-done.4.refs_2_), channel_id=1, source_target_pairs={{0,16},{1,3},{2,18},{3,1},{4,20},{5,7},{6,22},{7,5},{8,24},{9,11},... | collective-permute-start | bytes 282632 | tf_op jit(solution)/shard_map/ppermute | solution.py:168
  19.2 5.4 %collective-permute-start.9 = (bf16[32,2944]{1,0:T(8,128)(2,1)S(1)}, bf16[32,2944]{1,0:T(8,128)(2,1)S(1)}, u32[]{:S(2)}, u32[]{:S(2)}) collective-permute-start(bf16[32,2944]{1,0:T(8,128)(2,1)S(1)} %collective-permute-done.3.refs_1_), channel_id=1, source_target_pairs={{0,1},{1,0},{2,3},{3,2},{4,5},{5,4},{6,7},{7,6},{8,9},{9,8},{10,11... | collective-permute-start | bytes 565256 | tf_op jit(solution)/shard_map/ppermute | solution.py:168
  28.0 8.2 %collective-permute-start.14 = (bf16[32,2944]{1,0:T(8,128)(2,1)S(1)}, bf16[32,2944]{1,0:T(8,128)(2,1)S(1)}, u32[]{:S(2)}, u32[]{:S(2)}) collective-permute-start(bf16[32,2944]{1,0:T(8,128)(2,1)S(1)} %get-tuple-element.27), channel_id=1, source_target_pairs={{0,1},{1,0},{2,3},{3,2},{4,5},{5,4},{6,7},{7,6},{8,9},{9,8},{10,11... | collective-permute-start | bytes 565256 | tf_op jit(solution)/shard_map/ppermute | solution.py:168
  29.4 5.6 %collective-permute-start.19 = (bf16[32,2944]{1,0:T(8,128)(2,1)S(1)}, bf16[32,2944]{1,0:T(8,128)(2,1)S(1)}, u32[]{:S(2)}, u32[]{:S(2)}) collective-permute-start(bf16[32,2944]{1,0:T(8,128)(2,1)S(1)} %add_convert_fusion.4), channel_id=1, source_target_pairs={{0,16},{1,3},{2,18},{3,1},{4,20},{5,7},{6,22},{7,5},{8,24},{9,11},... | collective-permute-start | bytes 565256 | tf_op jit(solution)/shard_map/ppermute | solution.py:168
  30.0 7.0 %collective-permute-start.16 = (bf16[32,2944]{1,0:T(8,128)(2,1)S(1)}, bf16[32,2944]{1,0:T(8,128)(2,1)S(1)}, u32[]{:S(2)}, u32[]{:S(2)}) collective-permute-start(bf16[32,2944]{1,0:T(8,128)(2,1)S(1)} %add_convert_fusion.5), channel_id=1, source_target_pairs={{0,16},{1,3},{2,18},{3,1},{4,20},{5,7},{6,22},{7,5},{8,24},{9,11},... | collective-permute-start | bytes 565256 | tf_op jit(solution)/shard_map/ppermute | solution.py:168
  35.1 5.6 %collective-permute-start.20 = (bf16[32,2944]{1,0:T(8,128)(2,1)S(1)}, bf16[32,2944]{1,0:T(8,128)(2,1)S(1)}, u32[]{:S(2)}, u32[]{:S(2)}) collective-permute-start(bf16[32,2944]{1,0:T(8,128)(2,1)S(1)} %add_convert_fusion.3), channel_id=1, source_target_pairs={{0,2},{1,17},{2,0},{3,19},{4,6},{5,21},{6,4},{7,23},{8,10},{9,25},... | collective-permute-start | bytes 565256 | tf_op jit(solution)/shard_map/ppermute | solution.py:168
  40.8 6.1 %collective-permute-start.23 = (bf16[8,2944]{1,0:T(8,128)(2,1)S(1)}, bf16[8,2944]{1,0:T(8,128)(2,1)S(1)}, u32[]{:S(2)}, u32[]{:S(2)}) collective-permute-start(bf16[8,2944]{1,0:T(8,128)(2,1)S(1)} %get-tuple-element.52), channel_id=1, source_target_pairs={{0,12},{1,13},{2,14},{3,15},{4,8},{5,9},{6,10},{7,11},{8,4},{9,5},... | collective-permute-start | bytes 141320 | tf_op jit(solution)/shard_map/ppermute | solution.py:168
  43.1 5.1 %collective-permute-start.22 = (bf16[8,2944]{1,0:T(8,128)(2,1)S(1)}, bf16[8,2944]{1,0:T(8,128)(2,1)S(1)}, u32[]{:S(2)}, u32[]{:S(2)}) collective-permute-start(bf16[8,2944]{1,0:T(8,128)(2,1)S(1)} %get-tuple-element.53), channel_id=1, source_target_pairs={{0,8},{1,9},{2,10},{3,11},{4,12},{5,13},{6,14},{7,15},{8,0},{9,1},... | collective-permute-start | bytes 141320 | tf_op jit(solution)/shard_map/ppermute | solution.py:168
  43.7 4.6 %collective-permute-start.21 = (bf16[8,2944]{1,0:T(8,128)(2,1)S(1)}, bf16[8,2944]{1,0:T(8,128)(2,1)S(1)}, u32[]{:S(2)}, u32[]{:S(2)}) collective-permute-start(bf16[8,2944]{1,0:T(8,128)(2,1)S(1)} %get-tuple-element.54), channel_id=1, source_target_pairs={{0,4},{1,5},{2,6},{3,7},{4,0},{5,1},{6,2},{7,3},{8,12},{9,13},{10,... | collective-permute-start | bytes 141320 | tf_op jit(solution)/shard_map/ppermute | solution.py:168
  48.6 6.0 %collective-permute-start.26 = (bf16[8,2944]{1,0:T(8,128)(2,1)S(1)}, bf16[8,2944]{1,0:T(8,128)(2,1)S(1)}, u32[]{:S(2)}, u32[]{:S(2)}) collective-permute-start(bf16[8,2944]{1,0:T(8,128)(2,1)S(1)} %get-tuple-element.35), channel_id=1, source_target_pairs={{0,12},{1,13},{2,14},{3,15},{4,8},{5,9},{6,10},{7,11},{8,4},{9,5},... | collective-permute-start | bytes 141320 | tf_op jit(solution)/shard_map/ppermute | solution.py:168
  51.0 5.1 %collective-permute-start.24 = (bf16[8,2944]{1,0:T(8,128)(2,1)S(1)}, bf16[8,2944]{1,0:T(8,128)(2,1)S(1)}, u32[]{:S(2)}, u32[]{:S(2)}) collective-permute-start(bf16[8,2944]{1,0:T(8,128)(2,1)S(1)} %get-tuple-element.35), channel_id=1, source_target_pairs={{0,8},{1,9},{2,10},{3,11},{4,12},{5,13},{6,14},{7,15},{8,0},{9,1},... | collective-permute-start | bytes 141320 | tf_op jit(solution)/shard_map/ppermute | solution.py:168
  55.0 4.6 %collective-permute-start.29 = (bf16[16,2944]{1,0:T(8,128)(2,1)S(1)}, bf16[16,2944]{1,0:T(8,128)(2,1)S(1)}, u32[]{:S(2)}, u32[]{:S(2)}) collective-permute-start(bf16[16,2944]{1,0:T(8,128)(2,1)S(1)} %pad_maximum_fusion.3), channel_id=1, source_target_pairs={{0,2},{1,17},{2,0},{3,19},{4,6},{5,21},{6,4},{7,23},{8,10},{9,25},... | collective-permute-start | bytes 282632 | tf_op jit(solution)/shard_map/ppermute | solution.py:168
  56.2 6.7 %collective-permute-start.27 = (bf16[32,2944]{1,0:T(8,128)(2,1)S(1)}, bf16[32,2944]{1,0:T(8,128)(2,1)S(1)}, u32[]{:S(2)}, u32[]{:S(2)}) collective-permute-start(bf16[32,2944]{1,0:T(8,128)(2,1)S(1)} %constant_dynamic-update-slice_fusion.4.refs_0_), channel_id=1, source_target_pairs={{0,16},{1,3},{2,18},{3,1},{4,20},{5,7},{6,22},{7,5},{8,24},{9,11},... | collective-permute-start | bytes 565256 | tf_op jit(solution)/shard_map/ppermute | solution.py:168
  57.1 4.6 %collective-permute-start.28 = (bf16[16,2944]{1,0:T(8,128)(2,1)S(1)}, bf16[16,2944]{1,0:T(8,128)(2,1)S(1)}, u32[]{:S(2)}, u32[]{:S(2)}) collective-permute-start(bf16[16,2944]{1,0:T(8,128)(2,1)S(1)} %pad_maximum_fusion.2), channel_id=1, source_target_pairs={{0,2},{1,17},{2,0},{3,19},{4,6},{5,21},{6,4},{7,23},{8,10},{9,25},... | collective-permute-start | bytes 282632 | tf_op jit(solution)/shard_map/ppermute | solution.py:168
  59.7 6.6 %collective-permute-start.32 = (bf16[32,2944]{1,0:T(8,128)(2,1)S(1)}, bf16[32,2944]{1,0:T(8,128)(2,1)S(1)}, u32[]{:S(2)}, u32[]{:S(2)}) collective-permute-start(bf16[32,2944]{1,0:T(8,128)(2,1)S(1)} %constant_dynamic-update-slice_fusion.4.refs_0_), channel_id=1, source_target_pairs={{0,1},{1,0},{2,3},{3,2},{4,5},{5,4},{6,7},{7,6},{8,9},{9,8},{10,11... | collective-permute-start | bytes 565256 | tf_op jit(solution)/shard_map/ppermute | solution.py:168
  60.2 4.6 %collective-permute-start.31 = (bf16[16,2944]{1,0:T(8,128)(2,1)S(1)}, bf16[16,2944]{1,0:T(8,128)(2,1)S(1)}, u32[]{:S(2)}, u32[]{:S(2)}) collective-permute-start(bf16[16,2944]{1,0:T(8,128)(2,1)S(1)} %collective-permute-done.29.refs_3_), channel_id=1, source_target_pairs={{0,16},{1,3},{2,18},{3,1},{4,20},{5,7},{6,22},{7,5},{8,24},{9,11},... | collective-permute-start | bytes 282632 | tf_op jit(solution)/shard_map/ppermute | solution.py:168
  61.7 4.6 %collective-permute-start.30 = (bf16[16,2944]{1,0:T(8,128)(2,1)S(1)}, bf16[16,2944]{1,0:T(8,128)(2,1)S(1)}, u32[]{:S(2)}, u32[]{:S(2)}) collective-permute-start(bf16[16,2944]{1,0:T(8,128)(2,1)S(1)} %collective-permute-done.28.refs_2_), channel_id=1, source_target_pairs={{0,16},{1,3},{2,18},{3,1},{4,20},{5,7},{6,22},{7,5},{8,24},{9,11},... | collective-permute-start | bytes 282632 | tf_op jit(solution)/shard_map/ppermute | solution.py:168
  62.9 4.7 %collective-permute-start.33 = (bf16[32,2944]{1,0:T(8,128)(2,1)S(1)}, bf16[32,2944]{1,0:T(8,128)(2,1)S(1)}, u32[]{:S(2)}, u32[]{:S(2)}) collective-permute-start(bf16[32,2944]{1,0:T(8,128)(2,1)S(1)} %collective-permute-done.27.refs_1_), channel_id=1, source_target_pairs={{0,1},{1,0},{2,3},{3,2},{4,5},{5,4},{6,7},{7,6},{8,9},{9,8},{10,11... | collective-permute-start | bytes 565256 | tf_op jit(solution)/shard_map/ppermute | solution.py:168
  71.0 7.8 %collective-permute-start.38 = (bf16[32,2944]{1,0:T(8,128)(2,1)S(1)}, bf16[32,2944]{1,0:T(8,128)(2,1)S(1)}, u32[]{:S(2)}, u32[]{:S(2)}) collective-permute-start(bf16[32,2944]{1,0:T(8,128)(2,1)S(1)} %get-tuple-element.37), channel_id=1, source_target_pairs={{0,1},{1,0},{2,3},{3,2},{4,5},{5,4},{6,7},{7,6},{8,9},{9,8},{10,11... | collective-permute-start | bytes 565256 | tf_op jit(solution)/shard_map/ppermute | solution.py:168
  72.3 5.6 %collective-permute-start.43 = (bf16[32,2944]{1,0:T(8,128)(2,1)S(1)}, bf16[32,2944]{1,0:T(8,128)(2,1)S(1)}, u32[]{:S(2)}, u32[]{:S(2)}) collective-permute-start(bf16[32,2944]{1,0:T(8,128)(2,1)S(1)} %add_convert_fusion.1), channel_id=1, source_target_pairs={{0,16},{1,3},{2,18},{3,1},{4,20},{5,7},{6,22},{7,5},{8,24},{9,11},... | collective-permute-start | bytes 565256 | tf_op jit(solution)/shard_map/ppermute | solution.py:168
  73.6 6.4 %collective-permute-start.40 = (bf16[32,2944]{1,0:T(8,128)(2,1)S(1)}, bf16[32,2944]{1,0:T(8,128)(2,1)S(1)}, u32[]{:S(2)}, u32[]{:S(2)}) collective-permute-start(bf16[32,2944]{1,0:T(8,128)(2,1)S(1)} %add_convert_fusion.2), channel_id=1, source_target_pairs={{0,16},{1,3},{2,18},{3,1},{4,20},{5,7},{6,22},{7,5},{8,24},{9,11},... | collective-permute-start | bytes 565256 | tf_op jit(solution)/shard_map/ppermute | solution.py:168
  78.1 5.6 %collective-permute-start.44 = (bf16[32,2944]{1,0:T(8,128)(2,1)S(1)}, bf16[32,2944]{1,0:T(8,128)(2,1)S(1)}, u32[]{:S(2)}, u32[]{:S(2)}) collective-permute-start(bf16[32,2944]{1,0:T(8,128)(2,1)S(1)} %add_convert_fusion), channel_id=1, source_target_pairs={{0,2},{1,17},{2,0},{3,19},{4,6},{5,21},{6,4},{7,23},{8,10},{9,25},... | collective-permute-start | bytes 565256 | tf_op jit(solution)/shard_map/ppermute | solution.py:168
  83.8 5.9 %collective-permute-start.47 = (bf16[8,2944]{1,0:T(8,128)(2,1)S(1)}, bf16[8,2944]{1,0:T(8,128)(2,1)S(1)}, u32[]{:S(2)}, u32[]{:S(2)}) collective-permute-start(bf16[8,2944]{1,0:T(8,128)(2,1)S(1)} %get-tuple-element.49), channel_id=1, source_target_pairs={{0,12},{1,13},{2,14},{3,15},{4,8},{5,9},{6,10},{7,11},{8,4},{9,5},... | collective-permute-start | bytes 141320 | tf_op jit(solution)/shard_map/ppermute | solution.py:168
  85.7 5.2 %collective-permute-start.46 = (bf16[8,2944]{1,0:T(8,128)(2,1)S(1)}, bf16[8,2944]{1,0:T(8,128)(2,1)S(1)}, u32[]{:S(2)}, u32[]{:S(2)}) collective-permute-start(bf16[8,2944]{1,0:T(8,128)(2,1)S(1)} %get-tuple-element.50), channel_id=1, source_target_pairs={{0,8},{1,9},{2,10},{3,11},{4,12},{5,13},{6,14},{7,15},{8,0},{9,1},... | collective-permute-start | bytes 141320 | tf_op jit(solution)/shard_map/ppermute | solution.py:168
  86.3 4.6 %collective-permute-start.45 = (bf16[8,2944]{1,0:T(8,128)(2,1)S(1)}, bf16[8,2944]{1,0:T(8,128)(2,1)S(1)}, u32[]{:S(2)}, u32[]{:S(2)}) collective-permute-start(bf16[8,2944]{1,0:T(8,128)(2,1)S(1)} %get-tuple-element.51), channel_id=1, source_target_pairs={{0,4},{1,5},{2,6},{3,7},{4,0},{5,1},{6,2},{7,3},{8,12},{9,13},{10,... | collective-permute-start | bytes 141320 | tf_op jit(solution)/shard_map/ppermute | solution.py:168
  (21 other events, 134.6 us)

commit v6 on v5

--- a/solution.py
+++ b/solution.py
@@ -181,8 +181,8 @@
             mine.astype(jnp.float32) + move(theirs, core_swap).astype(jnp.float32) for mine, theirs in zip(outs[:4], outs[4:])
         ]
         first = first + move(across.astype(jnp.bfloat16), second_swap).astype(jnp.float32)
-        here = here + move(second.astype(jnp.bfloat16), second_swap).astype(jnp.float32)
-        here = here + move(first.astype(jnp.bfloat16), first_swap).astype(jnp.float32)
+        side = move(second.astype(jnp.bfloat16), second_swap).astype(jnp.float32)
+        here = here + (side + move(first.astype(jnp.bfloat16), first_swap).astype(jnp.float32))
         pieces = here.reshape(lengths, tok_rows, width)
         pieces = [pieces[sequence.index(step)] for step in range(lengths)]
         arrived = [move(pieces[step].astype(jnp.bfloat16), shift(step)) for step in range(1, lengths)]

time: 91.9 us -> 91.9 us (level)
  no operation moved by 1% of the time
where the time goes in v6:
time: 91.9 us; the launch traced here: 91.7 us
  waiting for transfers between devices  42 us (46%)
  starting transfers between devices  39.7 us (43%)
  Pallas kernels  7.62 us (8%)
  other arithmetic  1.29 us (1%)
  local copies, waits for them, and re-layouts  0.92 us (1%)
    ppermute x48, waiting for transfers between devices, move(): return lax.ppermute(value, axes, pairs)  42 us
    ppermute x48, starting transfers between devices, move(): return lax.ppermute(value, axes, pairs)  39.7 us
    pallas_call x2, Pallas kernels, expert_ffn(): pl.pallas_call(functools.partial(ffn_kernel, layer, count), out_shape=[ja...  6.38 us
  transfers between devices with their start and end apart: 48, of which 27 were waited for; matrix products, arithmetic and copies ran while one was open for 0% of the time, Pallas kernels for 0%

profile of v6, /device:TPU:0, one launch (start us, length us, event | category | flops | bytes accessed | tf_op | source)
XLA Modules:
  0.0 91.7 jit_solution(7031772221200128635)
XLA Ops:
  1.7 5.1 %collective-permute-start.2 = (bf16[8,2944]{1,0:T(8,128)(2,1)S(1)}, bf16[8,2944]{1,0:T(8,128)(2,1)S(1)}, u32[]{:S(2)}, u32[]{:S(2)}) collective-permute-start(bf16[8,2944]{1,0:T(8,128)(2,1)S(1)} %get-tuple-element.25), channel_id=1, source_target_pairs={{0,12},{1,13},{2,14},{3,15},{4,8},{5,9},{6,10},{7,11},{8,4},{9,5},... | collective-permute-start | bytes 141320 | tf_op jit(solution)/shard_map/ppermute | solution.py:168
  7.4 1.6 %collective-permute-done.2 = bf16[8,2944]{1,0:T(8,128)(2,1)S(1)} collective-permute-done((bf16[8,2944]{1,0:T(8,128)(2,1)S(1)}, bf16[8,2944]{1,0:T(8,128)(2,1)S(1)}, u32[]{:S(2)}, u32[]{:S(2)}) %collective-permute-start.2) | collective-permute-done | bytes 47136 | tf_op jit(solution)/shard_map/ppermute | solution.py:168
  9.0 1.9 %collective-permute-done.1 = bf16[8,2944]{1,0:T(8,128)(2,1)S(1)} collective-permute-done((bf16[8,2944]{1,0:T(8,128)(2,1)S(1)}, bf16[8,2944]{1,0:T(8,128)(2,1)S(1)}, u32[]{:S(2)}, u32[]{:S(2)}) %collective-permute-start.1) | collective-permute-done | bytes 47136 | tf_op jit(solution)/shard_map/ppermute | solution.py:168
  10.9 1.6 %collective-permute-start.5 = (bf16[16,2944]{1,0:T(8,128)(2,1)S(1)}, bf16[16,2944]{1,0:T(8,128)(2,1)S(1)}, u32[]{:S(2)}, u32[]{:S(2)}) collective-permute-start(bf16[16,2944]{1,0:T(8,128)(2,1)S(1)} %pad_maximum_fusion.1), channel_id=1, source_target_pairs={{0,2},{1,17},{2,0},{3,19},{4,6},{5,21},{6,4},{7,23},{8,10},{9,25},... | collective-permute-start | bytes 282632 | tf_op jit(solution)/shard_map/ppermute | solution.py:168
  12.5 1.6 %collective-permute-start.3 = (bf16[32,2944]{1,0:T(8,128)(2,1)S(1)}, bf16[32,2944]{1,0:T(8,128)(2,1)S(1)}, u32[]{:S(2)}, u32[]{:S(2)}) collective-permute-start(bf16[32,2944]{1,0:T(8,128)(2,1)S(1)} %constant_dynamic-update-slice_fusion.refs_0_), channel_id=1, source_target_pairs={{0,16},{1,3},{2,18},{3,1},{4,20},{5,7},{6,22},{7,5},{8,24},{9,11},... | collective-permute-start | bytes 565256 | tf_op jit(solution)/shard_map/ppermute | solution.py:168
  15.2 1.2 %collective-permute-done.5.refs_3_ = bf16[16,2944]{1,0:T(8,128)(2,1)S(1)} collective-permute-done((bf16[16,2944]{1,0:T(8,128)(2,1)S(1)}, bf16[16,2944]{1,0:T(8,128)(2,1)S(1)}, u32[]{:S(2)}, u32[]{:S(2)}) %collective-permute-start.5) | collective-permute-done | bytes 94240 | tf_op jit(solution)/shard_map/ppermute | solution.py:168
  19.7 1.8 %collective-permute-done.7.refs_5_ = bf16[16,2944]{1,0:T(8,128)(2,1)S(1)} collective-permute-done((bf16[16,2944]{1,0:T(8,128)(2,1)S(1)}, bf16[16,2944]{1,0:T(8,128)(2,1)S(1)}, u32[]{:S(2)}, u32[]{:S(2)}) %collective-permute-start.7) | collective-permute-done | bytes 94240 | tf_op jit(solution)/shard_map/ppermute | solution.py:168
  21.5 1.8 %collective-permute-done.6.refs_4_ = bf16[16,2944]{1,0:T(8,128)(2,1)S(1)} collective-permute-done((bf16[16,2944]{1,0:T(8,128)(2,1)S(1)}, bf16[16,2944]{1,0:T(8,128)(2,1)S(1)}, u32[]{:S(2)}, u32[]{:S(2)}) %collective-permute-start.6) | collective-permute-done | bytes 94240 | tf_op jit(solution)/shard_map/ppermute | solution.py:168
  23.3 1.3 %collective-permute-done.12.refs_10_ = bf16[16,2944]{1,0:T(8,128)(2,1)S(1)} collective-permute-done((bf16[16,2944]{1,0:T(8,128)(2,1)S(1)}, bf16[16,2944]{1,0:T(8,128)(2,1)S(1)}, u32[]{:S(2)}, u32[]{:S(2)}) %collective-permute-start.12) | collective-permute-done | bytes 94240 | tf_op jit(solution)/shard_map/ppermute | solution.py:168
  24.6 3.2 %ffn_0.1 = (bf16[32,2944]{1,0:T(8,128)(2,1)S(1)}, bf16[32,2944]{1,0:T(8,128)(2,1)S(1)}, bf16[32,2944]{1,0:T(8,128)(2,1)S(1)}, bf16[32,2944]{1,0:T(8,128)(2,1)S(1...) custom-call(bf16[32,2944]{1,0:T(8,128)(2,1)S(1)} %constant_dynamic-u, ...), custom_call_target="tpu_custom_call" | custom-call | tf_op jit(solution)/shard_map/ffn_0/pallas_call | solution.py:101
  30.0 1.6 %collective-permute-start.16 = (bf16[32,2944]{1,0:T(8,128)(2,1)S(1)}, bf16[32,2944]{1,0:T(8,128)(2,1)S(1)}, u32[]{:S(2)}, u32[]{:S(2)}) collective-permute-start(bf16[32,2944]{1,0:T(8,128)(2,1)S(1)} %add_convert_fusion.5), channel_id=1, source_target_pairs={{0,16},{1,3},{2,18},{3,1},{4,20},{5,7},{6,22},{7,5},{8,24},{9,11},... | collective-permute-start | bytes 565256 | tf_op jit(solution)/shard_map/ppermute | solution.py:168
  31.6 3.4 %collective-permute-done.19 = bf16[32,2944]{1,0:T(8,128)(2,1)S(1)} collective-permute-done((bf16[32,2944]{1,0:T(8,128)(2,1)S(1)}, bf16[32,2944]{1,0:T(8,128)(2,1)S(1)}, u32[]{:S(2)}, u32[]{:S(2)}) %collective-permute-start.19) | collective-permute-done | bytes 188448 | tf_op jit(solution)/shard_map/ppermute | solution.py:168
  37.0 3.7 %collective-permute-done.20 = bf16[32,2944]{1,0:T(8,128)(2,1)S(1)} collective-permute-done((bf16[32,2944]{1,0:T(8,128)(2,1)S(1)}, bf16[32,2944]{1,0:T(8,128)(2,1)S(1)}, u32[]{:S(2)}, u32[]{:S(2)}) %collective-permute-start.20) | collective-permute-done | bytes 188448 | tf_op jit(solution)/shard_map/ppermute | solution.py:168
  40.9 2.3 %collective-permute-start.23 = (bf16[8,2944]{1,0:T(8,128)(2,1)S(1)}, bf16[8,2944]{1,0:T(8,128)(2,1)S(1)}, u32[]{:S(2)}, u32[]{:S(2)}) collective-permute-start(bf16[8,2944]{1,0:T(8,128)(2,1)S(1)} %get-tuple-element.52), channel_id=1, source_target_pairs={{0,12},{1,13},{2,14},{3,15},{4,8},{5,9},{6,10},{7,11},{8,4},{9,5},... | collective-permute-start | bytes 141320 | tf_op jit(solution)/shard_map/ppermute | solution.py:168
  43.7 1.6 %collective-permute-start.21 = (bf16[8,2944]{1,0:T(8,128)(2,1)S(1)}, bf16[8,2944]{1,0:T(8,128)(2,1)S(1)}, u32[]{:S(2)}, u32[]{:S(2)}) collective-permute-start(bf16[8,2944]{1,0:T(8,128)(2,1)S(1)} %get-tuple-element.54), channel_id=1, source_target_pairs={{0,4},{1,5},{2,6},{3,7},{4,0},{5,1},{6,2},{7,3},{8,12},{9,13},{10,... | collective-permute-start | bytes 141320 | tf_op jit(solution)/shard_map/ppermute | solution.py:168
  45.3 1.7 %collective-permute-done.23.refs_2_ = bf16[8,2944]{1,0:T(8,128)(2,1)S(1)} collective-permute-done((bf16[8,2944]{1,0:T(8,128)(2,1)S(1)}, bf16[8,2944]{1,0:T(8,128)(2,1)S(1)}, u32[]{:S(2)}, u32[]{:S(2)}) %collective-permute-start.23) | collective-permute-done | bytes 47136 | tf_op jit(solution)/shard_map/ppermute | solution.py:168
  47.0 1.2 %collective-permute-done.22.refs_1_ = bf16[8,2944]{1,0:T(8,128)(2,1)S(1)} collective-permute-done((bf16[8,2944]{1,0:T(8,128)(2,1)S(1)}, bf16[8,2944]{1,0:T(8,128)(2,1)S(1)}, u32[]{:S(2)}, u32[]{:S(2)}) %collective-permute-start.22) | collective-permute-done | bytes 47136 | tf_op jit(solution)/shard_map/ppermute | solution.py:168
  48.6 1.9 %collective-permute-start.26 = (bf16[8,2944]{1,0:T(8,128)(2,1)S(1)}, bf16[8,2944]{1,0:T(8,128)(2,1)S(1)}, u32[]{:S(2)}, u32[]{:S(2)}) collective-permute-start(bf16[8,2944]{1,0:T(8,128)(2,1)S(1)} %get-tuple-element.35), channel_id=1, source_target_pairs={{0,12},{1,13},{2,14},{3,15},{4,8},{5,9},{6,10},{7,11},{8,4},{9,5},... | collective-permute-start | bytes 141320 | tf_op jit(solution)/shard_map/ppermute | solution.py:168
  51.0 2.0 %collective-permute-start.24 = (bf16[8,2944]{1,0:T(8,128)(2,1)S(1)}, bf16[8,2944]{1,0:T(8,128)(2,1)S(1)}, u32[]{:S(2)}, u32[]{:S(2)}) collective-permute-start(bf16[8,2944]{1,0:T(8,128)(2,1)S(1)} %get-tuple-element.35), channel_id=1, source_target_pairs={{0,8},{1,9},{2,10},{3,11},{4,12},{5,13},{6,14},{7,15},{8,0},{9,1},... | collective-permute-start | bytes 141320 | tf_op jit(solution)/shard_map/ppermute | solution.py:168
  53.0 1.5 %collective-permute-done.26 = bf16[8,2944]{1,0:T(8,128)(2,1)S(1)} collective-permute-done((bf16[8,2944]{1,0:T(8,128)(2,1)S(1)}, bf16[8,2944]{1,0:T(8,128)(2,1)S(1)}, u32[]{:S(2)}, u32[]{:S(2)}) %collective-permute-start.26) | collective-permute-done | bytes 47136 | tf_op jit(solution)/shard_map/ppermute | solution.py:168
  57.8 1.9 %collective-permute-done.29.refs_3_ = bf16[16,2944]{1,0:T(8,128)(2,1)S(1)} collective-permute-done((bf16[16,2944]{1,0:T(8,128)(2,1)S(1)}, bf16[16,2944]{1,0:T(8,128)(2,1)S(1)}, u32[]{:S(2)}, u32[]{:S(2)}) %collective-permute-start.29) | collective-permute-done | bytes 94240 | tf_op jit(solution)/shard_map/ppermute | solution.py:168
  63.4 1.3 %collective-permute-done.31.refs_5_ = bf16[16,2944]{1,0:T(8,128)(2,1)S(1)} collective-permute-done((bf16[16,2944]{1,0:T(8,128)(2,1)S(1)}, bf16[16,2944]{1,0:T(8,128)(2,1)S(1)}, u32[]{:S(2)}, u32[]{:S(2)}) %collective-permute-start.31) | collective-permute-done | bytes 94240 | tf_op jit(solution)/shard_map/ppermute | solution.py:168
  64.8 1.5 %collective-permute-done.30.refs_4_ = bf16[16,2944]{1,0:T(8,128)(2,1)S(1)} collective-permute-done((bf16[16,2944]{1,0:T(8,128)(2,1)S(1)}, bf16[16,2944]{1,0:T(8,128)(2,1)S(1)}, u32[]{:S(2)}, u32[]{:S(2)}) %collective-permute-start.30) | collective-permute-done | bytes 94240 | tf_op jit(solution)/shard_map/ppermute | solution.py:168
  66.3 1.3 %collective-permute-done.36.refs_10_ = bf16[16,2944]{1,0:T(8,128)(2,1)S(1)} collective-permute-done((bf16[16,2944]{1,0:T(8,128)(2,1)S(1)}, bf16[16,2944]{1,0:T(8,128)(2,1)S(1)}, u32[]{:S(2)}, u32[]{:S(2)}) %collective-permute-start.36) | collective-permute-done | bytes 94240 | tf_op jit(solution)/shard_map/ppermute | solution.py:168
  67.6 3.2 %ffn_1.1 = (bf16[32,2944]{1,0:T(8,128)(2,1)S(1)}, bf16[32,2944]{1,0:T(8,128)(2,1)S(1)}, bf16[32,2944]{1,0:T(8,128)(2,1)S(1)}, bf16[32,2944]{1,0:T(8,128)(2,1)S(1...) custom-call(bf16[32,2944]{1,0:T(8,128)(2,1)S(1)} %constant_dynamic-u, ...), custom_call_target="tpu_custom_call" | custom-call | tf_op jit(solution)/shard_map/ffn_1/pallas_call | solution.py:101
  72.3 1.3 %collective-permute-start.43 = (bf16[32,2944]{1,0:T(8,128)(2,1)S(1)}, bf16[32,2944]{1,0:T(8,128)(2,1)S(1)}, u32[]{:S(2)}, u32[]{:S(2)}) collective-permute-start(bf16[32,2944]{1,0:T(8,128)(2,1)S(1)} %add_convert_fusion.1), channel_id=1, source_target_pairs={{0,16},{1,3},{2,18},{3,1},{4,20},{5,7},{6,22},{7,5},{8,24},{9,11},... | collective-permute-start | bytes 565256 | tf_op jit(solution)/shard_map/ppermute | solution.py:168
  74.6 3.4 %collective-permute-done.43 = bf16[32,2944]{1,0:T(8,128)(2,1)S(1)} collective-permute-done((bf16[32,2944]{1,0:T(8,128)(2,1)S(1)}, bf16[32,2944]{1,0:T(8,128)(2,1)S(1)}, u32[]{:S(2)}, u32[]{:S(2)}) %collective-permute-start.43) | collective-permute-done | bytes 188448 | tf_op jit(solution)/shard_map/ppermute | solution.py:168
  78.8 1.2 %collective-permute-done.40 = bf16[32,2944]{1,0:T(8,128)(2,1)S(1)} collective-permute-done((bf16[32,2944]{1,0:T(8,128)(2,1)S(1)}, bf16[32,2944]{1,0:T(8,128)(2,1)S(1)}, u32[]{:S(2)}, u32[]{:S(2)}) %collective-permute-start.40) | collective-permute-done | bytes 188448 | tf_op jit(solution)/shard_map/ppermute | solution.py:168
  80.0 3.7 %collective-permute-done.44 = bf16[32,2944]{1,0:T(8,128)(2,1)S(1)} collective-permute-done((bf16[32,2944]{1,0:T(8,128)(2,1)S(1)}, bf16[32,2944]{1,0:T(8,128)(2,1)S(1)}, u32[]{:S(2)}, u32[]{:S(2)}) %collective-permute-start.44) | collective-permute-done | bytes 188448 | tf_op jit(solution)/shard_map/ppermute | solution.py:168
  83.8 1.9 %collective-permute-start.47 = (bf16[8,2944]{1,0:T(8,128)(2,1)S(1)}, bf16[8,2944]{1,0:T(8,128)(2,1)S(1)}, u32[]{:S(2)}, u32[]{:S(2)}) collective-permute-start(bf16[8,2944]{1,0:T(8,128)(2,1)S(1)} %get-tuple-element.49), channel_id=1, source_target_pairs={{0,12},{1,13},{2,14},{3,15},{4,8},{5,9},{6,10},{7,11},{8,4},{9,5},... | collective-permute-start | bytes 141320 | tf_op jit(solution)/shard_map/ppermute | solution.py:168
  86.3 2.0 %collective-permute-start.45 = (bf16[8,2944]{1,0:T(8,128)(2,1)S(1)}, bf16[8,2944]{1,0:T(8,128)(2,1)S(1)}, u32[]{:S(2)}, u32[]{:S(2)}) collective-permute-start(bf16[8,2944]{1,0:T(8,128)(2,1)S(1)} %get-tuple-element.51), channel_id=1, source_target_pairs={{0,4},{1,5},{2,6},{3,7},{4,0},{5,1},{6,2},{7,3},{8,12},{9,13},{10,... | collective-permute-start | bytes 141320 | tf_op jit(solution)/shard_map/ppermute | solution.py:168
  88.3 1.5 %collective-permute-done.47.refs_2_ = bf16[8,2944]{1,0:T(8,128)(2,1)S(1)} collective-permute-done((bf16[8,2944]{1,0:T(8,128)(2,1)S(1)}, bf16[8,2944]{1,0:T(8,128)(2,1)S(1)}, u32[]{:S(2)}, u32[]{:S(2)}) %collective-permute-start.47) | collective-permute-done | bytes 47136 | tf_op jit(solution)/shard_map/ppermute | solution.py:168
  (104 shorter events, 25.6 us)
Async XLA Ops:
  1.7 7.3 %collective-permute-start.2 = (bf16[8,2944]{1,0:T(8,128)(2,1)S(1)}, bf16[8,2944]{1,0:T(8,128)(2,1)S(1)}, u32[]{:S(2)}, u32[]{:S(2)}) collective-permute-start(bf16[8,2944]{1,0:T(8,128)(2,1)S(1)} %get-tuple-element.25), channel_id=1, source_target_pairs={{0,12},{1,13},{2,14},{3,15},{4,8},{5,9},{6,10},{7,11},{8,4},{9,5},... | collective-permute-start | bytes 141320 | tf_op jit(solution)/shard_map/ppermute | solution.py:168
  6.8 5.6 %collective-permute-start = (bf16[8,2944]{1,0:T(8,128)(2,1)S(1)}, bf16[8,2944]{1,0:T(8,128)(2,1)S(1)}, u32[]{:S(2)}, u32[]{:S(2)}) collective-permute-start(bf16[8,2944]{1,0:T(8,128)(2,1)S(1)} %get-tuple-element.25), channel_id=1, source_target_pairs={{0,8},{1,9},{2,10},{3,11},{4,12},{5,13},{6,14},{7,15},{8,0},{9,1},... | collective-permute-start | bytes 141320 | tf_op jit(solution)/shard_map/ppermute | solution.py:168
  10.9 5.6 %collective-permute-start.5 = (bf16[16,2944]{1,0:T(8,128)(2,1)S(1)}, bf16[16,2944]{1,0:T(8,128)(2,1)S(1)}, u32[]{:S(2)}, u32[]{:S(2)}) collective-permute-start(bf16[16,2944]{1,0:T(8,128)(2,1)S(1)} %pad_maximum_fusion.1), channel_id=1, source_target_pairs={{0,2},{1,17},{2,0},{3,19},{4,6},{5,21},{6,4},{7,23},{8,10},{9,25},... | collective-permute-start | bytes 282632 | tf_op jit(solution)/shard_map/ppermute | solution.py:168
  12.5 6.7 %collective-permute-start.3 = (bf16[32,2944]{1,0:T(8,128)(2,1)S(1)}, bf16[32,2944]{1,0:T(8,128)(2,1)S(1)}, u32[]{:S(2)}, u32[]{:S(2)}) collective-permute-start(bf16[32,2944]{1,0:T(8,128)(2,1)S(1)} %constant_dynamic-update-slice_fusion.refs_0_), channel_id=1, source_target_pairs={{0,16},{1,3},{2,18},{3,1},{4,20},{5,7},{6,22},{7,5},{8,24},{9,11},... | collective-permute-start | bytes 565256 | tf_op jit(solution)/shard_map/ppermute | solution.py:168
  14.1 4.6 %collective-permute-start.4 = (bf16[16,2944]{1,0:T(8,128)(2,1)S(1)}, bf16[16,2944]{1,0:T(8,128)(2,1)S(1)}, u32[]{:S(2)}, u32[]{:S(2)}) collective-permute-start(bf16[16,2944]{1,0:T(8,128)(2,1)S(1)} %pad_maximum_fusion), channel_id=1, source_target_pairs={{0,2},{1,17},{2,0},{3,19},{4,6},{5,21},{6,4},{7,23},{8,10},{9,25},... | collective-permute-start | bytes 282632 | tf_op jit(solution)/shard_map/ppermute | solution.py:168
  16.4 6.8 %collective-permute-start.8 = (bf16[32,2944]{1,0:T(8,128)(2,1)S(1)}, bf16[32,2944]{1,0:T(8,128)(2,1)S(1)}, u32[]{:S(2)}, u32[]{:S(2)}) collective-permute-start(bf16[32,2944]{1,0:T(8,128)(2,1)S(1)} %constant_dynamic-update-slice_fusion.refs_0_), channel_id=1, source_target_pairs={{0,1},{1,0},{2,3},{3,2},{4,5},{5,4},{6,7},{7,6},{8,9},{9,8},{10,11... | collective-permute-start | bytes 565256 | tf_op jit(solution)/shard_map/ppermute | solution.py:168
  16.9 4.6 %collective-permute-start.7 = (bf16[16,2944]{1,0:T(8,128)(2,1)S(1)}, bf16[16,2944]{1,0:T(8,128)(2,1)S(1)}, u32[]{:S(2)}, u32[]{:S(2)}) collective-permute-start(bf16[16,2944]{1,0:T(8,128)(2,1)S(1)} %collective-permute-done.5.refs_3_), channel_id=1, source_target_pairs={{0,16},{1,3},{2,18},{3,1},{4,20},{5,7},{6,22},{7,5},{8,24},{9,11},... | collective-permute-start | bytes 282632 | tf_op jit(solution)/shard_map/ppermute | solution.py:168
  18.7 4.6 %collective-permute-start.6 = (bf16[16,2944]{1,0:T(8,128)(2,1)S(1)}, bf16[16,2944]{1,0:T(8,128)(2,1)S(1)}, u32[]{:S(2)}, u32[]{:S(2)}) collective-permute-start(bf16[16,2944]{1,0:T(8,128)(2,1)S(1)} %collective-permute-done.4.refs_2_), channel_id=1, source_target_pairs={{0,16},{1,3},{2,18},{3,1},{4,20},{5,7},{6,22},{7,5},{8,24},{9,11},... | collective-permute-start | bytes 282632 | tf_op jit(solution)/shard_map/ppermute | solution.py:168
  19.2 5.4 %collective-permute-start.9 = (bf16[32,2944]{1,0:T(8,128)(2,1)S(1)}, bf16[32,2944]{1,0:T(8,128)(2,1)S(1)}, u32[]{:S(2)}, u32[]{:S(2)}) collective-permute-start(bf16[32,2944]{1,0:T(8,128)(2,1)S(1)} %collective-permute-done.3.refs_1_), channel_id=1, source_target_pairs={{0,1},{1,0},{2,3},{3,2},{4,5},{5,4},{6,7},{7,6},{8,9},{9,8},{10,11... | collective-permute-start | bytes 565256 | tf_op jit(solution)/shard_map/ppermute | solution.py:168
  28.0 8.2 %collective-permute-start.14 = (bf16[32,2944]{1,0:T(8,128)(2,1)S(1)}, bf16[32,2944]{1,0:T(8,128)(2,1)S(1)}, u32[]{:S(2)}, u32[]{:S(2)}) collective-permute-start(bf16[32,2944]{1,0:T(8,128)(2,1)S(1)} %get-tuple-element.27), channel_id=1, source_target_pairs={{0,1},{1,0},{2,3},{3,2},{4,5},{5,4},{6,7},{7,6},{8,9},{9,8},{10,11... | collective-permute-start | bytes 565256 | tf_op jit(solution)/shard_map/ppermute | solution.py:168
  29.4 5.6 %collective-permute-start.19 = (bf16[32,2944]{1,0:T(8,128)(2,1)S(1)}, bf16[32,2944]{1,0:T(8,128)(2,1)S(1)}, u32[]{:S(2)}, u32[]{:S(2)}) collective-permute-start(bf16[32,2944]{1,0:T(8,128)(2,1)S(1)} %add_convert_fusion.4), channel_id=1, source_target_pairs={{0,16},{1,3},{2,18},{3,1},{4,20},{5,7},{6,22},{7,5},{8,24},{9,11},... | collective-permute-start | bytes 565256 | tf_op jit(solution)/shard_map/ppermute | solution.py:168
  30.0 7.0 %collective-permute-start.16 = (bf16[32,2944]{1,0:T(8,128)(2,1)S(1)}, bf16[32,2944]{1,0:T(8,128)(2,1)S(1)}, u32[]{:S(2)}, u32[]{:S(2)}) collective-permute-start(bf16[32,2944]{1,0:T(8,128)(2,1)S(1)} %add_convert_fusion.5), channel_id=1, source_target_pairs={{0,16},{1,3},{2,18},{3,1},{4,20},{5,7},{6,22},{7,5},{8,24},{9,11},... | collective-permute-start | bytes 565256 | tf_op jit(solution)/shard_map/ppermute | solution.py:168
  35.1 5.6 %collective-permute-start.20 = (bf16[32,2944]{1,0:T(8,128)(2,1)S(1)}, bf16[32,2944]{1,0:T(8,128)(2,1)S(1)}, u32[]{:S(2)}, u32[]{:S(2)}) collective-permute-start(bf16[32,2944]{1,0:T(8,128)(2,1)S(1)} %add_convert_fusion.3), channel_id=1, source_target_pairs={{0,2},{1,17},{2,0},{3,19},{4,6},{5,21},{6,4},{7,23},{8,10},{9,25},... | collective-permute-start | bytes 565256 | tf_op jit(solution)/shard_map/ppermute | solution.py:168
  40.9 6.1 %collective-permute-start.23 = (bf16[8,2944]{1,0:T(8,128)(2,1)S(1)}, bf16[8,2944]{1,0:T(8,128)(2,1)S(1)}, u32[]{:S(2)}, u32[]{:S(2)}) collective-permute-start(bf16[8,2944]{1,0:T(8,128)(2,1)S(1)} %get-tuple-element.52), channel_id=1, source_target_pairs={{0,12},{1,13},{2,14},{3,15},{4,8},{5,9},{6,10},{7,11},{8,4},{9,5},... | collective-permute-start | bytes 141320 | tf_op jit(solution)/shard_map/ppermute | solution.py:168
  43.1 5.1 %collective-permute-start.22 = (bf16[8,2944]{1,0:T(8,128)(2,1)S(1)}, bf16[8,2944]{1,0:T(8,128)(2,1)S(1)}, u32[]{:S(2)}, u32[]{:S(2)}) collective-permute-start(bf16[8,2944]{1,0:T(8,128)(2,1)S(1)} %get-tuple-element.53), channel_id=1, source_target_pairs={{0,8},{1,9},{2,10},{3,11},{4,12},{5,13},{6,14},{7,15},{8,0},{9,1},... | collective-permute-start | bytes 141320 | tf_op jit(solution)/shard_map/ppermute | solution.py:168
  43.7 4.6 %collective-permute-start.21 = (bf16[8,2944]{1,0:T(8,128)(2,1)S(1)}, bf16[8,2944]{1,0:T(8,128)(2,1)S(1)}, u32[]{:S(2)}, u32[]{:S(2)}) collective-permute-start(bf16[8,2944]{1,0:T(8,128)(2,1)S(1)} %get-tuple-element.54), channel_id=1, source_target_pairs={{0,4},{1,5},{2,6},{3,7},{4,0},{5,1},{6,2},{7,3},{8,12},{9,13},{10,... | collective-permute-start | bytes 141320 | tf_op jit(solution)/shard_map/ppermute | solution.py:168
  48.6 6.0 %collective-permute-start.26 = (bf16[8,2944]{1,0:T(8,128)(2,1)S(1)}, bf16[8,2944]{1,0:T(8,128)(2,1)S(1)}, u32[]{:S(2)}, u32[]{:S(2)}) collective-permute-start(bf16[8,2944]{1,0:T(8,128)(2,1)S(1)} %get-tuple-element.35), channel_id=1, source_target_pairs={{0,12},{1,13},{2,14},{3,15},{4,8},{5,9},{6,10},{7,11},{8,4},{9,5},... | collective-permute-start | bytes 141320 | tf_op jit(solution)/shard_map/ppermute | solution.py:168
  51.0 5.1 %collective-permute-start.24 = (bf16[8,2944]{1,0:T(8,128)(2,1)S(1)}, bf16[8,2944]{1,0:T(8,128)(2,1)S(1)}, u32[]{:S(2)}, u32[]{:S(2)}) collective-permute-start(bf16[8,2944]{1,0:T(8,128)(2,1)S(1)} %get-tuple-element.35), channel_id=1, source_target_pairs={{0,8},{1,9},{2,10},{3,11},{4,12},{5,13},{6,14},{7,15},{8,0},{9,1},... | collective-permute-start | bytes 141320 | tf_op jit(solution)/shard_map/ppermute | solution.py:168
  55.0 4.6 %collective-permute-start.29 = (bf16[16,2944]{1,0:T(8,128)(2,1)S(1)}, bf16[16,2944]{1,0:T(8,128)(2,1)S(1)}, u32[]{:S(2)}, u32[]{:S(2)}) collective-permute-start(bf16[16,2944]{1,0:T(8,128)(2,1)S(1)} %pad_maximum_fusion.3), channel_id=1, source_target_pairs={{0,2},{1,17},{2,0},{3,19},{4,6},{5,21},{6,4},{7,23},{8,10},{9,25},... | collective-permute-start | bytes 282632 | tf_op jit(solution)/shard_map/ppermute | solution.py:168
  56.2 6.7 %collective-permute-start.27 = (bf16[32,2944]{1,0:T(8,128)(2,1)S(1)}, bf16[32,2944]{1,0:T(8,128)(2,1)S(1)}, u32[]{:S(2)}, u32[]{:S(2)}) collective-permute-start(bf16[32,2944]{1,0:T(8,128)(2,1)S(1)} %constant_dynamic-update-slice_fusion.4.refs_0_), channel_id=1, source_target_pairs={{0,16},{1,3},{2,18},{3,1},{4,20},{5,7},{6,22},{7,5},{8,24},{9,11},... | collective-permute-start | bytes 565256 | tf_op jit(solution)/shard_map/ppermute | solution.py:168
  57.1 4.6 %collective-permute-start.28 = (bf16[16,2944]{1,0:T(8,128)(2,1)S(1)}, bf16[16,2944]{1,0:T(8,128)(2,1)S(1)}, u32[]{:S(2)}, u32[]{:S(2)}) collective-permute-start(bf16[16,2944]{1,0:T(8,128)(2,1)S(1)} %pad_maximum_fusion.2), channel_id=1, source_target_pairs={{0,2},{1,17},{2,0},{3,19},{4,6},{5,21},{6,4},{7,23},{8,10},{9,25},... | collective-permute-start | bytes 282632 | tf_op jit(solution)/shard_map/ppermute | solution.py:168
  59.7 6.6 %collective-permute-start.32 = (bf16[32,2944]{1,0:T(8,128)(2,1)S(1)}, bf16[32,2944]{1,0:T(8,128)(2,1)S(1)}, u32[]{:S(2)}, u32[]{:S(2)}) collective-permute-start(bf16[32,2944]{1,0:T(8,128)(2,1)S(1)} %constant_dynamic-update-slice_fusion.4.refs_0_), channel_id=1, source_target_pairs={{0,1},{1,0},{2,3},{3,2},{4,5},{5,4},{6,7},{7,6},{8,9},{9,8},{10,11... | collective-permute-start | bytes 565256 | tf_op jit(solution)/shard_map/ppermute | solution.py:168
  60.2 4.6 %collective-permute-start.31 = (bf16[16,2944]{1,0:T(8,128)(2,1)S(1)}, bf16[16,2944]{1,0:T(8,128)(2,1)S(1)}, u32[]{:S(2)}, u32[]{:S(2)}) collective-permute-start(bf16[16,2944]{1,0:T(8,128)(2,1)S(1)} %collective-permute-done.29.refs_3_), channel_id=1, source_target_pairs={{0,16},{1,3},{2,18},{3,1},{4,20},{5,7},{6,22},{7,5},{8,24},{9,11},... | collective-permute-start | bytes 282632 | tf_op jit(solution)/shard_map/ppermute | solution.py:168
  61.7 4.6 %collective-permute-start.30 = (bf16[16,2944]{1,0:T(8,128)(2,1)S(1)}, bf16[16,2944]{1,0:T(8,128)(2,1)S(1)}, u32[]{:S(2)}, u32[]{:S(2)}) collective-permute-start(bf16[16,2944]{1,0:T(8,128)(2,1)S(1)} %collective-permute-done.28.refs_2_), channel_id=1, source_target_pairs={{0,16},{1,3},{2,18},{3,1},{4,20},{5,7},{6,22},{7,5},{8,24},{9,11},... | collective-permute-start | bytes 282632 | tf_op jit(solution)/shard_map/ppermute | solution.py:168
  62.9 4.7 %collective-permute-start.33 = (bf16[32,2944]{1,0:T(8,128)(2,1)S(1)}, bf16[32,2944]{1,0:T(8,128)(2,1)S(1)}, u32[]{:S(2)}, u32[]{:S(2)}) collective-permute-start(bf16[32,2944]{1,0:T(8,128)(2,1)S(1)} %collective-permute-done.27.refs_1_), channel_id=1, source_target_pairs={{0,1},{1,0},{2,3},{3,2},{4,5},{5,4},{6,7},{7,6},{8,9},{9,8},{10,11... | collective-permute-start | bytes 565256 | tf_op jit(solution)/shard_map/ppermute | solution.py:168
  71.0 7.8 %collective-permute-start.38 = (bf16[32,2944]{1,0:T(8,128)(2,1)S(1)}, bf16[32,2944]{1,0:T(8,128)(2,1)S(1)}, u32[]{:S(2)}, u32[]{:S(2)}) collective-permute-start(bf16[32,2944]{1,0:T(8,128)(2,1)S(1)} %get-tuple-element.37), channel_id=1, source_target_pairs={{0,1},{1,0},{2,3},{3,2},{4,5},{5,4},{6,7},{7,6},{8,9},{9,8},{10,11... | collective-permute-start | bytes 565256 | tf_op jit(solution)/shard_map/ppermute | solution.py:168
  72.3 5.6 %collective-permute-start.43 = (bf16[32,2944]{1,0:T(8,128)(2,1)S(1)}, bf16[32,2944]{1,0:T(8,128)(2,1)S(1)}, u32[]{:S(2)}, u32[]{:S(2)}) collective-permute-start(bf16[32,2944]{1,0:T(8,128)(2,1)S(1)} %add_convert_fusion.1), channel_id=1, source_target_pairs={{0,16},{1,3},{2,18},{3,1},{4,20},{5,7},{6,22},{7,5},{8,24},{9,11},... | collective-permute-start | bytes 565256 | tf_op jit(solution)/shard_map/ppermute | solution.py:168
  73.6 6.4 %collective-permute-start.40 = (bf16[32,2944]{1,0:T(8,128)(2,1)S(1)}, bf16[32,2944]{1,0:T(8,128)(2,1)S(1)}, u32[]{:S(2)}, u32[]{:S(2)}) collective-permute-start(bf16[32,2944]{1,0:T(8,128)(2,1)S(1)} %add_convert_fusion.2), channel_id=1, source_target_pairs={{0,16},{1,3},{2,18},{3,1},{4,20},{5,7},{6,22},{7,5},{8,24},{9,11},... | collective-permute-start | bytes 565256 | tf_op jit(solution)/shard_map/ppermute | solution.py:168
  78.1 5.6 %collective-permute-start.44 = (bf16[32,2944]{1,0:T(8,128)(2,1)S(1)}, bf16[32,2944]{1,0:T(8,128)(2,1)S(1)}, u32[]{:S(2)}, u32[]{:S(2)}) collective-permute-start(bf16[32,2944]{1,0:T(8,128)(2,1)S(1)} %add_convert_fusion), channel_id=1, source_target_pairs={{0,2},{1,17},{2,0},{3,19},{4,6},{5,21},{6,4},{7,23},{8,10},{9,25},... | collective-permute-start | bytes 565256 | tf_op jit(solution)/shard_map/ppermute | solution.py:168
  83.8 5.9 %collective-permute-start.47 = (bf16[8,2944]{1,0:T(8,128)(2,1)S(1)}, bf16[8,2944]{1,0:T(8,128)(2,1)S(1)}, u32[]{:S(2)}, u32[]{:S(2)}) collective-permute-start(bf16[8,2944]{1,0:T(8,128)(2,1)S(1)} %get-tuple-element.49), channel_id=1, source_target_pairs={{0,12},{1,13},{2,14},{3,15},{4,8},{5,9},{6,10},{7,11},{8,4},{9,5},... | collective-permute-start | bytes 141320 | tf_op jit(solution)/shard_map/ppermute | solution.py:168
  85.7 5.2 %collective-permute-start.46 = (bf16[8,2944]{1,0:T(8,128)(2,1)S(1)}, bf16[8,2944]{1,0:T(8,128)(2,1)S(1)}, u32[]{:S(2)}, u32[]{:S(2)}) collective-permute-start(bf16[8,2944]{1,0:T(8,128)(2,1)S(1)} %get-tuple-element.50), channel_id=1, source_target_pairs={{0,8},{1,9},{2,10},{3,11},{4,12},{5,13},{6,14},{7,15},{8,0},{9,1},... | collective-permute-start | bytes 141320 | tf_op jit(solution)/shard_map/ppermute | solution.py:168
  86.3 4.6 %collective-permute-start.45 = (bf16[8,2944]{1,0:T(8,128)(2,1)S(1)}, bf16[8,2944]{1,0:T(8,128)(2,1)S(1)}, u32[]{:S(2)}, u32[]{:S(2)}) collective-permute-start(bf16[8,2944]{1,0:T(8,128)(2,1)S(1)} %get-tuple-element.51), channel_id=1, source_target_pairs={{0,4},{1,5},{2,6},{3,7},{4,0},{5,1},{6,2},{7,3},{8,12},{9,13},{10,... | collective-permute-start | bytes 141320 | tf_op jit(solution)/shard_map/ppermute | solution.py:168
  (21 other events, 134.6 us)
